TPU v7x, 128 devices: a whole 4x4x4 slice. The times are simulated.
128 devices in a mesh: row: 8 (over y_lo, z), col: 16 (over x, y_hi, core).
Axes of the slice: x: 4, y: 4 (y_hi: 2, y_lo: 2; y = y_hi * 2 + y_lo), z: 4, core: 2. Of those that a mesh axis runs over, the one named last changes fastest.
Arguments:
- tokens: bfloat16 [12288, 8192], P(('row', 'col')), may hold values from -6 to 6
- up_weight: bfloat16 [8192, 14336], P('row', 'col'), may hold values from -0.0625 to 0.0625
Outputs:
- projected: bfloat16 [12288, 14336], P('row', 'col')
All inputs are finite; a program needn't handle non-finite values.
Results may differ from a plain program's by a relative error of at most 0.001.
Values may be sent and summed in bfloat16 or wider, within the bound.
No kernel may reach another device: no remote copies, remote signals or barrier semaphores. Data moves between devices by JAX's collectives and lax.ppermute only.
A program may use at most 128 MiB of HBM per device.

v0:
```python
import jax
import jax.numpy as jnp
from jax import lax
from jax.sharding import PartitionSpec as P


def on_device(tokens, up_weight):
    w_column = lax.all_gather(up_weight, "row", axis=0, tiled=True)
    return jnp.dot(
        lax.all_gather(tokens, "col", axis=0, tiled=True),
        w_column,
        preferred_element_type=jnp.float32,
    ).astype(jnp.bfloat16)


def solution(mesh):
    in_specs = (P(("row", "col"), None), P("row", "col"))
    out_specs = P("row", "col")
    return jax.shard_map(
        on_device, mesh=mesh, in_specs=in_specs, out_specs=out_specs, check_vma=False
    )
```

profile of v0, /device:TPU:1, one launch (start us, length us, event | category | flops | bytes accessed | tf_op | source)
XLA Modules:
  0.0 352.5 jit_solution(15638347445463018)
XLA Ops:
  6.5 0.0 all-gather.5.cloned.1.call-start
  6.5 0.7 all-gather.5.cloned.1.call-update
  7.3 0.0 all-gather.3.cloned.1.call-start
  7.3 0.7 all-gather.3.cloned.1.call-update
  8.0 155.1 %all-gather.5.cloned.1.call-done = bf16[8192,896]{1,0:T(8,128)(2,1)} async-done(((bf16[1024,896]{1,0:T(8,128)(2,1)}), bf16[8192,896]{1,0:T(8,128)(2,1)}) %all-gather.5.cloned.1.call-update) | async-done | bytes 14680080 | tf_op jit(solution)/shard_map/all_gather | solution.py:8
  163.1 150.1 %all-gather.3.cloned.1.call-done = bf16[1536,8192]{1,0:T(8,128)(2,1)} async-done(((bf16[96,8192]{1,0:T(8,128)(2,1)}), bf16[1536,8192]{1,0:T(8,128)(2,1)}) %all-gather.3.cloned.1.call-update) | async-done | bytes 25165840 | tf_op jit(solution)/shard_map/all_gather | solution.py:10
  313.2 32.5 %convolution_convert_fusion = bf16[1536,896]{1,0:T(8,128)(2,1)} fusion(bf16[1536,8192]{1,0:T(8,128)(2,1)} %all-gather.3.cloned.1.call-done, bf16[8192,896]{1,0:T(8,128)(2,1)} %all-gather.5.cloned.1.call-done), kind=kOutput, calls=%fused_computation | convolution fusion | flops 22549954560 | bytes 42598400 | tf_op jit(solution)/shard_map/dot_general | solution.py:9
Async XLA Ops:
  6.5 156.6 %all-gather.5.cloned.1.call-start = ((), (), s32[]{:S(2)}) async-start(), calls=%async_computation.1 | async-start | bytes 16515072 | tf_op jit(solution)/shard_map/all_gather | solution.py:8
  7.3 305.9 %all-gather.3.cloned.1.call-start = ((), (), s32[]{:S(2)}) async-start(), calls=%async_computation | async-start | bytes 26738688 | tf_op jit(solution)/shard_map/all_gather | solution.py:10
Sparse Core Ops, SparseCore 0:
  9.0 154.0 all-gather.4
  165.5 147.6 all-gather.2
where the time goes:
time: 353 us
  waiting for transfers between devices  307 us (87%)
  matrix products  32.5 us (9%)
  between operations  13.4 us (4%)
    all_gather x1, waiting for transfers between devices, on_device(): w_column = lax.all_gather(up_weight, 'row', axis=0, tiled=True)  155 us
    all_gather x1, waiting for transfers between devices, on_device(): lax.all_gather(tokens, 'col', axis=0, tiled=True)  150 us
    dot_general x1, matrix products, on_device(): jnp.dot(lax.all_gather(tokens, 'col', axis=0, tiled=True), w_column, pref...  32.5 us
  transfers between devices with their start and end apart: 2, of which 2 were waited for; matrix products, arithmetic and copies ran while one was open for 0% of the time, Pallas kernels for 0%

commit v1 on v0

v1 whole, which is shorter than its diff:
```python
import functools

import jax
import jax.numpy as jnp
from jax import lax
from jax.experimental import pallas as pl
from jax.experimental.pallas import tpu as pltpu
from jax.sharding import PartitionSpec as P

N = 896
KB = 1024
ROWS = 96


def row_perm(fn):
    return [(yl * 4 + z, fn(yl, z)[0] * 4 + fn(yl, z)[1]) for yl in range(2) for z in range(4)]


def col_perm(fn):
    at = lambda x, yh, c: x * 4 + yh * 2 + c
    return [(at(x, yh, c), at(*fn(x, yh, c))) for x in range(4) for yh in range(2) for c in range(2)]


WAYS = {
    "z+": ("row", row_perm(lambda yl, z: (yl, (z + 1) % 4))),
    "z-": ("row", row_perm(lambda yl, z: (yl, (z + 3) % 4))),
    "yl": ("row", row_perm(lambda yl, z: (1 - yl, z))),
    "x+": ("col", col_perm(lambda x, yh, c: ((x + 1) % 4, yh, c))),
    "x-": ("col", col_perm(lambda x, yh, c: ((x + 3) % 4, yh, c))),
    "yh": ("col", col_perm(lambda x, yh, c: (x, 1 - yh, c))),
    "co": ("col", col_perm(lambda x, yh, c: (x, yh, 1 - c))),
}

STEPS = [
    ("wLA", "z+", "wA"), ("wRB", "z-", "wB"), ("tL", "x+", "t"), ("tR", "x-", "t"), ("t1", "yh", "t"),
    ("wLB", "z+", "wB"), ("wRA", "z-", "wA"), ("w1A", "yl", "wA"), ("w1B", "yl", "wB"), ("ct", "co", "t"),
    ("wDA", "z+", "wLA"), ("wDB", "z-", "wRB"),
    ("tLA", "tL"), ("tDA", "x+", "tLA"), ("tRB", "tR"), ("tDB", "x-", "tRB"), ("t1L", "x+", "t1"), ("t1R", "x-", "t1"),
    ("ct1", "co", "t1"), ("ctL", "co", "tL"), ("ctR", "co", "tR"),
    ("w1LA", "z+", "w1A"), ("w1RA", "z-", "w1A"), ("ctDA", "co", "tDA"), ("ctDB", "co", "tDB"),
    ("k1",),
    ("w1LB", "z+", "w1B"), ("w1RB", "z-", "w1B"),
    ("w1DA", "z+", "w1LA"),
    ("t1LA", "t1L"), ("t1DA", "x+", "t1LA"), ("t1RB", "t1R"), ("t1DB", "x-", "t1RB"), ("ct1L", "co", "t1L"), ("ct1R", "co", "t1R"),
    ("k2",),
    ("w1DB", "z-", "w1RB"),
    ("k3",),
    ("ct1DA", "co", "t1DA"), ("ct1DB", "co", "t1DB"),
    ("k4",),
    ("k5",),
]
FAR = {"": 0, "L": 3, "R": 1, "D": 2}


def kernel(plan, at_ref, *refs):
    n_t, n_w, n_a = len(plan["t"]), len(plan["w"]), len(plan["acc"])
    t_refs, w_refs, a_refs = refs[:n_t], refs[n_t : n_t + n_w], refs[n_t + n_w : n_t + n_w + n_a]
    out_ref, t_vm, w_vm, acc, sem_t, sem_w, sem_a, *rest = refs[n_t + n_w + n_a :]
    blocks = plan["blocks"]
    a_copies = []
    for i, (first, rows) in enumerate(plan["acc"]):
        a_copies.append(pltpu.make_async_copy(a_refs[i], acc.at[pl.ds(first, rows)], sem_a.at[i]))
    copies = []
    for b, block in enumerate(blocks):
        col = pl.multiple_of(at_ref[plan["col"][b]], KB)
        mine = []
        for i, (name, row, rows) in enumerate(plan["t"]):
            if row >= block[0] and row < block[1]:
                mine.append(pltpu.make_async_copy(t_refs[i].at[:, pl.ds(col, KB)], t_vm.at[b, pl.ds(row, rows)], sem_t.at[b, i]))
        for i, (name, b_, row, rows) in enumerate(plan["w"]):
            if b_ == b:
                mine.append(pltpu.make_async_copy(w_refs[i], w_vm.at[b, pl.ds(row, rows)], sem_w.at[i]))
        copies.append(mine)
    for c in copies[0] + a_copies + sum(copies[1:], []):
        c.start()
    started = set(r for first, rows in plan["acc"] for r in range(first, first + rows, ROWS))
    for b, (lo, hi) in enumerate(blocks):
        for c in copies[b]:
            c.wait()
        if b == 0:
            for c in a_copies:
                c.wait()
        tile = plan["tile"]
        fresh = lo not in started
        started |= set(range(lo, hi, ROWS))

        @pl.loop(0, (hi - lo) // tile)
        def _(i, b=b, lo=lo, fresh=fresh):
            at = pl.ds(pl.multiple_of(lo + i * tile, 16), tile)
            part = jnp.dot(t_vm[b, at], w_vm[b], preferred_element_type=jnp.float32)
            acc[at] = part if fresh else acc[at] + part

    if not plan["last"]:
        c = pltpu.make_async_copy(acc, out_ref, sem_a.at[0])
        c.start()
        c.wait()
    else:
        res, sem_o = rest
        outs = []
        for i in range(16):
            at = pl.ds(i * ROWS, ROWS)
            res[at] = acc[at].astype(jnp.bfloat16)
            to = pl.multiple_of(at_ref[8 + i], 16)
            outs.append(pltpu.make_async_copy(res.at[at], out_ref.at[pl.ds(to, ROWS)], sem_o.at[i]))
            outs[-1].start()
        for c in outs:
            c.wait()


def call(at, got, accs, rows, t, w, blocks, acc=(), tile=256, last=False):
    t_in, w_in = [got[n] for n, _ in t], [got[n] for n, *_ in w]
    plan = {
        "t": [(n, r, v.shape[0]) for (n, r), v in zip(t, t_in)],
        "w": [(n, b, r, v.shape[0]) for (n, b, r), v in zip(w, w_in)],
        "acc": [(r, v.shape[0]) for r, v in zip(acc, accs)],
        "blocks": [b[1:] for b in blocks],
        "col": [b[0] for b in blocks],
        "tile": tile,
        "last": last,
    }
    nb = len(blocks)
    scratch = [
        pltpu.VMEM((nb, rows, KB), jnp.bfloat16),
        pltpu.VMEM((nb, KB, N), jnp.bfloat16),
        pltpu.VMEM((rows, N), jnp.float32),
        pltpu.SemaphoreType.DMA((nb, len(t))),
        pltpu.SemaphoreType.DMA((len(w),)),
        pltpu.SemaphoreType.DMA((max(1, len(accs)),)),
    ]
    if last:
        scratch += [pltpu.VMEM((rows, N), jnp.bfloat16), pltpu.SemaphoreType.DMA((16,))]
    flops = sum(2 * (hi - lo) * KB * N for _, lo, hi in blocks)
    hbm = pl.BlockSpec(memory_space=pltpu.HBM)
    return pl.pallas_call(
        functools.partial(kernel, plan),
        out_shape=jax.ShapeDtypeStruct((rows, N), jnp.bfloat16 if last else jnp.float32),
        in_specs=[pl.BlockSpec(memory_space=pltpu.SMEM)] + [hbm] * (len(t_in) + len(w_in) + len(accs)),
        out_specs=hbm,
        scratch_shapes=scratch,
        compiler_params=pltpu.CompilerParams(vmem_limit_bytes=50 * 2**20),
        cost_estimate=pl.CostEstimate(flops=flops, bytes_accessed=nb * rows * KB * 2, transcendentals=0),
    )(at, *t_in, *w_in, *accs)


def pieces(one, base):
    own = [(one + "", 0), (one + "L", 96), (one + "R", 192), (one + "DA", 288), (one + "DB", 336)]
    return [("t" + n, base + r) for n, r in own] + [("ct" + n, base + 384 + r) for n, r in own]


def on_device(tokens, up_weight):
    r, c = lax.axis_index("row"), lax.axis_index("col")
    yl, z = r // 4, r % 4
    x, yh, co = c // 4, c // 2 % 2, c % 2
    at = [((yl ^ one) * 4 + (z + FAR[k]) % 4) * KB for one in range(2) for k in ("", "L", "R", "D")]
    at += [
        ((x + FAR[k]) % 4 * 4 + (yh ^ one) * 2 + (co ^ cc)) * ROWS
        for one in range(2) for cc in range(2) for k in ("", "L", "R", "D")
    ]
    at = jnp.stack(at).astype(jnp.int32)
    got = {"t": tokens, "wA": up_weight[:512], "wB": up_weight[512:]}
    w0 = [("w" + k + h, b, 512 * (h == "B")) for b, k in enumerate(("", "L", "R", "D")) for h in "AB"]
    w1 = [("w1" + k + h, b, 512 * (h == "B")) for b, k in enumerate(("", "L", "R")) for h in "AB"]
    for step in STEPS:
        if len(step) == 3:
            name, way, operand = step
            got[name] = lax.ppermute(got[operand], *WAYS[way])
            continue
        if len(step) == 2:
            whole, half = got[step[1]], ROWS // 2
            got[step[0]] = whole[:half] if step[0][-1] == "A" else whole[half:]
            continue
        name, = step
        if name == "k1":
            a0 = call(at, got, [], 768, pieces("", 0), w0, [(b, 0, 768) for b in range(4)])
        if name == "k2":
            t = [("t1", 0), ("t1L", 96), ("t1R", 192), ("ct1", 288), ("ct1L", 384), ("ct1R", 480)]
            a1 = call(at, got, [], 576, t, w0, [(b, 0, 576) for b in range(4)], tile=288)
        if name == "k3":
            a0 = call(at, got, [a0], 768, pieces("", 0), w1, [(b, 0, 768) for b in (4, 5, 6)], acc=(0,))
        if name == "k4":
            t = [("t1", 0), ("t1L", 96), ("t1R", 192), ("ct1", 288), ("ct1L", 384), ("ct1R", 480)]
            t += [("t1DA", 576), ("t1DB", 624), ("ct1DA", 672), ("ct1DB", 720)]
            w = [(n, b, r_) for n, b, r_ in w0] + [(n, b + 4, r_) for n, b, r_ in w1]
            a1 = call(
                at, got, [a1], 768, t, w,
                [(b, 576, 768) for b in range(4)] + [(b, 0, 768) for b in (4, 5, 6)], acc=(0,), tile=192,
            )
        if name == "k5":
            t = pieces("", 0) + [("t1", 768), ("t1L", 864), ("t1R", 960), ("ct1", 1056), ("ct1L", 1152), ("ct1R", 1248)]
            t += [("t1DA", 1344), ("t1DB", 1392), ("ct1DA", 1440), ("ct1DB", 1488)]
            order = list(range(8)) + [8, 9, 10, 12, 13, 14, 11, 15]
            at5 = jnp.concatenate([at[:8], jnp.stack([at[8 + o] for o in order])])
            return call(
                at5, got, [a0, a1], 1536, t, [("w1DA", 0, 0), ("w1DB", 0, 512)], [(7, 0, 1536)],
                acc=(0, 768), last=True,
            )


def solution(mesh):
    return jax.shard_map(
        on_device, mesh=mesh, in_specs=(P(("row", "col"), None), P("row", "col")), out_specs=P("row", "col"), check_vma=False
    )
```

time: 353 us -> 261 us (0.74)
  waiting for transfers between devices: 307 us -> 131 us
  Pallas kernels: 0 us -> 60.2 us
  starting transfers between devices: 0.04 us -> 58.3 us
  matrix products: 32.5 us -> 0 us
  between operations: 13.4 us -> 0.55 us
  local copies, waits for them, and re-layouts: 0 us -> 10.2 us
    all_gather x2 -> x0, waiting for transfers between devices: 305 us -> none  [the longest x1 155 us: on_device(): w_column = lax.all_gather(up_weight, 'row', axis=0, tiled=True)]
    ppermute x0 -> x33, waiting for transfers between devices: none -> 131 us  [on_device(): got[name] = lax.ppermute(got[operand], *WAYS[way])]
    pallas_call x0 -> x5, Pallas kernels: none -> 60.2 us  [call(): pl.pallas_call(functools.partial(kernel, plan), out_shape=jax.ShapeDtypeS...]
    ppermute x0 -> x33, starting transfers between devices: none -> 58.3 us  [on_device(): got[name] = lax.ppermute(got[operand], *WAYS[way])]
    dot_general x1 -> x0, matrix products: 32.5 us -> none  [on_device(): jnp.dot(lax.all_gather(tokens, 'col', axis=0, tiled=True), w_column, pref...]
    slice x0 -> x5, local copies, waits for them, and re-layouts: none -> 6.01 us  [the longest x4 4.29 us: on_device(): got[step[0]] = whole[:half] if step[0][-1] == 'A' else whole[half:]]
    unnamed x0 -> x58, local copies, waits for them, and re-layouts: none -> 3.97 us
  transfers between devices with their start and end apart: 2 -> 33, of which waited for: 2 -> 11; matrix products, arithmetic and copies ran while one was open for 0% -> 2% of each run, Pallas kernels for 0% -> 19%
where the time goes in v1:
time: 261 us; the launch traced here: 260 us
  waiting for transfers between devices  131 us (50%)
  Pallas kernels  60.2 us (23%)
  starting transfers between devices  58.3 us (22%)
  local copies, waits for them, and re-layouts  10.2 us (4%)
    ppermute x33, waiting for transfers between devices, on_device(): got[name] = lax.ppermute(got[operand], *WAYS[way])  131 us
    pallas_call x5, Pallas kernels, call(): pl.pallas_call(functools.partial(kernel, plan), out_shape=jax.ShapeDtypeS...  60.2 us
    ppermute x33, starting transfers between devices, on_device(): got[name] = lax.ppermute(got[operand], *WAYS[way])  58.3 us
  transfers between devices with their start and end apart: 33, of which 11 were waited for; matrix products, arithmetic and copies ran while one was open for 2% of the time, Pallas kernels for 19%

profile of v1, /device:TPU:1, one launch (start us, length us, event | category | flops | bytes accessed | tf_op | source)
XLA Modules:
  0.0 260.3 jit_solution(1727375913903540814)
XLA Ops:
  0.0 1.7 fusion
  1.7 2.5 collective-permute-start.27
  4.3 2.2 collective-permute-start.30
  6.5 2.7 %collective-permute-start.29 = (bf16[512,896]{1,0:T(8,128)(2,1)S(1)}, bf16[512,896]{1,0:T(8,128)(2,1)S(1)}, u32[]{:S(2)}, u32[]{:S(2)}) collective-permute-start(bf16[512,896]{1,0:T(8,128)(2,1)S(1)} %get-tuple-element.6.refs_10_.refs_6_), channel_id=1, source_target_pairs={{0,48},{16,0},{32,16},{48,32},{64,112},{80,64},{96,80},{112,96},{1... | collective-permute-start | bytes 2752520 | tf_op jit(solution)/shard_map/ppermute | solution.py:166
  10.4 16.0 %collective-permute-done.27.refs_12_.refs_8_ = bf16[512,896]{1,0:T(8,128)(2,1)S(1)} collective-permute-done((bf16[512,896]{1,0:T(8,128)(2,1)S(1)}, bf16[512,896]{1,0:T(8,128)(2,1)S(1)}, u32[]{:S(2)}, u32[]{:S(2)}) %collective-permute-start.27) | collective-permute-done | bytes 917536 | tf_op jit(solution)/shard_map/ppermute | solution.py:166
  26.4 2.9 %collective-permute-start.9 = (bf16[96,8192]{1,0:T(8,128)(2,1)S(1)}, bf16[96,8192]{1,0:T(8,128)(2,1)}, u32[]{:S(2)}, u32[]{:S(2)}) collective-permute-start(bf16[96,8192]{1,0:T(8,128)(2,1)S(1)} %copy-done.14), channel_id=1, source_target_pairs={{0,2},{1,3},{2,0},{3,1},{4,6},{5,7},{6,4},{7,5},{8,10},{9,11},{10,... | collective-permute-start | bytes 4718600 | tf_op jit(solution)/shard_map/ppermute | solution.py:166
  30.6 15.6 %collective-permute-done.28.refs_13_.refs_9_ = bf16[512,896]{1,0:T(8,128)(2,1)S(1)} collective-permute-done((bf16[512,896]{1,0:T(8,128)(2,1)S(1)}, bf16[512,896]{1,0:T(8,128)(2,1)S(1)}, u32[]{:S(2)}, u32[]{:S(2)}) %collective-permute-start.28) | collective-permute-done | bytes 917536 | tf_op jit(solution)/shard_map/ppermute | solution.py:166
  47.4 2.5 collective-permute-start.1
  49.9 1.9 collective-permute-start.4
  51.8 31.1 %collective-permute-done.22.refs_11_.refs_19_ = bf16[512,896]{1,0:T(8,128)(2,1)S(1)} collective-permute-done((bf16[512,896]{1,0:T(8,128)(2,1)S(1)}, bf16[512,896]{1,0:T(8,128)(2,1)S(1)}, u32[]{:S(2)}, u32[]{:S(2)}) %collective-permute-start.22) | collective-permute-done | bytes 917536 | tf_op jit(solution)/shard_map/ppermute | solution.py:166
  82.8 2.7 %collective-permute-start.32 = (bf16[512,896]{1,0:T(8,128)(2,1)S(1)}, bf16[512,896]{1,0:T(8,128)(2,1)S(1)}, u32[]{:S(2)}, u32[]{:S(2)}) collective-permute-start(bf16[512,896]{1,0:T(8,128)(2,1)S(1)} %collective-permute-done.30.refs_15_.refs_11_), channel_id=1, source_target_pairs={{0,48},{16,0},{32,16},{48,32},{64,112},{80,64},{96,80},{112,96},{1... | collective-permute-start | bytes 2752520 | tf_op jit(solution)/shard_map/ppermute | solution.py:166
  85.5 2.7 %collective-permute-start.23 = (bf16[512,896]{1,0:T(8,128)(2,1)S(1)}, bf16[512,896]{1,0:T(8,128)(2,1)S(1)}, u32[]{:S(2)}, u32[]{:S(2)}) collective-permute-start(bf16[512,896]{1,0:T(8,128)(2,1)S(1)} %collective-permute-done.22.refs_11_.refs_19_), channel_id=1, source_target_pairs={{0,48},{16,0},{32,16},{48,32},{64,112},{80,64},{96,80},{112,96},{1... | collective-permute-start | bytes 2752520 | tf_op jit(solution)/shard_map/ppermute | solution.py:166
  88.2 15.3 %collective-permute-done.31.refs_16_.refs_12_ = bf16[512,896]{1,0:T(8,128)(2,1)S(1)} collective-permute-done((bf16[512,896]{1,0:T(8,128)(2,1)S(1)}, bf16[512,896]{1,0:T(8,128)(2,1)S(1)}, u32[]{:S(2)}, u32[]{:S(2)}) %collective-permute-start.31) | collective-permute-done | bytes 917536 | tf_op jit(solution)/shard_map/ppermute | solution.py:166
  106.9 16.3 %collective-permute-done.20.refs_12_.refs_20_ = bf16[512,896]{1,0:T(8,128)(2,1)S(1)} collective-permute-done((bf16[512,896]{1,0:T(8,128)(2,1)S(1)}, bf16[512,896]{1,0:T(8,128)(2,1)S(1)}, u32[]{:S(2)}, u32[]{:S(2)}) %collective-permute-start.20) | collective-permute-done | bytes 917536 | tf_op jit(solution)/shard_map/ppermute | solution.py:166
  124.5 1.6 collective-permute-start.11
  126.1 16.8 %collective-permute-done.25.refs_13_.refs_21_ = bf16[512,896]{1,0:T(8,128)(2,1)S(1)} collective-permute-done((bf16[512,896]{1,0:T(8,128)(2,1)S(1)}, bf16[512,896]{1,0:T(8,128)(2,1)S(1)}, u32[]{:S(2)}, u32[]{:S(2)}) %collective-permute-start.25) | collective-permute-done | bytes 917536 | tf_op jit(solution)/shard_map/ppermute | solution.py:166
  142.9 2.5 collective-permute-start.3
  145.4 3.5 %collective-permute-start.5 = (bf16[96,8192]{1,0:T(8,128)(2,1)S(1)}, bf16[96,8192]{1,0:T(8,128)(2,1)S(1)}, u32[]{:S(2)}, u32[]{:S(2)}) collective-permute-start(bf16[96,8192]{1,0:T(8,128)(2,1)S(1)} %collective-permute-done.refs_1_), channel_id=1, source_target_pairs={{0,1},{1,0},{2,3},{3,2},{4,5},{5,4},{6,7},{7,6},{8,9},{9,8},{10,11... | collective-permute-start | bytes 4718600 | tf_op jit(solution)/shard_map/ppermute | solution.py:166
  148.9 2.6 %collective-permute-done.2.refs_3_ = bf16[48,8192]{1,0:T(8,128)(2,1)S(1)} collective-permute-done((bf16[48,8192]{1,0:T(8,128)(2,1)S(1)}, bf16[48,8192]{1,0:T(8,128)(2,1)S(1)}, u32[]{:S(2)}, u32[]{:S(2)}) %collective-permute-start.2) | collective-permute-done | bytes 786464 | tf_op jit(solution)/shard_map/ppermute | solution.py:166
  151.6 7.0 %collective-permute-start.6 = (bf16[96,8192]{1,0:T(8,128)(2,1)S(1)}, bf16[96,8192]{1,0:T(8,128)(2,1)S(1)}, u32[]{:S(2)}, u32[]{:S(2)}) collective-permute-start(bf16[96,8192]{1,0:T(8,128)(2,1)S(1)} %collective-permute-done.1.refs_2_), channel_id=1, source_target_pairs={{0,1},{1,0},{2,3},{3,2},{4,5},{5,4},{6,7},{7,6},{8,9},{9,8},{10,11... | collective-permute-start | bytes 4718600 | tf_op jit(solution)/shard_map/ppermute | solution.py:166
  158.6 12.5 %collective-permute-done.3.refs_4_ = bf16[48,8192]{1,0:T(8,128)(2,1)S(1)} collective-permute-done((bf16[48,8192]{1,0:T(8,128)(2,1)S(1)}, bf16[48,8192]{1,0:T(8,128)(2,1)S(1)}, u32[]{:S(2)}, u32[]{:S(2)}) %collective-permute-start.3) | collective-permute-done | bytes 786464 | tf_op jit(solution)/shard_map/ppermute | solution.py:166
  171.1 7.3 %collective-permute-start.7 = (bf16[48,8192]{1,0:T(8,128)(2,1)S(1)}, bf16[48,8192]{1,0:T(8,128)(2,1)S(1)}, u32[]{:S(2)}, u32[]{:S(2)}) collective-permute-start(bf16[48,8192]{1,0:T(8,128)(2,1)S(1)} %collective-permute-done.2.refs_3_), channel_id=1, source_target_pairs={{0,1},{1,0},{2,3},{3,2},{4,5},{5,4},{6,7},{7,6},{8,9},{9,8},{10,11... | collective-permute-start | bytes 2359304 | tf_op jit(solution)/shard_map/ppermute | solution.py:166
  182.7 2.1 slice.28
  184.8 2.1 slice.29
  188.2 2.7 %collective-permute-start.16 = (bf16[48,8192]{1,0:T(8,128)(2,1)}, bf16[48,8192]{1,0:T(8,128)(2,1)}, u32[]{:S(2)}, u32[]{:S(2)}) collective-permute-start(bf16[48,8192]{1,0:T(8,128)(2,1)} %slice.29), channel_id=1, source_target_pairs={{0,12},{1,13},{2,14},{3,15},{4,0},{5,1},{6,2},{7,3},{8,4},{9,5},{1... | collective-permute-start | bytes 2359304 | tf_op jit(solution)/shard_map/ppermute | solution.py:166
  192.2 12.8 %shard_map.28.refs_16_ = f32[768,896]{1,0:T(8,128)} custom-call(s32[24]{0:T(128)S(1)} %stack.100.at_ref, bf16[96,8192]{1,0:T(8,128)(2,1)} %refs_0_.5, bf16[96,8192]{1,0:T(8,128)(2,1)} %copy-done.12, bf16[96,8192]{1,0:T(8,128)(2,1)} %copy-done.13, bf16[48,8192]{1,0:T(8,128)(2,1)S(1)} %collective-permute-done.2.refs_3_, ...), custom_call_target="tpu_custom_call" | custom-call | flops 5637144576 | bytes 6291456 | tf_op jit(solution)/shard_map/pallas_call | solution.py:134
  205.2 2.6 collective-permute-done.15.refs_6_.refs_16_
  209.0 11.6 %shard_map.29.refs_22_ = f32[768,896]{1,0:T(8,128)} custom-call(s32[24]{0:T(128)S(1)} %stack.100.at_ref, bf16[96,8192]{1,0:T(8,128)(2,1)} %refs_0_.5, bf16[96,8192]{1,0:T(8,128)(2,1)} %copy-done.12, bf16[96,8192]{1,0:T(8,128)(2,1)} %copy-done.13, bf16[48,8192]{1,0:T(8,128)(2,1)S(1)} %collective-permute-done.2.refs_3_, ...), custom_call_target="tpu_custom_call" | custom-call | flops 4227858432 | bytes 4718592 | tf_op jit(solution)/shard_map/pallas_call | solution.py:134
  220.7 2.6 %collective-permute-start.24 = (bf16[512,896]{1,0:T(8,128)(2,1)S(1)}, bf16[512,896]{1,0:T(8,128)(2,1)}, u32[]{:S(2)}, u32[]{:S(2)}) collective-permute-start(bf16[512,896]{1,0:T(8,128)(2,1)S(1)} %copy-done.26), channel_id=1, source_target_pairs={{0,48},{16,0},{32,16},{48,32},{64,112},{80,64},{96,80},{112,96},{1... | collective-permute-start | bytes 2752520 | tf_op jit(solution)/shard_map/ppermute | solution.py:166
  223.3 9.8 %shard_map.30.refs_24_ = f32[576,896]{1,0:T(8,128)} custom-call(s32[24]{0:T(128)S(1)} %stack.100.at_ref, bf16[96,8192]{1,0:T(8,128)(2,1)} %collective-permute-done.9.refs_0_.refs_10_, bf16[96,8192]{1,0:T(8,128)(2,1)} %collective-permute-done.10.refs_1_.refs_11_, bf16[96,8192]{1,0:T(8,128)(2,1)} %collective-permute-done.11.refs_2_.refs_12_, ...), custom_call_target="tpu_custom_call" | custom-call | flops 4227858432 | bytes 4718592 | tf_op jit(solution)/shard_map/pallas_call | solution.py:134
  233.1 15.2 %shard_map.31.refs_23_ = f32[768,896]{1,0:T(8,128)} custom-call(s32[24]{0:T(128)S(1)} %stack.100.at_ref, bf16[96,8192]{1,0:T(8,128)(2,1)} %collective-permute-done.9.refs_0_.refs_10_, bf16[96,8192]{1,0:T(8,128)(2,1)} %collective-permute-done.10.refs_1_.refs_11_, bf16[96,8192]{1,0:T(8,128)(2,1)} %collective-permute-done.11.refs_2_.refs_12_, ...), custom_call_target="tpu_custom_call" | custom-call | flops 5637144576 | bytes 11010048 | tf_op jit(solution)/shard_map/pallas_call | solution.py:134
  249.3 10.8 %shard_map.32 = bf16[1536,896]{1,0:T(8,128)(2,1)} custom-call(s32[24]{0:T(128)S(1)} %concatenate.6.at_ref, bf16[96,8192]{1,0:T(8,128)(2,1)} %refs_0_.5, bf16[96,8192]{1,0:T(8,128)(2,1)} %copy-done.12, bf16[96,8192]{1,0:T(8,128)(2,1)} %copy-done.13, bf16[48,8192]{1,0:T(8,128)(2,1)S(1)} %collective-permute-done.2.refs_3_, ...), custom_call_target="tpu_custom_call" | custom-call | flops 2818572288 | bytes 3145728 | tf_op jit(solution)/shard_map/pallas_call | solution.py:134
  (104 shorter events, 17.5 us)
Async XLA Ops:
  1.7 24.7 %collective-permute-start.27 = (bf16[512,896]{1,0:T(8,128)(2,1)S(1)}, bf16[512,896]{1,0:T(8,128)(2,1)S(1)}, u32[]{:S(2)}, u32[]{:S(2)}) collective-permute-start(bf16[512,896]{1,0:T(8,128)(2,1)S(1)} %get-tuple-element.6.refs_10_.refs_6_), channel_id=1, source_target_pairs={{0,16},{16,32},{32,48},{48,0},{64,80},{80,96},{96,112},{112,64},{1... | collective-permute-start | bytes 2752520 | tf_op jit(solution)/shard_map/ppermute | solution.py:166
  4.3 25.1 %collective-permute-start.30 = (bf16[512,896]{1,0:T(8,128)(2,1)S(1)}, bf16[512,896]{1,0:T(8,128)(2,1)S(1)}, u32[]{:S(2)}, u32[]{:S(2)}) collective-permute-start(bf16[512,896]{1,0:T(8,128)(2,1)S(1)} %get-tuple-element.5.refs_11_.refs_7_), channel_id=1, source_target_pairs={{0,48},{16,0},{32,16},{48,32},{64,112},{80,64},{96,80},{112,96},{1... | collective-permute-start | bytes 2752520 | tf_op jit(solution)/shard_map/ppermute | solution.py:166
  6.5 39.7 %collective-permute-start.28 = (bf16[512,896]{1,0:T(8,128)(2,1)S(1)}, bf16[512,896]{1,0:T(8,128)(2,1)S(1)}, u32[]{:S(2)}, u32[]{:S(2)}) collective-permute-start(bf16[512,896]{1,0:T(8,128)(2,1)S(1)} %get-tuple-element.5.refs_11_.refs_7_), channel_id=1, source_target_pairs={{0,16},{16,32},{32,48},{48,0},{64,80},{80,96},{96,112},{112,64},{1... | collective-permute-start | bytes 2752520 | tf_op jit(solution)/shard_map/ppermute | solution.py:166
  6.5 40.9 %collective-permute-start.29 = (bf16[512,896]{1,0:T(8,128)(2,1)S(1)}, bf16[512,896]{1,0:T(8,128)(2,1)S(1)}, u32[]{:S(2)}, u32[]{:S(2)}) collective-permute-start(bf16[512,896]{1,0:T(8,128)(2,1)S(1)} %get-tuple-element.6.refs_10_.refs_6_), channel_id=1, source_target_pairs={{0,48},{16,0},{32,16},{48,32},{64,112},{80,64},{96,80},{112,96},{1... | collective-permute-start | bytes 2752520 | tf_op jit(solution)/shard_map/ppermute | solution.py:166
  9.1 40.7 %collective-permute-start.19 = (bf16[512,896]{1,0:T(8,128)(2,1)S(1)}, bf16[512,896]{1,0:T(8,128)(2,1)S(1)}, u32[]{:S(2)}, u32[]{:S(2)}) collective-permute-start(bf16[512,896]{1,0:T(8,128)(2,1)S(1)} %get-tuple-element.6.refs_10_.refs_6_), channel_id=1, source_target_pairs={{0,64},{16,80},{32,96},{48,112},{64,0},{80,16},{96,32},{112,48},{1... | collective-permute-start | bytes 2752520 | tf_op jit(solution)/shard_map/ppermute | solution.py:166
  26.4 56.4 %collective-permute-start.9 = (bf16[96,8192]{1,0:T(8,128)(2,1)S(1)}, bf16[96,8192]{1,0:T(8,128)(2,1)}, u32[]{:S(2)}, u32[]{:S(2)}) collective-permute-start(bf16[96,8192]{1,0:T(8,128)(2,1)S(1)} %copy-done.14), channel_id=1, source_target_pairs={{0,2},{1,3},{2,0},{3,1},{4,6},{5,7},{6,4},{7,5},{8,10},{9,11},{10,... | collective-permute-start | bytes 4718600 | tf_op jit(solution)/shard_map/ppermute | solution.py:166
  29.4 56.2 %collective-permute-start = (bf16[96,8192]{1,0:T(8,128)(2,1)S(1)}, bf16[96,8192]{1,0:T(8,128)(2,1)S(1)}, u32[]{:S(2)}, u32[]{:S(2)}) collective-permute-start(bf16[96,8192]{1,0:T(8,128)(2,1)S(1)} %copy-done.14), channel_id=1, source_target_pairs={{0,4},{1,5},{2,6},{3,7},{4,8},{5,9},{6,10},{7,11},{8,12},{9,13},{1... | collective-permute-start | bytes 4718600 | tf_op jit(solution)/shard_map/ppermute | solution.py:166
  46.2 36.6 %collective-permute-start.22 = (bf16[512,896]{1,0:T(8,128)(2,1)S(1)}, bf16[512,896]{1,0:T(8,128)(2,1)S(1)}, u32[]{:S(2)}, u32[]{:S(2)}) collective-permute-start(bf16[512,896]{1,0:T(8,128)(2,1)S(1)} %get-tuple-element.5.refs_11_.refs_7_), channel_id=1, source_target_pairs={{0,64},{16,80},{32,96},{48,112},{64,0},{80,16},{96,32},{112,48},{1... | collective-permute-start | bytes 2752520 | tf_op jit(solution)/shard_map/ppermute | solution.py:166
  47.4 38.1 %collective-permute-start.1 = (bf16[96,8192]{1,0:T(8,128)(2,1)S(1)}, bf16[96,8192]{1,0:T(8,128)(2,1)S(1)}, u32[]{:S(2)}, u32[]{:S(2)}) collective-permute-start(bf16[96,8192]{1,0:T(8,128)(2,1)S(1)} %copy-done.14), channel_id=1, source_target_pairs={{0,12},{1,13},{2,14},{3,15},{4,0},{5,1},{6,2},{7,3},{8,4},{9,5},{1... | collective-permute-start | bytes 4718600 | tf_op jit(solution)/shard_map/ppermute | solution.py:166
  49.9 38.3 %collective-permute-start.4 = (bf16[96,8192]{1,0:T(8,128)(2,1)S(1)}, bf16[96,8192]{1,0:T(8,128)(2,1)S(1)}, u32[]{:S(2)}, u32[]{:S(2)}) collective-permute-start(bf16[96,8192]{1,0:T(8,128)(2,1)S(1)} %copy-done.14), channel_id=1, source_target_pairs={{0,1},{1,0},{2,3},{3,2},{4,5},{5,4},{6,7},{7,6},{8,9},{9,8},{10,11... | collective-permute-start | bytes 4718600 | tf_op jit(solution)/shard_map/ppermute | solution.py:166
  82.8 20.7 %collective-permute-start.31 = (bf16[512,896]{1,0:T(8,128)(2,1)S(1)}, bf16[512,896]{1,0:T(8,128)(2,1)S(1)}, u32[]{:S(2)}, u32[]{:S(2)}) collective-permute-start(bf16[512,896]{1,0:T(8,128)(2,1)S(1)} %collective-permute-done.27.refs_12_.refs_8_), channel_id=1, source_target_pairs={{0,16},{16,32},{32,48},{48,0},{64,80},{80,96},{96,112},{112,64},{1... | collective-permute-start | bytes 2752520 | tf_op jit(solution)/shard_map/ppermute | solution.py:166
  82.8 21.9 %collective-permute-start.32 = (bf16[512,896]{1,0:T(8,128)(2,1)S(1)}, bf16[512,896]{1,0:T(8,128)(2,1)S(1)}, u32[]{:S(2)}, u32[]{:S(2)}) collective-permute-start(bf16[512,896]{1,0:T(8,128)(2,1)S(1)} %collective-permute-done.30.refs_15_.refs_11_), channel_id=1, source_target_pairs={{0,48},{16,0},{32,16},{48,32},{64,112},{80,64},{96,80},{112,96},{1... | collective-permute-start | bytes 2752520 | tf_op jit(solution)/shard_map/ppermute | solution.py:166
  85.5 37.8 %collective-permute-start.20 = (bf16[512,896]{1,0:T(8,128)(2,1)S(1)}, bf16[512,896]{1,0:T(8,128)(2,1)S(1)}, u32[]{:S(2)}, u32[]{:S(2)}) collective-permute-start(bf16[512,896]{1,0:T(8,128)(2,1)S(1)} %collective-permute-done.19.refs_10_.refs_18_), channel_id=1, source_target_pairs={{0,16},{16,32},{32,48},{48,0},{64,80},{80,96},{96,112},{112,64},{1... | collective-permute-start | bytes 2752520 | tf_op jit(solution)/shard_map/ppermute | solution.py:166
  85.5 38.9 %collective-permute-start.23 = (bf16[512,896]{1,0:T(8,128)(2,1)S(1)}, bf16[512,896]{1,0:T(8,128)(2,1)S(1)}, u32[]{:S(2)}, u32[]{:S(2)}) collective-permute-start(bf16[512,896]{1,0:T(8,128)(2,1)S(1)} %collective-permute-done.22.refs_11_.refs_19_), channel_id=1, source_target_pairs={{0,48},{16,0},{32,16},{48,32},{64,112},{80,64},{96,80},{112,96},{1... | collective-permute-start | bytes 2752520 | tf_op jit(solution)/shard_map/ppermute | solution.py:166
  88.2 54.7 %collective-permute-start.25 = (bf16[512,896]{1,0:T(8,128)(2,1)S(1)}, bf16[512,896]{1,0:T(8,128)(2,1)S(1)}, u32[]{:S(2)}, u32[]{:S(2)}) collective-permute-start(bf16[512,896]{1,0:T(8,128)(2,1)S(1)} %collective-permute-done.22.refs_11_.refs_19_), channel_id=1, source_target_pairs={{0,16},{16,32},{32,48},{48,0},{64,80},{80,96},{96,112},{112,64},{1... | collective-permute-start | bytes 2752520 | tf_op jit(solution)/shard_map/ppermute | solution.py:166
  103.5 74.9 %collective-permute-start.10 = (bf16[96,8192]{1,0:T(8,128)(2,1)}, bf16[96,8192]{1,0:T(8,128)(2,1)}, u32[]{:S(2)}, u32[]{:S(2)}) collective-permute-start(bf16[96,8192]{1,0:T(8,128)(2,1)} %collective-permute-done.9.refs_0_.refs_10_), channel_id=1, source_target_pairs={{0,4},{1,5},{2,6},{3,7},{4,8},{5,9},{6,10},{7,11},{8,12},{9,13},{1... | collective-permute-start | bytes 4718600 | tf_op jit(solution)/shard_map/ppermute | solution.py:166
  105.7 39.7 %collective-permute-start.26 = (bf16[512,896]{1,0:T(8,128)(2,1)S(1)}, bf16[512,896]{1,0:T(8,128)(2,1)}, u32[]{:S(2)}, u32[]{:S(2)}) collective-permute-start(bf16[512,896]{1,0:T(8,128)(2,1)S(1)} %collective-permute-done.19.refs_10_.refs_18_), channel_id=1, source_target_pairs={{0,48},{16,0},{32,16},{48,32},{64,112},{80,64},{96,80},{112,96},{1... | collective-permute-start | bytes 2752520 | tf_op jit(solution)/shard_map/ppermute | solution.py:166
  123.3 28.3 %collective-permute-start.2 = (bf16[48,8192]{1,0:T(8,128)(2,1)S(1)}, bf16[48,8192]{1,0:T(8,128)(2,1)S(1)}, u32[]{:S(2)}, u32[]{:S(2)}) collective-permute-start(bf16[48,8192]{1,0:T(8,128)(2,1)S(1)} %slice.26), channel_id=1, source_target_pairs={{0,4},{1,5},{2,6},{3,7},{4,8},{5,9},{6,10},{7,11},{8,12},{9,13},{1... | collective-permute-start | bytes 2359304 | tf_op jit(solution)/shard_map/ppermute | solution.py:166
  124.5 54.0 %collective-permute-start.11 = (bf16[96,8192]{1,0:T(8,128)(2,1)}, bf16[96,8192]{1,0:T(8,128)(2,1)}, u32[]{:S(2)}, u32[]{:S(2)}) collective-permute-start(bf16[96,8192]{1,0:T(8,128)(2,1)} %collective-permute-done.9.refs_0_.refs_10_), channel_id=1, source_target_pairs={{0,12},{1,13},{2,14},{3,15},{4,0},{5,1},{6,2},{7,3},{8,4},{9,5},{1... | collective-permute-start | bytes 4718600 | tf_op jit(solution)/shard_map/ppermute | solution.py:166
  142.9 28.2 %collective-permute-start.3 = (bf16[48,8192]{1,0:T(8,128)(2,1)S(1)}, bf16[48,8192]{1,0:T(8,128)(2,1)S(1)}, u32[]{:S(2)}, u32[]{:S(2)}) collective-permute-start(bf16[48,8192]{1,0:T(8,128)(2,1)S(1)} %slice.27), channel_id=1, source_target_pairs={{0,12},{1,13},{2,14},{3,15},{4,0},{5,1},{6,2},{7,3},{8,4},{9,5},{1... | collective-permute-start | bytes 2359304 | tf_op jit(solution)/shard_map/ppermute | solution.py:166
  145.4 41.5 %collective-permute-start.5 = (bf16[96,8192]{1,0:T(8,128)(2,1)S(1)}, bf16[96,8192]{1,0:T(8,128)(2,1)S(1)}, u32[]{:S(2)}, u32[]{:S(2)}) collective-permute-start(bf16[96,8192]{1,0:T(8,128)(2,1)S(1)} %collective-permute-done.refs_1_), channel_id=1, source_target_pairs={{0,1},{1,0},{2,3},{3,2},{4,5},{5,4},{6,7},{7,6},{8,9},{9,8},{10,11... | collective-permute-start | bytes 4718600 | tf_op jit(solution)/shard_map/ppermute | solution.py:166
  151.6 36.7 %collective-permute-start.6 = (bf16[96,8192]{1,0:T(8,128)(2,1)S(1)}, bf16[96,8192]{1,0:T(8,128)(2,1)S(1)}, u32[]{:S(2)}, u32[]{:S(2)}) collective-permute-start(bf16[96,8192]{1,0:T(8,128)(2,1)S(1)} %collective-permute-done.1.refs_2_), channel_id=1, source_target_pairs={{0,1},{1,0},{2,3},{3,2},{4,5},{5,4},{6,7},{7,6},{8,9},{9,8},{10,11... | collective-permute-start | bytes 4718600 | tf_op jit(solution)/shard_map/ppermute | solution.py:166
  171.1 9.2 %collective-permute-start.7 = (bf16[48,8192]{1,0:T(8,128)(2,1)S(1)}, bf16[48,8192]{1,0:T(8,128)(2,1)S(1)}, u32[]{:S(2)}, u32[]{:S(2)}) collective-permute-start(bf16[48,8192]{1,0:T(8,128)(2,1)S(1)} %collective-permute-done.2.refs_3_), channel_id=1, source_target_pairs={{0,1},{1,0},{2,3},{3,2},{4,5},{5,4},{6,7},{7,6},{8,9},{9,8},{10,11... | collective-permute-start | bytes 2359304 | tf_op jit(solution)/shard_map/ppermute | solution.py:166
  178.5 42.1 %collective-permute-start.12 = (bf16[96,8192]{1,0:T(8,128)(2,1)}, bf16[96,8192]{1,0:T(8,128)(2,1)}, u32[]{:S(2)}, u32[]{:S(2)}) collective-permute-start(bf16[96,8192]{1,0:T(8,128)(2,1)} %collective-permute-done.9.refs_0_.refs_10_), channel_id=1, source_target_pairs={{0,1},{1,0},{2,3},{3,2},{4,5},{5,4},{6,7},{7,6},{8,9},{9,8},{10,11... | collective-permute-start | bytes 4718600 | tf_op jit(solution)/shard_map/ppermute | solution.py:166
  180.4 40.3 %collective-permute-start.13 = (bf16[96,8192]{1,0:T(8,128)(2,1)}, bf16[96,8192]{1,0:T(8,128)(2,1)}, u32[]{:S(2)}, u32[]{:S(2)}) collective-permute-start(bf16[96,8192]{1,0:T(8,128)(2,1)} %collective-permute-done.10.refs_1_.refs_11_), channel_id=1, source_target_pairs={{0,1},{1,0},{2,3},{3,2},{4,5},{5,4},{6,7},{7,6},{8,9},{9,8},{10,11... | collective-permute-start | bytes 4718600 | tf_op jit(solution)/shard_map/ppermute | solution.py:166
  182.4 40.9 %collective-permute-start.14 = (bf16[96,8192]{1,0:T(8,128)(2,1)}, bf16[96,8192]{1,0:T(8,128)(2,1)}, u32[]{:S(2)}, u32[]{:S(2)}) collective-permute-start(bf16[96,8192]{1,0:T(8,128)(2,1)} %collective-permute-done.11.refs_2_.refs_12_), channel_id=1, source_target_pairs={{0,1},{1,0},{2,3},{3,2},{4,5},{5,4},{6,7},{7,6},{8,9},{9,8},{10,11... | collective-permute-start | bytes 4718600 | tf_op jit(solution)/shard_map/ppermute | solution.py:166
  186.9 20.8 %collective-permute-start.15 = (bf16[48,8192]{1,0:T(8,128)(2,1)}, bf16[48,8192]{1,0:T(8,128)(2,1)}, u32[]{:S(2)}, u32[]{:S(2)}) collective-permute-start(bf16[48,8192]{1,0:T(8,128)(2,1)} %slice.28), channel_id=1, source_target_pairs={{0,4},{1,5},{2,6},{3,7},{4,8},{5,9},{6,10},{7,11},{8,12},{9,13},{1... | collective-permute-start | bytes 2359304 | tf_op jit(solution)/shard_map/ppermute | solution.py:166
  188.2 20.4 %collective-permute-start.16 = (bf16[48,8192]{1,0:T(8,128)(2,1)}, bf16[48,8192]{1,0:T(8,128)(2,1)}, u32[]{:S(2)}, u32[]{:S(2)}) collective-permute-start(bf16[48,8192]{1,0:T(8,128)(2,1)} %slice.29), channel_id=1, source_target_pairs={{0,12},{1,13},{2,14},{3,15},{4,0},{5,1},{6,2},{7,3},{8,4},{9,5},{1... | collective-permute-start | bytes 2359304 | tf_op jit(solution)/shard_map/ppermute | solution.py:166
  207.7 25.4 %collective-permute-start.17 = (bf16[48,8192]{1,0:T(8,128)(2,1)}, bf16[48,8192]{1,0:T(8,128)(2,1)S(1)}, u32[]{:S(2)}, u32[]{:S(2)}) collective-permute-start(bf16[48,8192]{1,0:T(8,128)(2,1)} %collective-permute-done.15.refs_6_.refs_16_), channel_id=1, source_target_pairs={{0,1},{1,0},{2,3},{3,2},{4,5},{5,4},{6,7},{7,6},{8,9},{9,8},{10,11... | collective-permute-start | bytes 2359304 | tf_op jit(solution)/shard_map/ppermute | solution.py:166
  208.6 24.5 %collective-permute-start.18 = (bf16[48,8192]{1,0:T(8,128)(2,1)}, bf16[48,8192]{1,0:T(8,128)(2,1)S(1)}, u32[]{:S(2)}, u32[]{:S(2)}) collective-permute-start(bf16[48,8192]{1,0:T(8,128)(2,1)} %collective-permute-done.16.refs_7_.refs_17_), channel_id=1, source_target_pairs={{0,1},{1,0},{2,3},{3,2},{4,5},{5,4},{6,7},{7,6},{8,9},{9,8},{10,11... | collective-permute-start | bytes 2359304 | tf_op jit(solution)/shard_map/ppermute | solution.py:166
  220.6 27.8 %collective-permute-start.21 = (bf16[512,896]{1,0:T(8,128)(2,1)S(1)}, bf16[512,896]{1,0:T(8,128)(2,1)S(1)}, u32[]{:S(2)}, u32[]{:S(2)}) collective-permute-start(bf16[512,896]{1,0:T(8,128)(2,1)S(1)} %copy-done.24), channel_id=1, source_target_pairs={{0,16},{16,32},{32,48},{48,0},{64,80},{80,96},{96,112},{112,64},{1... | collective-permute-start | bytes 2752520 | tf_op jit(solution)/shard_map/ppermute | solution.py:166
  220.7 27.8 %collective-permute-start.24 = (bf16[512,896]{1,0:T(8,128)(2,1)S(1)}, bf16[512,896]{1,0:T(8,128)(2,1)}, u32[]{:S(2)}, u32[]{:S(2)}) collective-permute-start(bf16[512,896]{1,0:T(8,128)(2,1)S(1)} %copy-done.26), channel_id=1, source_target_pairs={{0,48},{16,0},{32,16},{48,32},{64,112},{80,64},{96,80},{112,96},{1... | collective-permute-start | bytes 2752520 | tf_op jit(solution)/shard_map/ppermute | solution.py:166
  (30 other events, 1018.3 us)

commit v2 on v0

v2 whole, which is shorter than its diff:
```python
import functools

import jax
import jax.numpy as jnp
from jax import lax
from jax.experimental import pallas as pl
from jax.experimental.pallas import tpu as pltpu
from jax.sharding import PartitionSpec as P

N = 896
KB = 1024
ROWS = 96


def row_perm(fn):
    return [(yl * 4 + z, fn(yl, z)[0] * 4 + fn(yl, z)[1]) for yl in range(2) for z in range(4)]


def col_perm(fn):
    at = lambda x, yh, c: x * 4 + yh * 2 + c
    return [(at(x, yh, c), at(*fn(x, yh, c))) for x in range(4) for yh in range(2) for c in range(2)]


WAYS = {
    "z+": ("row", row_perm(lambda yl, z: (yl, (z + 1) % 4))),
    "z-": ("row", row_perm(lambda yl, z: (yl, (z + 3) % 4))),
    "yl": ("row", row_perm(lambda yl, z: (1 - yl, z))),
    "x+": ("col", col_perm(lambda x, yh, c: ((x + 1) % 4, yh, c))),
    "x-": ("col", col_perm(lambda x, yh, c: ((x + 3) % 4, yh, c))),
    "yh": ("col", col_perm(lambda x, yh, c: (x, 1 - yh, c))),
    "co": ("col", col_perm(lambda x, yh, c: (x, yh, 1 - c))),
}

STEPS = [
    ("wLA", "z+", "wA"), ("wRB", "z-", "wB"), ("tLA", "x+", "tA"), ("tRB", "x-", "tB"), ("w1A", "yl", "wA"),
    ("wLB", "z+", "wB"), ("wRA", "z-", "wA"), ("tLB", "x+", "tB"), ("tRA", "x-", "tA"),
    ("t1A", "yh", "tA"), ("w1B", "yl", "wB"), ("t1B", "yh", "tB"), ("ct", "co", "t"),
    ("tDA", "x+", "tLA"), ("tDB", "x-", "tRB"), ("wDA", "z+", "wLA"), ("wDB", "z-", "wRB"),
    ("ctLA", "co", "tLA"), ("ctRB", "co", "tRB"),
    ("w1LA", "z+", "w1A"), ("ctLB", "co", "tLB"), ("ctRA", "co", "tRA"),
    ("t1LA", "x+", "t1A"), ("t1RA", "x-", "t1A"), ("ct1A", "co", "t1A"),
    ("kA",),
    ("ctDA", "co", "tDA"), ("ctDB", "co", "tDB"),
    ("w1RB", "z-", "w1B"), ("w1LB", "z+", "w1B"), ("w1RA", "z-", "w1A"),
    ("kB",),
    ("t1RB", "x-", "t1B"), ("t1LB", "x+", "t1B"), ("t1DA", "x+", "t1LA"),
    ("ct1B", "co", "t1B"), ("ct1LA", "co", "t1LA"), ("ct1RA", "co", "t1RA"),
    ("w1DA", "z+", "w1LA"), ("w1DB", "z-", "w1RB"),
    ("t1DB", "x-", "t1RB"), ("ct1RB", "co", "t1RB"), ("ct1LB", "co", "t1LB"),
    ("kC",),
    ("kD",),
    ("ct1DA", "co", "t1DA"), ("ct1DB", "co", "t1DB"),
    ("kE",),
    ("kF",),
]
FAR = {"": 0, "L": 3, "R": 1, "D": 2}


def rows_of(names):
    return [
        (p, ROWS * i + r) for i, n in enumerate(names) for p, r in ([(n, 0)] if n in ("t", "ct") else [(n + "A", 0), (n + "B", 48)])
    ]


A = ["t", "tL", "tR", "ct", "ctL", "ctR"]
D0 = ["tD", "ctD"]
B1 = ["t1", "t1L", "t1R", "ct1", "ct1L", "ct1R"]
B2 = ["t1D", "ct1D"]

W = [(b, 0, KB, [(f"w{k}A", 0, 512), (f"w{k}B", 0, 512)]) for b, k in enumerate(("", "L", "R", "D", "1", "1L", "1R", "1D"))]

KERNELS = {
    "kA": (A, [], [(0, 576, W[:3])]),
    "kB": (A + D0, [("kA", 0)], [(0, 576, W[3:5]), (576, 768, W[:5])]),
    "kC": (B1, [], [(0, 576, W[:5])]),
    "kD": (A + D0 + B1, [("kB", 0), ("kC", 768)], [(0, 1344, W[5:7])]),
    "kE": (B2, [], [(0, 192, W[:7])]),
    "kF": (A + D0 + B1 + B2, [("kD", 0), ("kE", 1344)], [(0, 1536, W[7:])]),
}
TILE = 288
VMEM, LAST_VMEM = 5, 7


def kernel(plan, *refs):
    r, c = lax.axis_index("row"), lax.axis_index("col")
    yl, z, x, yh, core = r // 4, r % 4, c // 4, c // 2 % 2, c % 2
    block_at = [((yl ^ one) * 4 + (z + FAR[k]) % 4) * KB for one in range(2) for k in ("", "L", "R", "D")]
    n_t, n_w, n_a = len(plan["t"]), len(plan["w"]), len(plan["acc"])
    t_refs, w_refs, a_refs = refs[:n_t], refs[n_t : n_t + n_w], refs[n_t + n_w : n_t + n_w + n_a]
    out_ref, *rest = refs[n_t + n_w + n_a :]
    rows_all = plan["rows"]

    def product(r, e, piece):
        block, k0, _, arrays = piece
        total, k = None, k0
        for name, first, rows in arrays:
            cols = pl.ds(pl.multiple_of(block_at[block] + k, 128), rows)
            lhs = [t_refs[i][:, cols] for i, (row, n) in enumerate(plan["t"]) if r <= row < e]
            lhs = lhs[0] if len(lhs) == 1 else jnp.concatenate(lhs, axis=0)
            part = jnp.dot(lhs, w_refs[plan["w"].index(name)][pl.ds(first, rows), :], preferred_element_type=jnp.float32)
            total = part if total is None else total + part
            k += rows
        return total

    tiles, have = [], {}
    for i, (first, rows) in enumerate(plan["acc"]):
        for r in range(first, first + rows, ROWS):
            have[r] = (i, r - first)
    done = set()
    for lo, hi, pieces in plan["groups"]:
        r = lo
        while r < hi:
            e, of = r, have.get(r)
            while e < hi and e - r < plan["tile"] and (e in done) == (r in done) and (
                e in done or (None if have.get(e) is None else have[e][0]) == (None if of is None else of[0])
            ):
                e += ROWS
            total = None
            for piece in pieces:
                part = product(r, e, piece)
                total = part if total is None else total + part
            at = pl.ds(r, e - r)
            if r in done:
                total = total + out_ref[at]
            elif of is not None:
                total = total + a_refs[of[0]][pl.ds(of[1], e - r)]
            if plan["last"]:
                res, sem_o = rest
                res[at] = total.astype(jnp.bfloat16)
                for q in range(r, e, ROWS):
                    name = plan["names"][q // ROWS]
                    far = (x + FAR[name.lstrip("ct1")]) % 4 * 4 + (yh ^ ("1" in name)) * 2 + (core ^ ("c" in name))
                    to = pl.multiple_of(far * ROWS, 16)
                    tiles.append(pltpu.make_async_copy(res.at[pl.ds(q, ROWS)], out_ref.at[pl.ds(to, ROWS)], sem_o.at[q // ROWS]))
                    tiles[-1].start()
            else:
                out_ref[at] = total
            done |= set(range(r, e, ROWS))
            r = e
    for c in tiles:
        c.wait()
    for r in range(0, rows_all, ROWS):
        if r not in done:
            i, first = have[r]
            out_ref[pl.ds(r, ROWS)] = a_refs[i][pl.ds(first, ROWS)]


def call(name, got, sums):
    names, taken, groups = KERNELS[name]
    rows, last = ROWS * len(names), name == "kF"
    layout = rows_of(names)
    arrays = []
    for _, _, pieces in groups:
        for piece in pieces:
            arrays += [a for a, _, _ in piece[3] if a not in arrays]
    t_in, w_in, a_in = [got[n] for n, _ in layout], [got[n] for n in arrays], [sums[k] for k, _ in taken]
    plan = {
        "rows": rows,
        "names": names,
        "t": [(r, v.shape[0]) for (_, r), v in zip(layout, t_in)],
        "w": arrays,
        "acc": [(first, v.shape[0]) for (_, first), v in zip(taken, a_in)],
        "groups": groups,
        "tile": TILE,
        "last": last,
    }
    width = [sum(p[2] for p in pieces) for _, _, pieces in groups]
    scratch = []
    if last:
        scratch += [pltpu.VMEM((rows, N), jnp.bfloat16), pltpu.SemaphoreType.DMA((16,))]
    flops = sum(2 * (hi - lo) * k * N for (lo, hi, _), k in zip(groups, width))
    vmem = pl.BlockSpec(memory_space=pltpu.VMEM)
    ins = [pltpu.with_memory_space_constraint(v, pltpu.MemorySpace.VMEM) for v in (*t_in, *w_in, *a_in)]
    return pl.pallas_call(
        functools.partial(kernel, plan),
        out_shape=jax.ShapeDtypeStruct((rows, N), jnp.bfloat16) if last else pltpu.MemorySpace.VMEM((rows, N), jnp.float32),
        in_specs=[vmem] * len(ins),
        out_specs=pl.BlockSpec(memory_space=pltpu.HBM) if last else vmem,
        scratch_shapes=scratch,
        compiler_params=pltpu.CompilerParams(vmem_limit_bytes=(LAST_VMEM if last else VMEM) * 2**20),
        cost_estimate=pl.CostEstimate(flops=flops, bytes_accessed=rows * sum(width) * 2, transcendentals=0),
    )(*ins)


def on_device(tokens, up_weight):
    got = {"t": tokens, "tA": tokens[:48], "tB": tokens[48:], "wA": up_weight[:512], "wB": up_weight[512:]}
    sums = {}
    for step in STEPS:
        if len(step) == 3:
            got[step[0]] = lax.ppermute(got[step[2]], *WAYS[step[1]])
        else:
            sums[step[0]] = call(step[0], got, sums)
    return sums["kF"]


def solution(mesh):
    return jax.shard_map(
        on_device, mesh=mesh, in_specs=(P(("row", "col"), None), P("row", "col")), out_specs=P("row", "col"), check_vma=False
    )
```

time: 353 us -> 231 us (0.65)
  waiting for transfers between devices: 307 us -> 135 us
  starting transfers between devices: 0.04 us -> 63.8 us
  matrix products: 32.5 us -> 0 us
  Pallas kernels: 0 us -> 28.3 us
  between operations: 13.4 us -> 0.32 us
    all_gather x2 -> x0, waiting for transfers between devices: 305 us -> none  [the longest x1 155 us: on_device(): w_column = lax.all_gather(up_weight, 'row', axis=0, tiled=True)]
    ppermute x0 -> x43, waiting for transfers between devices: none -> 135 us  [on_device(): got[step[0]] = lax.ppermute(got[step[2]], *WAYS[step[1]])]
    ppermute x0 -> x43, starting transfers between devices: none -> 63.8 us  [on_device(): got[step[0]] = lax.ppermute(got[step[2]], *WAYS[step[1]])]
    dot_general x1 -> x0, matrix products: 32.5 us -> none  [on_device(): jnp.dot(lax.all_gather(tokens, 'col', axis=0, tiled=True), w_column, pref...]
    pallas_call x0 -> x6, Pallas kernels: none -> 28.3 us  [call(): pl.pallas_call(functools.partial(kernel, plan), out_shape=jax.ShapeDtypeS...]
  transfers between devices with their start and end apart: 2 -> 43, of which waited for: 2 -> 15; matrix products, arithmetic and copies ran while one was open for 0% -> 0% of each run, Pallas kernels for 0% -> 10%
where the time goes in v2:
time: 231 us; the launch traced here: 229 us
  waiting for transfers between devices  135 us (58%)
  starting transfers between devices  63.8 us (28%)
  Pallas kernels  28.3 us (12%)
    ppermute x43, waiting for transfers between devices, on_device(): got[step[0]] = lax.ppermute(got[step[2]], *WAYS[step[1]])  135 us
    ppermute x43, starting transfers between devices, on_device(): got[step[0]] = lax.ppermute(got[step[2]], *WAYS[step[1]])  63.8 us
    pallas_call x6, Pallas kernels, call(): pl.pallas_call(functools.partial(kernel, plan), out_shape=jax.ShapeDtypeS...  28.3 us
  transfers between devices with their start and end apart: 43, of which 15 were waited for; matrix products, arithmetic and copies ran while one was open for 0% of the time, Pallas kernels for 10%

profile of v2, /device:TPU:1, one launch (start us, length us, event | category | flops | bytes accessed | tf_op | source)
XLA Modules:
  0.0 228.8 jit_solution(9141310580842611878)
XLA Ops:
  1.6 3.8 %collective-permute-start.13 = (bf16[48,8192]{1,0:T(8,128)(2,1)S(1)}, bf16[48,8192]{1,0:T(8,128)(2,1)S(1)}, u32[]{:S(2)}, u32[]{:S(2)}) collective-permute-start(bf16[48,8192]{1,0:T(8,128)(2,1)S(1)} %get-tuple-element.8), channel_id=1, source_target_pairs={{0,2},{1,3},{2,0},{3,1},{4,6},{5,7},{6,4},{7,5},{8,10},{9,11},{10,... | collective-permute-start | bytes 2359304 | tf_op jit(solution)/shard_map/ppermute | solution.py:190
  8.4 14.1 %collective-permute-done.13.refs_0_.refs_14_ = bf16[48,8192]{1,0:T(8,128)(2,1)S(1)} collective-permute-done((bf16[48,8192]{1,0:T(8,128)(2,1)S(1)}, bf16[48,8192]{1,0:T(8,128)(2,1)S(1)}, u32[]{:S(2)}, u32[]{:S(2)}) %collective-permute-start.13) | collective-permute-done | bytes 786464 | tf_op jit(solution)/shard_map/ppermute | solution.py:190
  23.7 15.6 %collective-permute-done.14.refs_1_.refs_15_ = bf16[48,8192]{1,0:T(8,128)(2,1)S(1)} collective-permute-done((bf16[48,8192]{1,0:T(8,128)(2,1)S(1)}, bf16[48,8192]{1,0:T(8,128)(2,1)S(1)}, u32[]{:S(2)}, u32[]{:S(2)}) %collective-permute-start.14) | collective-permute-done | bytes 786464 | tf_op jit(solution)/shard_map/ppermute | solution.py:190
  39.3 2.5 %collective-permute-start.2 = (bf16[48,8192]{1,0:T(8,128)(2,1)S(1)}, bf16[48,8192]{1,0:T(8,128)(2,1)S(1)}, u32[]{:S(2)}, u32[]{:S(2)}) collective-permute-start(bf16[48,8192]{1,0:T(8,128)(2,1)S(1)} %get-tuple-element.8), channel_id=1, source_target_pairs={{0,12},{1,13},{2,14},{3,15},{4,0},{5,1},{6,2},{7,3},{8,4},{9,5},{1... | collective-permute-start | bytes 2359304 | tf_op jit(solution)/shard_map/ppermute | solution.py:190
  44.7 2.2 collective-permute-start.39
  46.9 9.1 %collective-permute-done.2.refs_3_ = bf16[48,8192]{1,0:T(8,128)(2,1)S(1)} collective-permute-done((bf16[48,8192]{1,0:T(8,128)(2,1)S(1)}, bf16[48,8192]{1,0:T(8,128)(2,1)S(1)}, u32[]{:S(2)}, u32[]{:S(2)}) %collective-permute-start.2) | collective-permute-done | bytes 786464 | tf_op jit(solution)/shard_map/ppermute | solution.py:190
  59.3 3.8 %collective-permute-start.42 = (bf16[512,896]{1,0:T(8,128)(2,1)S(1)}, bf16[512,896]{1,0:T(8,128)(2,1)S(1)}, u32[]{:S(2)}, u32[]{:S(2)}) collective-permute-start(bf16[512,896]{1,0:T(8,128)(2,1)S(1)} %get-tuple-element.6.refs_10_.refs_18_.refs_12_.refs_4_), channel_id=1, source_target_pairs={{0,48},{16,0},{32,16},{48,32},{64,112},{80,64},{96,80},{112,96},{1... | collective-permute-start | bytes 2752520 | tf_op jit(solution)/shard_map/ppermute | solution.py:190
  63.1 15.9 %collective-permute-done.32.refs_17_.refs_21_.refs_13_ = bf16[512,896]{1,0:T(8,128)(2,1)S(1)} collective-permute-done((bf16[512,896]{1,0:T(8,128)(2,1)S(1)}, bf16[512,896]{1,0:T(8,128)(2,1)S(1)}, u32[]{:S(2)}, u32[]{:S(2)}) %collective-permute-start.32) | collective-permute-done | bytes 917536 | tf_op jit(solution)/shard_map/ppermute | solution.py:190
  81.7 2.4 %collective-permute-done.41.refs_13_.refs_21_.refs_15_.refs_7_ = bf16[512,896]{1,0:T(8,128)(2,1)S(1)} collective-permute-done((bf16[512,896]{1,0:T(8,128)(2,1)S(1)}, bf16[512,896]{1,0:T(8,128)(2,1)S(1)}, u32[]{:S(2)}, u32[]{:S(2)}) %collective-permute-start.41) | collective-permute-done | bytes 917536 | tf_op jit(solution)/shard_map/ppermute | solution.py:190
  84.6 4.1 %collective-permute-start.19 = (bf16[48,8192]{1,0:T(8,128)(2,1)S(1)}, bf16[48,8192]{1,0:T(8,128)(2,1)S(1)}, u32[]{:S(2)}, u32[]{:S(2)}) collective-permute-start(bf16[48,8192]{1,0:T(8,128)(2,1)S(1)} %collective-permute-done.13.refs_0_.refs_14_), channel_id=1, source_target_pairs={{0,1},{1,0},{2,3},{3,2},{4,5},{5,4},{6,7},{7,6},{8,9},{9,8},{10,11... | collective-permute-start | bytes 2359304 | tf_op jit(solution)/shard_map/ppermute | solution.py:190
  88.6 9.1 %collective-permute-done.15.refs_2_.refs_16_ = bf16[48,8192]{1,0:T(8,128)(2,1)S(1)} collective-permute-done((bf16[48,8192]{1,0:T(8,128)(2,1)S(1)}, bf16[48,8192]{1,0:T(8,128)(2,1)S(1)}, u32[]{:S(2)}, u32[]{:S(2)}) %collective-permute-start.15) | collective-permute-done | bytes 786464 | tf_op jit(solution)/shard_map/ppermute | solution.py:190
  97.8 4.4 %collective-permute-start.20 = (bf16[48,8192]{1,0:T(8,128)(2,1)S(1)}, bf16[48,8192]{1,0:T(8,128)(2,1)S(1)}, u32[]{:S(2)}, u32[]{:S(2)}) collective-permute-start(bf16[48,8192]{1,0:T(8,128)(2,1)S(1)} %collective-permute-done.14.refs_1_.refs_15_), channel_id=1, source_target_pairs={{0,1},{1,0},{2,3},{3,2},{4,5},{5,4},{6,7},{7,6},{8,9},{9,8},{10,11... | collective-permute-start | bytes 2359304 | tf_op jit(solution)/shard_map/ppermute | solution.py:190
  102.4 12.2 %collective-permute-done.16.refs_3_.refs_17_ = bf16[48,8192]{1,0:T(8,128)(2,1)S(1)} collective-permute-done((bf16[48,8192]{1,0:T(8,128)(2,1)S(1)}, bf16[48,8192]{1,0:T(8,128)(2,1)S(1)}, u32[]{:S(2)}, u32[]{:S(2)}) %collective-permute-start.16) | collective-permute-done | bytes 786464 | tf_op jit(solution)/shard_map/ppermute | solution.py:190
  114.6 2.4 %collective-permute-start.5 = (bf16[48,8192]{1,0:T(8,128)(2,1)S(1)}, bf16[48,8192]{1,0:T(8,128)(2,1)S(1)}, u32[]{:S(2)}, u32[]{:S(2)}) collective-permute-start(bf16[48,8192]{1,0:T(8,128)(2,1)S(1)} %collective-permute-done.refs_1_), channel_id=1, source_target_pairs={{0,1},{1,0},{2,3},{3,2},{4,5},{5,4},{6,7},{7,6},{8,9},{9,8},{10,11... | collective-permute-start | bytes 2359304 | tf_op jit(solution)/shard_map/ppermute | solution.py:190
  123.2 2.8 %collective-permute-start.33 = (bf16[512,896]{1,0:T(8,128)(2,1)S(1)}, bf16[512,896]{1,0:T(8,128)(2,1)S(1)}, u32[]{:S(2)}, u32[]{:S(2)}) collective-permute-start(bf16[512,896]{1,0:T(8,128)(2,1)S(1)} %collective-permute-done.32.refs_17_.refs_21_.refs_13_), channel_id=1, source_target_pairs={{0,48},{16,0},{32,16},{48,32},{64,112},{80,64},{96,80},{112,96},{1... | collective-permute-start | bytes 2752520 | tf_op jit(solution)/shard_map/ppermute | solution.py:190
  126.0 12.8 %collective-permute-done.9.refs_10_ = bf16[48,8192]{1,0:T(8,128)(2,1)S(1)} collective-permute-done((bf16[48,8192]{1,0:T(8,128)(2,1)S(1)}, bf16[48,8192]{1,0:T(8,128)(2,1)S(1)}, u32[]{:S(2)}, u32[]{:S(2)}) %collective-permute-start.9) | collective-permute-done | bytes 786464 | tf_op jit(solution)/shard_map/ppermute | solution.py:190
  138.8 3.8 %collective-permute-start.40 = (bf16[512,896]{1,0:T(8,128)(2,1)S(1)}, bf16[512,896]{1,0:T(8,128)(2,1)S(1)}, u32[]{:S(2)}, u32[]{:S(2)}) collective-permute-start(bf16[512,896]{1,0:T(8,128)(2,1)S(1)} %collective-permute-done.39.refs_15_.refs_23_.refs_17_.refs_9_), channel_id=1, source_target_pairs={{0,48},{16,0},{32,16},{48,32},{64,112},{80,64},{96,80},{112,96},{1... | collective-permute-start | bytes 2752520 | tf_op jit(solution)/shard_map/ppermute | solution.py:190
  142.6 2.5 %collective-permute-done.30.refs_26_.refs_14_ = bf16[512,896]{1,0:T(8,128)(2,1)S(1)} collective-permute-done((bf16[512,896]{1,0:T(8,128)(2,1)S(1)}, bf16[512,896]{1,0:T(8,128)(2,1)S(1)}, u32[]{:S(2)}, u32[]{:S(2)}) %collective-permute-start.30) | collective-permute-done | bytes 917536 | tf_op jit(solution)/shard_map/ppermute | solution.py:190
  145.1 2.6 %collective-permute-start.21 = (bf16[48,8192]{1,0:T(8,128)(2,1)S(1)}, bf16[48,8192]{1,0:T(8,128)(2,1)S(1)}, u32[]{:S(2)}, u32[]{:S(2)}) collective-permute-start(bf16[48,8192]{1,0:T(8,128)(2,1)S(1)} %collective-permute-done.15.refs_2_.refs_16_), channel_id=1, source_target_pairs={{0,1},{1,0},{2,3},{3,2},{4,5},{5,4},{6,7},{7,6},{8,9},{9,8},{10,11... | collective-permute-start | bytes 2359304 | tf_op jit(solution)/shard_map/ppermute | solution.py:190
  147.8 17.0 %collective-permute-done.38.refs_14_.refs_18_.refs_10_ = bf16[512,896]{1,0:T(8,128)(2,1)S(1)} collective-permute-done((bf16[512,896]{1,0:T(8,128)(2,1)S(1)}, bf16[512,896]{1,0:T(8,128)(2,1)S(1)}, u32[]{:S(2)}, u32[]{:S(2)}) %collective-permute-start.38) | collective-permute-done | bytes 917536 | tf_op jit(solution)/shard_map/ppermute | solution.py:190
  164.8 2.6 %collective-permute-start.22 = (bf16[48,8192]{1,0:T(8,128)(2,1)S(1)}, bf16[48,8192]{1,0:T(8,128)(2,1)S(1)}, u32[]{:S(2)}, u32[]{:S(2)}) collective-permute-start(bf16[48,8192]{1,0:T(8,128)(2,1)S(1)} %collective-permute-done.16.refs_3_.refs_17_), channel_id=1, source_target_pairs={{0,1},{1,0},{2,3},{3,2},{4,5},{5,4},{6,7},{7,6},{8,9},{9,8},{10,11... | collective-permute-start | bytes 2359304 | tf_op jit(solution)/shard_map/ppermute | solution.py:190
  167.4 17.0 %collective-permute-done.35.refs_27_.refs_15_ = bf16[512,896]{1,0:T(8,128)(2,1)S(1)} collective-permute-done((bf16[512,896]{1,0:T(8,128)(2,1)S(1)}, bf16[512,896]{1,0:T(8,128)(2,1)S(1)}, u32[]{:S(2)}, u32[]{:S(2)}) %collective-permute-start.35) | collective-permute-done | bytes 917536 | tf_op jit(solution)/shard_map/ppermute | solution.py:190
  185.8 2.5 %collective-permute-start.26 = (bf16[48,8192]{1,0:T(8,128)(2,1)S(1)}, bf16[48,8192]{1,0:T(8,128)(2,1)S(1)}, u32[]{:S(2)}, u32[]{:S(2)}) collective-permute-start(bf16[48,8192]{1,0:T(8,128)(2,1)S(1)} %collective-permute-done.18.refs_5_.refs_19_), channel_id=1, source_target_pairs={{0,12},{1,13},{2,14},{3,15},{4,0},{5,1},{6,2},{7,3},{8,4},{9,5},{1... | collective-permute-start | bytes 2359304 | tf_op jit(solution)/shard_map/ppermute | solution.py:190
  188.3 2.6 %collective-permute-start.11 = (bf16[48,8192]{1,0:T(8,128)(2,1)S(1)}, bf16[48,8192]{1,0:T(8,128)(2,1)S(1)}, u32[]{:S(2)}, u32[]{:S(2)}) collective-permute-start(bf16[48,8192]{1,0:T(8,128)(2,1)S(1)} %collective-permute-done.9.refs_10_), channel_id=1, source_target_pairs={{0,1},{1,0},{2,3},{3,2},{4,5},{5,4},{6,7},{7,6},{8,9},{9,8},{10,11... | collective-permute-start | bytes 2359304 | tf_op jit(solution)/shard_map/ppermute | solution.py:190
  191.1 3.8 %shard_map.28.refs_24_ = f32[576,896]{1,0:T(8,128)S(1)} custom-call(bf16[96,8192]{1,0:T(8,128)(2,1)S(1)} %copy-done, bf16[48,8192]{1,0:T(8,128)(2,1)S(1)} %collective-permute-done.refs_1_, bf16[48,8192]{1,0:T(8,128)(2,1)S(1)} %collective-permute-done.1.refs_2_, bf16[48,8192]{1,0:T(8,128)(2,1)S(1)} %collective-permute-done.2.refs_3_, ...), custom_call_target="tpu_custom_call" | custom-call | flops 3170893824 | bytes 3538944 | tf_op jit(solution)/shard_map/pallas_call | solution.py:174
  194.9 6.3 %shard_map.30.refs_31_ = f32[576,896]{1,0:T(8,128)S(1)} custom-call(bf16[48,8192]{1,0:T(8,128)(2,1)S(1)} %collective-permute-done.13.refs_0_.refs_14_, bf16[48,8192]{1,0:T(8,128)(2,1)S(1)} %collective-permute-done.14.refs_1_.refs_15_, bf16[48,8192]{1,0:T(8,128)(2,1)S(1)} %collective-permute-done.15.refs_2_.refs_16_, ...), custom_call_target="tpu_custom_call" | custom-call | flops 5284823040 | bytes 5898240 | tf_op jit(solution)/shard_map/pallas_call | solution.py:174
  201.2 2.7 %collective-permute-done.25.refs_0_.refs_26_ = bf16[48,8192]{1,0:T(8,128)(2,1)S(1)} collective-permute-done((bf16[48,8192]{1,0:T(8,128)(2,1)S(1)}, bf16[48,8192]{1,0:T(8,128)(2,1)S(1)}, u32[]{:S(2)}, u32[]{:S(2)}) %collective-permute-start.25) | collective-permute-done | bytes 786464 | tf_op jit(solution)/shard_map/ppermute | solution.py:190
  206.6 3.5 %collective-permute-start.27 = (bf16[48,8192]{1,0:T(8,128)(2,1)S(1)}, bf16[48,8192]{1,0:T(8,128)(2,1)S(1)}, u32[]{:S(2)}, u32[]{:S(2)}) collective-permute-start(bf16[48,8192]{1,0:T(8,128)(2,1)S(1)} %collective-permute-done.25.refs_0_.refs_26_), channel_id=1, source_target_pairs={{0,1},{1,0},{2,3},{3,2},{4,5},{5,4},{6,7},{7,6},{8,9},{9,8},{10,11... | collective-permute-start | bytes 2359304 | tf_op jit(solution)/shard_map/ppermute | solution.py:190
  210.4 4.7 %shard_map.29.refs_30_ = f32[768,896]{1,0:T(8,128)S(1)} custom-call(bf16[96,8192]{1,0:T(8,128)(2,1)S(1)} %copy-done, bf16[48,8192]{1,0:T(8,128)(2,1)S(1)} %collective-permute-done.refs_1_, bf16[48,8192]{1,0:T(8,128)(2,1)S(1)} %collective-permute-done.1.refs_2_, bf16[48,8192]{1,0:T(8,128)(2,1)S(1)} %collective-permute-done.2.refs_3_, ...), custom_call_target="tpu_custom_call" | custom-call | flops 3875536896 | bytes 11010048 | tf_op jit(solution)/shard_map/pallas_call | solution.py:174
  215.1 6.0 %shard_map.31.refs_32_ = f32[1344,896]{1,0:T(8,128)S(1)} custom-call(bf16[96,8192]{1,0:T(8,128)(2,1)S(1)} %copy-done, bf16[48,8192]{1,0:T(8,128)(2,1)S(1)} %collective-permute-done.refs_1_, bf16[48,8192]{1,0:T(8,128)(2,1)S(1)} %collective-permute-done.1.refs_2_, bf16[48,8192]{1,0:T(8,128)(2,1)S(1)} %collective-permute-done.2.refs_3_, ...), custom_call_target="tpu_custom_call" | custom-call | flops 4932501504 | bytes 5505024 | tf_op jit(solution)/shard_map/pallas_call | solution.py:174
  221.1 3.1 %shard_map.32.refs_33_ = f32[192,896]{1,0:T(8,128)S(1)} custom-call(bf16[48,8192]{1,0:T(8,128)(2,1)S(1)} %collective-permute-done.25.refs_0_.refs_26_, bf16[48,8192]{1,0:T(8,128)(2,1)S(1)} %collective-permute-done.26.refs_1_.refs_27_, bf16[48,8192]{1,0:T(8,128)(2,1)S(1)} %collective-permute-done.27.refs_2_.refs_28_, ...), custom_call_target="tpu_custom_call" | custom-call | flops 2466250752 | bytes 2752512 | tf_op jit(solution)/shard_map/pallas_call | solution.py:174
  224.2 4.4 %shard_map.33 = bf16[1536,896]{1,0:T(8,128)(2,1)} custom-call(bf16[96,8192]{1,0:T(8,128)(2,1)S(1)} %copy-done, bf16[48,8192]{1,0:T(8,128)(2,1)S(1)} %collective-permute-done.refs_1_, bf16[48,8192]{1,0:T(8,128)(2,1)S(1)} %collective-permute-done.1.refs_2_, bf16[48,8192]{1,0:T(8,128)(2,1)S(1)} %collective-permute-done.2.refs_3_, ...), custom_call_target="tpu_custom_call" | custom-call | flops 2818572288 | bytes 3145728 | tf_op jit(solution)/shard_map/pallas_call | solution.py:174
  (66 shorter events, 26.3 us)
Async XLA Ops:
  1.6 20.8 %collective-permute-start.13 = (bf16[48,8192]{1,0:T(8,128)(2,1)S(1)}, bf16[48,8192]{1,0:T(8,128)(2,1)S(1)}, u32[]{:S(2)}, u32[]{:S(2)}) collective-permute-start(bf16[48,8192]{1,0:T(8,128)(2,1)S(1)} %get-tuple-element.8), channel_id=1, source_target_pairs={{0,2},{1,3},{2,0},{3,1},{4,6},{5,7},{6,4},{7,5},{8,10},{9,11},{10,... | collective-permute-start | bytes 2359304 | tf_op jit(solution)/shard_map/ppermute | solution.py:190
  5.4 33.9 %collective-permute-start.14 = (bf16[48,8192]{1,0:T(8,128)(2,1)S(1)}, bf16[48,8192]{1,0:T(8,128)(2,1)S(1)}, u32[]{:S(2)}, u32[]{:S(2)}) collective-permute-start(bf16[48,8192]{1,0:T(8,128)(2,1)S(1)} %get-tuple-element.7), channel_id=1, source_target_pairs={{0,2},{1,3},{2,0},{3,1},{4,6},{5,7},{6,4},{7,5},{8,10},{9,11},{10,... | collective-permute-start | bytes 2359304 | tf_op jit(solution)/shard_map/ppermute | solution.py:190
  5.5 36.3 %collective-permute-start = (bf16[48,8192]{1,0:T(8,128)(2,1)S(1)}, bf16[48,8192]{1,0:T(8,128)(2,1)S(1)}, u32[]{:S(2)}, u32[]{:S(2)}) collective-permute-start(bf16[48,8192]{1,0:T(8,128)(2,1)S(1)} %get-tuple-element.8), channel_id=1, source_target_pairs={{0,4},{1,5},{2,6},{3,7},{4,8},{5,9},{6,10},{7,11},{8,12},{9,13},{1... | collective-permute-start | bytes 2359304 | tf_op jit(solution)/shard_map/ppermute | solution.py:190
  6.7 36.3 %collective-permute-start.3 = (bf16[48,8192]{1,0:T(8,128)(2,1)S(1)}, bf16[48,8192]{1,0:T(8,128)(2,1)S(1)}, u32[]{:S(2)}, u32[]{:S(2)}) collective-permute-start(bf16[48,8192]{1,0:T(8,128)(2,1)S(1)} %get-tuple-element.7), channel_id=1, source_target_pairs={{0,12},{1,13},{2,14},{3,15},{4,0},{5,1},{6,2},{7,3},{8,4},{9,5},{1... | collective-permute-start | bytes 2359304 | tf_op jit(solution)/shard_map/ppermute | solution.py:190
  8.2 36.5 %collective-permute-start.1 = (bf16[48,8192]{1,0:T(8,128)(2,1)S(1)}, bf16[48,8192]{1,0:T(8,128)(2,1)S(1)}, u32[]{:S(2)}, u32[]{:S(2)}) collective-permute-start(bf16[48,8192]{1,0:T(8,128)(2,1)S(1)} %get-tuple-element.7), channel_id=1, source_target_pairs={{0,4},{1,5},{2,6},{3,7},{4,8},{5,9},{6,10},{7,11},{8,12},{9,13},{1... | collective-permute-start | bytes 2359304 | tf_op jit(solution)/shard_map/ppermute | solution.py:190
  22.5 36.8 %collective-permute-start.29 = (bf16[512,896]{1,0:T(8,128)(2,1)S(1)}, bf16[512,896]{1,0:T(8,128)(2,1)S(1)}, u32[]{:S(2)}, u32[]{:S(2)}) collective-permute-start(bf16[512,896]{1,0:T(8,128)(2,1)S(1)} %get-tuple-element.6.refs_10_.refs_18_.refs_12_.refs_4_), channel_id=1, source_target_pairs={{0,64},{16,80},{32,96},{48,112},{64,0},{80,16},{96,32},{112,48},{1... | collective-permute-start | bytes 2752520 | tf_op jit(solution)/shard_map/ppermute | solution.py:190
  41.8 37.2 %collective-permute-start.32 = (bf16[512,896]{1,0:T(8,128)(2,1)S(1)}, bf16[512,896]{1,0:T(8,128)(2,1)S(1)}, u32[]{:S(2)}, u32[]{:S(2)}) collective-permute-start(bf16[512,896]{1,0:T(8,128)(2,1)S(1)} %get-tuple-element.5.refs_11_.refs_19_.refs_13_.refs_5_), channel_id=1, source_target_pairs={{0,64},{16,80},{32,96},{48,112},{64,0},{80,16},{96,32},{112,48},{1... | collective-permute-start | bytes 2752520 | tf_op jit(solution)/shard_map/ppermute | solution.py:190
  43.1 37.1 %collective-permute-start.37 = (bf16[512,896]{1,0:T(8,128)(2,1)S(1)}, bf16[512,896]{1,0:T(8,128)(2,1)S(1)}, u32[]{:S(2)}, u32[]{:S(2)}) collective-permute-start(bf16[512,896]{1,0:T(8,128)(2,1)S(1)} %get-tuple-element.6.refs_10_.refs_18_.refs_12_.refs_4_), channel_id=1, source_target_pairs={{0,16},{16,32},{32,48},{48,0},{64,80},{80,96},{96,112},{112,64},{1... | collective-permute-start | bytes 2752520 | tf_op jit(solution)/shard_map/ppermute | solution.py:190
  44.7 36.9 %collective-permute-start.39 = (bf16[512,896]{1,0:T(8,128)(2,1)S(1)}, bf16[512,896]{1,0:T(8,128)(2,1)S(1)}, u32[]{:S(2)}, u32[]{:S(2)}) collective-permute-start(bf16[512,896]{1,0:T(8,128)(2,1)S(1)} %get-tuple-element.5.refs_11_.refs_19_.refs_13_.refs_5_), channel_id=1, source_target_pairs={{0,48},{16,0},{32,16},{48,32},{64,112},{80,64},{96,80},{112,96},{1... | collective-permute-start | bytes 2752520 | tf_op jit(solution)/shard_map/ppermute | solution.py:190
  56.0 28.0 %collective-permute-start.41 = (bf16[512,896]{1,0:T(8,128)(2,1)S(1)}, bf16[512,896]{1,0:T(8,128)(2,1)S(1)}, u32[]{:S(2)}, u32[]{:S(2)}) collective-permute-start(bf16[512,896]{1,0:T(8,128)(2,1)S(1)} %get-tuple-element.5.refs_11_.refs_19_.refs_13_.refs_5_), channel_id=1, source_target_pairs={{0,16},{16,32},{32,48},{48,0},{64,80},{80,96},{96,112},{112,64},{1... | collective-permute-start | bytes 2752520 | tf_op jit(solution)/shard_map/ppermute | solution.py:190
  59.3 25.3 %collective-permute-start.42 = (bf16[512,896]{1,0:T(8,128)(2,1)S(1)}, bf16[512,896]{1,0:T(8,128)(2,1)S(1)}, u32[]{:S(2)}, u32[]{:S(2)}) collective-permute-start(bf16[512,896]{1,0:T(8,128)(2,1)S(1)} %get-tuple-element.6.refs_10_.refs_18_.refs_12_.refs_4_), channel_id=1, source_target_pairs={{0,48},{16,0},{32,16},{48,32},{64,112},{80,64},{96,80},{112,96},{1... | collective-permute-start | bytes 2752520 | tf_op jit(solution)/shard_map/ppermute | solution.py:190
  80.2 21.9 %collective-permute-start.18 = (bf16[48,8192]{1,0:T(8,128)(2,1)S(1)}, bf16[48,8192]{1,0:T(8,128)(2,1)S(1)}, u32[]{:S(2)}, u32[]{:S(2)}) collective-permute-start(bf16[48,8192]{1,0:T(8,128)(2,1)S(1)} %collective-permute-done.14.refs_1_.refs_15_), channel_id=1, source_target_pairs={{0,12},{1,13},{2,14},{3,15},{4,0},{5,1},{6,2},{7,3},{8,4},{9,5},{1... | collective-permute-start | bytes 2359304 | tf_op jit(solution)/shard_map/ppermute | solution.py:190
  81.7 32.9 %collective-permute-start.16 = (bf16[48,8192]{1,0:T(8,128)(2,1)S(1)}, bf16[48,8192]{1,0:T(8,128)(2,1)S(1)}, u32[]{:S(2)}, u32[]{:S(2)}) collective-permute-start(bf16[48,8192]{1,0:T(8,128)(2,1)S(1)} %collective-permute-done.14.refs_1_.refs_15_), channel_id=1, source_target_pairs={{0,4},{1,5},{2,6},{3,7},{4,8},{5,9},{6,10},{7,11},{8,12},{9,13},{1... | collective-permute-start | bytes 2359304 | tf_op jit(solution)/shard_map/ppermute | solution.py:190
  84.0 33.0 %collective-permute-start.17 = (bf16[48,8192]{1,0:T(8,128)(2,1)S(1)}, bf16[48,8192]{1,0:T(8,128)(2,1)S(1)}, u32[]{:S(2)}, u32[]{:S(2)}) collective-permute-start(bf16[48,8192]{1,0:T(8,128)(2,1)S(1)} %collective-permute-done.13.refs_0_.refs_14_), channel_id=1, source_target_pairs={{0,12},{1,13},{2,14},{3,15},{4,0},{5,1},{6,2},{7,3},{8,4},{9,5},{1... | collective-permute-start | bytes 2359304 | tf_op jit(solution)/shard_map/ppermute | solution.py:190
  84.6 32.4 %collective-permute-start.19 = (bf16[48,8192]{1,0:T(8,128)(2,1)S(1)}, bf16[48,8192]{1,0:T(8,128)(2,1)S(1)}, u32[]{:S(2)}, u32[]{:S(2)}) collective-permute-start(bf16[48,8192]{1,0:T(8,128)(2,1)S(1)} %collective-permute-done.13.refs_0_.refs_14_), channel_id=1, source_target_pairs={{0,1},{1,0},{2,3},{3,2},{4,5},{5,4},{6,7},{7,6},{8,9},{9,8},{10,11... | collective-permute-start | bytes 2359304 | tf_op jit(solution)/shard_map/ppermute | solution.py:190
  97.8 19.8 %collective-permute-start.20 = (bf16[48,8192]{1,0:T(8,128)(2,1)S(1)}, bf16[48,8192]{1,0:T(8,128)(2,1)S(1)}, u32[]{:S(2)}, u32[]{:S(2)}) collective-permute-start(bf16[48,8192]{1,0:T(8,128)(2,1)S(1)} %collective-permute-done.14.refs_1_.refs_15_), channel_id=1, source_target_pairs={{0,1},{1,0},{2,3},{3,2},{4,5},{5,4},{6,7},{7,6},{8,9},{9,8},{10,11... | collective-permute-start | bytes 2359304 | tf_op jit(solution)/shard_map/ppermute | solution.py:190
  102.1 23.9 %collective-permute-start.4 = (bf16[96,8192]{1,0:T(8,128)(2,1)S(1)}, bf16[96,8192]{1,0:T(8,128)(2,1)S(1)}, u32[]{:S(2)}, u32[]{:S(2)}) collective-permute-start(bf16[96,8192]{1,0:T(8,128)(2,1)S(1)} %copy-done), channel_id=1, source_target_pairs={{0,1},{1,0},{2,3},{3,2},{4,5},{5,4},{6,7},{7,6},{8,9},{9,8},{10,11... | collective-permute-start | bytes 4718600 | tf_op jit(solution)/shard_map/ppermute | solution.py:190
  118.9 19.9 %collective-permute-start.9 = (bf16[48,8192]{1,0:T(8,128)(2,1)S(1)}, bf16[48,8192]{1,0:T(8,128)(2,1)S(1)}, u32[]{:S(2)}, u32[]{:S(2)}) collective-permute-start(bf16[48,8192]{1,0:T(8,128)(2,1)S(1)} %collective-permute-done.refs_1_), channel_id=1, source_target_pairs={{0,4},{1,5},{2,6},{3,7},{4,8},{5,9},{6,10},{7,11},{8,12},{9,13},{1... | collective-permute-start | bytes 2359304 | tf_op jit(solution)/shard_map/ppermute | solution.py:190
  120.0 22.6 %collective-permute-start.10 = (bf16[48,8192]{1,0:T(8,128)(2,1)S(1)}, bf16[48,8192]{1,0:T(8,128)(2,1)S(1)}, u32[]{:S(2)}, u32[]{:S(2)}) collective-permute-start(bf16[48,8192]{1,0:T(8,128)(2,1)S(1)} %collective-permute-done.3.refs_4_), channel_id=1, source_target_pairs={{0,12},{1,13},{2,14},{3,15},{4,0},{5,1},{6,2},{7,3},{8,4},{9,5},{1... | collective-permute-start | bytes 2359304 | tf_op jit(solution)/shard_map/ppermute | solution.py:190
  121.6 23.6 %collective-permute-start.30 = (bf16[512,896]{1,0:T(8,128)(2,1)S(1)}, bf16[512,896]{1,0:T(8,128)(2,1)S(1)}, u32[]{:S(2)}, u32[]{:S(2)}) collective-permute-start(bf16[512,896]{1,0:T(8,128)(2,1)S(1)} %collective-permute-done.29.refs_16_.refs_20_.refs_12_), channel_id=1, source_target_pairs={{0,16},{16,32},{32,48},{48,0},{64,80},{80,96},{96,112},{112,64},{1... | collective-permute-start | bytes 2752520 | tf_op jit(solution)/shard_map/ppermute | solution.py:190
  123.2 24.5 %collective-permute-start.33 = (bf16[512,896]{1,0:T(8,128)(2,1)S(1)}, bf16[512,896]{1,0:T(8,128)(2,1)S(1)}, u32[]{:S(2)}, u32[]{:S(2)}) collective-permute-start(bf16[512,896]{1,0:T(8,128)(2,1)S(1)} %collective-permute-done.32.refs_17_.refs_21_.refs_13_), channel_id=1, source_target_pairs={{0,48},{16,0},{32,16},{48,32},{64,112},{80,64},{96,80},{112,96},{1... | collective-permute-start | bytes 2752520 | tf_op jit(solution)/shard_map/ppermute | solution.py:190
  126.0 38.8 %collective-permute-start.38 = (bf16[512,896]{1,0:T(8,128)(2,1)S(1)}, bf16[512,896]{1,0:T(8,128)(2,1)S(1)}, u32[]{:S(2)}, u32[]{:S(2)}) collective-permute-start(bf16[512,896]{1,0:T(8,128)(2,1)S(1)} %collective-permute-done.37.refs_12_.refs_20_.refs_14_.refs_6_), channel_id=1, source_target_pairs={{0,16},{16,32},{32,48},{48,0},{64,80},{80,96},{96,112},{112,64},{1... | collective-permute-start | bytes 2752520 | tf_op jit(solution)/shard_map/ppermute | solution.py:190
  138.8 28.6 %collective-permute-start.40 = (bf16[512,896]{1,0:T(8,128)(2,1)S(1)}, bf16[512,896]{1,0:T(8,128)(2,1)S(1)}, u32[]{:S(2)}, u32[]{:S(2)}) collective-permute-start(bf16[512,896]{1,0:T(8,128)(2,1)S(1)} %collective-permute-done.39.refs_15_.refs_23_.refs_17_.refs_9_), channel_id=1, source_target_pairs={{0,48},{16,0},{32,16},{48,32},{64,112},{80,64},{96,80},{112,96},{1... | collective-permute-start | bytes 2752520 | tf_op jit(solution)/shard_map/ppermute | solution.py:190
  142.6 41.9 %collective-permute-start.35 = (bf16[512,896]{1,0:T(8,128)(2,1)S(1)}, bf16[512,896]{1,0:T(8,128)(2,1)S(1)}, u32[]{:S(2)}, u32[]{:S(2)}) collective-permute-start(bf16[512,896]{1,0:T(8,128)(2,1)S(1)} %collective-permute-done.32.refs_17_.refs_21_.refs_13_), channel_id=1, source_target_pairs={{0,16},{16,32},{32,48},{48,0},{64,80},{80,96},{96,112},{112,64},{1... | collective-permute-start | bytes 2752520 | tf_op jit(solution)/shard_map/ppermute | solution.py:190
  145.1 40.5 %collective-permute-start.21 = (bf16[48,8192]{1,0:T(8,128)(2,1)S(1)}, bf16[48,8192]{1,0:T(8,128)(2,1)S(1)}, u32[]{:S(2)}, u32[]{:S(2)}) collective-permute-start(bf16[48,8192]{1,0:T(8,128)(2,1)S(1)} %collective-permute-done.15.refs_2_.refs_16_), channel_id=1, source_target_pairs={{0,1},{1,0},{2,3},{3,2},{4,5},{5,4},{6,7},{7,6},{8,9},{9,8},{10,11... | collective-permute-start | bytes 2359304 | tf_op jit(solution)/shard_map/ppermute | solution.py:190
  147.8 38.1 %collective-permute-start.24 = (bf16[48,8192]{1,0:T(8,128)(2,1)S(1)}, bf16[48,8192]{1,0:T(8,128)(2,1)S(1)}, u32[]{:S(2)}, u32[]{:S(2)}) collective-permute-start(bf16[48,8192]{1,0:T(8,128)(2,1)S(1)} %collective-permute-done.18.refs_5_.refs_19_), channel_id=1, source_target_pairs={{0,1},{1,0},{2,3},{3,2},{4,5},{5,4},{6,7},{7,6},{8,9},{9,8},{10,11... | collective-permute-start | bytes 2359304 | tf_op jit(solution)/shard_map/ppermute | solution.py:190
  164.8 23.5 %collective-permute-start.22 = (bf16[48,8192]{1,0:T(8,128)(2,1)S(1)}, bf16[48,8192]{1,0:T(8,128)(2,1)S(1)}, u32[]{:S(2)}, u32[]{:S(2)}) collective-permute-start(bf16[48,8192]{1,0:T(8,128)(2,1)S(1)} %collective-permute-done.16.refs_3_.refs_17_), channel_id=1, source_target_pairs={{0,1},{1,0},{2,3},{3,2},{4,5},{5,4},{6,7},{7,6},{8,9},{9,8},{10,11... | collective-permute-start | bytes 2359304 | tf_op jit(solution)/shard_map/ppermute | solution.py:190
  167.4 23.5 %collective-permute-start.23 = (bf16[48,8192]{1,0:T(8,128)(2,1)S(1)}, bf16[48,8192]{1,0:T(8,128)(2,1)S(1)}, u32[]{:S(2)}, u32[]{:S(2)}) collective-permute-start(bf16[48,8192]{1,0:T(8,128)(2,1)S(1)} %collective-permute-done.17.refs_4_.refs_18_), channel_id=1, source_target_pairs={{0,1},{1,0},{2,3},{3,2},{4,5},{5,4},{6,7},{7,6},{8,9},{9,8},{10,11... | collective-permute-start | bytes 2359304 | tf_op jit(solution)/shard_map/ppermute | solution.py:190
  184.5 30.6 %collective-permute-start.36 = (bf16[512,896]{1,0:T(8,128)(2,1)S(1)}, bf16[512,896]{1,0:T(8,128)(2,1)S(1)}, u32[]{:S(2)}, u32[]{:S(2)}) collective-permute-start(bf16[512,896]{1,0:T(8,128)(2,1)S(1)} %collective-permute-done.29.refs_16_.refs_20_.refs_12_), channel_id=1, source_target_pairs={{0,48},{16,0},{32,16},{48,32},{64,112},{80,64},{96,80},{112,96},{1... | collective-permute-start | bytes 2752520 | tf_op jit(solution)/shard_map/ppermute | solution.py:190
  191.0 19.1 %collective-permute-start.12 = (bf16[48,8192]{1,0:T(8,128)(2,1)S(1)}, bf16[48,8192]{1,0:T(8,128)(2,1)S(1)}, u32[]{:S(2)}, u32[]{:S(2)}) collective-permute-start(bf16[48,8192]{1,0:T(8,128)(2,1)S(1)} %collective-permute-done.10.refs_11_), channel_id=1, source_target_pairs={{0,1},{1,0},{2,3},{3,2},{4,5},{5,4},{6,7},{7,6},{8,9},{9,8},{10,11... | collective-permute-start | bytes 2359304 | tf_op jit(solution)/shard_map/ppermute | solution.py:190
  203.9 20.3 %collective-permute-start.31 = (bf16[512,896]{1,0:T(8,128)(2,1)S(1)}, bf16[512,896]{1,0:T(8,128)(2,1)S(1)}, u32[]{:S(2)}, u32[]{:S(2)}) collective-permute-start(bf16[512,896]{1,0:T(8,128)(2,1)S(1)} %collective-permute-done.30.refs_26_.refs_14_), channel_id=1, source_target_pairs={{0,16},{16,32},{32,48},{48,0},{64,80},{80,96},{96,112},{112,64},{1... | collective-permute-start | bytes 2752520 | tf_op jit(solution)/shard_map/ppermute | solution.py:190
  204.5 19.7 %collective-permute-start.34 = (bf16[512,896]{1,0:T(8,128)(2,1)S(1)}, bf16[512,896]{1,0:T(8,128)(2,1)S(1)}, u32[]{:S(2)}, u32[]{:S(2)}) collective-permute-start(bf16[512,896]{1,0:T(8,128)(2,1)S(1)} %collective-permute-done.33.refs_29_.refs_17_), channel_id=1, source_target_pairs={{0,48},{16,0},{32,16},{48,32},{64,112},{80,64},{96,80},{112,96},{1... | collective-permute-start | bytes 2752520 | tf_op jit(solution)/shard_map/ppermute | solution.py:190
  (13 other events, 242.5 us)

commit v3 on v2

v3 whole, which is shorter than its diff:
```python
import functools
import itertools

import jax
import jax.numpy as jnp
from jax import lax
from jax.experimental import pallas as pl
from jax.experimental.pallas import tpu as pltpu
from jax.sharding import PartitionSpec as P

N = 896
KB = 1024
ROWS = 96


F = 256
H = (KB - F) // 2


def way(fn):
    at = lambda yl, z, x, yh, c: (yl * 4 + z % 4) * 16 + x % 4 * 4 + yh * 2 + c
    places = itertools.product(range(2), range(4), range(4), range(2), range(2))
    return [(at(*p), at(*fn(*p))) for p in places]


WAYS = {
    "zP": way(lambda yl, z, x, yh, c: (yl, z + 1 - 2 * c, x, yh, c)),
    "zM": way(lambda yl, z, x, yh, c: (yl, z - 1 + 2 * c, x, yh, c)),
    "xP": way(lambda yl, z, x, yh, c: (yl, z, x + 1 - 2 * c, yh, c)),
    "xM": way(lambda yl, z, x, yh, c: (yl, z, x - 1 + 2 * c, yh, c)),
    "yl": way(lambda yl, z, x, yh, c: (1 - yl, z, x, yh, c)),
    "yh": way(lambda yl, z, x, yh, c: (yl, z, x, 1 - yh, c)),
    "co": way(lambda yl, z, x, yh, c: (yl, z, x, yh, 1 - c)),
}

STEPS = [
    ("t1", "yh", "t"), ("tP", "xP", "t"), ("tM", "xM", "t"),
    ("FP", "zP", "F"), ("FM", "zM", "F"), ("SP", "zP", "S"), ("SM", "zM", "S"), ("ct", "co", "t"),
    ("FD", "zP", "FP"),
    ("S1a", "yl", "Sa"), ("S1b", "yl", "Sb"),
    ("t1P", "xP", "t1"), ("t1M", "xM", "t1"), ("ct1", "co", "t1"), ("ctP", "co", "tP"), ("ctM", "co", "tM"), ("tD", "xP", "tP"),
    ("SD", "zP", "SP"),
    ("kA",),
    ("F1", "yl", "F"), ("F1P", "yl", "FP"), ("F1M", "yl", "FM"),
    ("S1aP", "zP", "S1a"), ("S1aM", "zM", "S1a"), ("F1D", "yl", "FD"),
    ("S1bP", "zP", "S1b"), ("S1bM", "zM", "S1b"),
    ("kB",),
    ("t1D", "xP", "t1P"), ("ct1P", "co", "t1P"), ("ct1M", "co", "t1M"),
    ("kC",),
    ("S1aD", "zP", "S1aP"),
    ("ctD", "co", "tD"),
    ("kD",),
    ("S1bD", "zP", "S1bP"),
    ("kE",),
    ("ct1D", "co", "t1D"),
    ("kF",),
    ("kG",),
]
A = ["t", "tP", "tM", "t1", "ct", "ctP", "ctM", "ct1"]
B1 = ["t1P", "t1M", "ct1P", "ct1M"]
D0 = ["tD", "ctD"]
B2 = ["t1D", "ct1D"]

W0 = [(b, 0, [(f"F{k}", F), (f"S{k}", KB - F)]) for b, k in enumerate(("", "P", "M"))]
WD = [(3, 0, [("FD", F), ("SD", KB - F)])]
S1 = [(4, F, [("S1a", H), ("S1b", H)])]
W1 = [(4, 0, [("F1", F)])] + [(b, 0, [(f"F1{k}", F), (f"S1a{k}", H), (f"S1b{k}", H)]) for b, k in ((5, "P"), (6, "M"))]
W1D = [(7, 0, [("F1D", F), ("S1aD", H), ("S1bD", H)])]

KERNELS = {
    "kA": (A, [], [(0, 768, W0)]),
    "kB": (A, [("kA", 0)], [(0, 768, WD + S1)]),
    "kC": (B1, [], [(0, 384, W0 + WD + S1)]),
    "kD": (D0, [], [(0, 192, W0 + WD + S1)]),
    "kE": (A + B1 + D0, [("kB", 0), ("kC", 768), ("kD", 1152)], [(0, 1344, W1)]),
    "kF": (A + B1 + D0, [("kE", 0)], [(0, 1344, W1D)]),
    "kG": (B2, [], [(0, 192, W0 + WD + S1 + W1 + W1D)]),
}
TILE = 384
VMEM, LAST_VMEM = 6, 8


def kernel(plan, *refs):
    row, col = lax.axis_index("row"), lax.axis_index("col")
    yl, z, x, yh, core = row // 4, row % 4, col // 4, col // 2 % 2, col % 2
    far = lambda name, c: 3 - 2 * c if "P" in name else 1 + 2 * c if "M" in name else 2 if "D" in name else 0
    block_at = [((yl ^ one) * 4 + (z + far(k, core)) % 4) * KB for one in range(2) for k in ("", "P", "M", "D")]
    n_t, n_w, n_a = len(plan["t"]), len(plan["w"]), len(plan["acc"])
    t_refs, w_refs, a_refs = refs[:n_t], refs[n_t : n_t + n_w], refs[n_t + n_w : n_t + n_w + n_a]
    out_ref, *rest = refs[n_t + n_w + n_a + plan["onto"] :]

    def product(r, e, piece):
        block, k, arrays = piece
        total = None
        for name, rows in arrays:
            cols = pl.ds(pl.multiple_of(block_at[block] + k, 128), rows)
            lhs = jnp.concatenate([t_refs[i][:, cols] for i in range(r // ROWS, e // ROWS)], axis=0)
            part = jnp.dot(lhs, w_refs[plan["w"].index(name)][...], preferred_element_type=jnp.float32)
            total = part if total is None else total + part
            k += rows
        return total

    tiles, have = [], {}
    for i, (first, rows) in enumerate(plan["acc"]):
        for r in range(first, first + rows, ROWS):
            have[r] = (i, r - first)
    done = set()
    for lo, hi, pieces in plan["groups"]:
        r = lo
        while r < hi:
            e, of = r, have.get(r)
            while e < hi and e - r < plan["tile"] and (e in done) == (r in done) and (
                e in done or (None if have.get(e) is None else have[e][0]) == (None if of is None else of[0])
            ):
                e += ROWS
            total = None
            for piece in pieces:
                part = product(r, e, piece)
                total = part if total is None else total + part
            at = pl.ds(r, e - r)
            if r in done:
                total = total + out_ref[at]
            elif of is not None:
                total = total + a_refs[of[0]][pl.ds(of[1], e - r)]
            if plan["last"]:
                res, sem_o = rest
                res[at] = total.astype(jnp.bfloat16)
                for q in range(r, e, ROWS):
                    name = plan["names"][q // ROWS]
                    c = core ^ ("c" in name)
                    place = (x + far(name, c)) % 4 * 4 + (yh ^ ("1" in name)) * 2 + c
                    to = pl.multiple_of(place * ROWS, 16)
                    tiles.append(pltpu.make_async_copy(res.at[pl.ds(q, ROWS)], out_ref.at[pl.ds(to, ROWS)], sem_o.at[q // ROWS]))
                    tiles[-1].start()
            else:
                out_ref[at] = total
            done |= set(range(r, e, ROWS))
            r = e
    for c in tiles:
        c.wait()


def call(name, got, sums):
    names, taken, groups = KERNELS[name]
    rows, last, onto = ROWS * len(names), name in ("kF", "kG"), name == "kG"
    arrays = []
    for _, _, blocks in groups:
        for block in blocks:
            arrays += [a for a, _ in block[2] if a not in arrays]
    t_in, w_in, a_in = [got[n] for n in names], [got[n] for n in arrays], [sums[k] for k, _ in taken]
    plan = {
        "names": names,
        "t": names,
        "w": arrays,
        "acc": [(first, v.shape[0]) for (_, first), v in zip(taken, a_in)],
        "groups": groups,
        "tile": TILE,
        "last": last,
        "onto": int(onto),
    }
    width = [sum(rows for b in blocks for _, rows in b[2]) for _, _, blocks in groups]
    scratch = []
    if last:
        scratch += [pltpu.VMEM((rows, N), jnp.bfloat16), pltpu.SemaphoreType.DMA((len(names),))]
    flops = sum(2 * (hi - lo) * k * N for (lo, hi, _), k in zip(groups, width))
    vmem = pl.BlockSpec(memory_space=pltpu.VMEM)
    ins = [pltpu.with_memory_space_constraint(v, pltpu.MemorySpace.VMEM) for v in (*t_in, *w_in, *a_in)]
    n_in, hbm = len(ins), pl.BlockSpec(memory_space=pltpu.HBM)
    return pl.pallas_call(
        functools.partial(kernel, plan),
        out_shape=jax.ShapeDtypeStruct((16 * ROWS, N), jnp.bfloat16) if last else pltpu.MemorySpace.VMEM((rows, N), jnp.float32),
        in_specs=[vmem] * n_in + [hbm] * onto,
        out_specs=hbm if last else vmem,
        input_output_aliases={n_in: 0} if onto else {},
        scratch_shapes=scratch,
        compiler_params=pltpu.CompilerParams(vmem_limit_bytes=(LAST_VMEM if last else VMEM) * 2**20),
        cost_estimate=pl.CostEstimate(flops=flops, bytes_accessed=rows * sum(width) * 2, transcendentals=0),
    )(*ins, *([sums["kF"]] if onto else []))


def on_device(tokens, up_weight):
    got = {"t": tokens, "F": up_weight[:F], "S": up_weight[F:], "Sa": up_weight[F : F + H], "Sb": up_weight[F + H :]}
    sums = {}
    for step in STEPS:
        if len(step) == 3:
            got[step[0]] = lax.ppermute(got[step[2]], ("row", "col"), WAYS[step[1]])
        else:
            sums[step[0]] = call(step[0], got, sums)
    return sums["kG"]


def solution(mesh):
    return jax.shard_map(
        on_device, mesh=mesh, in_specs=(P(("row", "col"), None), P("row", "col")), out_specs=P("row", "col"), check_vma=False
    )
```

time: 231 us -> 260 us (1.13)
  waiting for transfers between devices: 135 us -> 158 us
  Pallas kernels: 28.3 us -> 31.6 us
    ppermute x43 -> x33, waiting for transfers between devices: 135 us -> 158 us  [on_device(): got[step[0]] = lax.ppermute(got[step[2]], ('row', 'col'), WAYS[step[1]])]
    pallas_call x6 -> x7, Pallas kernels: 28.3 us -> 31.6 us  [call(): pl.pallas_call(functools.partial(kernel, plan), out_shape=jax.ShapeDtypeS...]
    ppermute x43 -> x33, starting transfers between devices: 63.8 us -> 64.5 us  [on_device(): got[step[0]] = lax.ppermute(got[step[2]], ('row', 'col'), WAYS[step[1]])]
  transfers between devices with their start and end apart: 43 -> 33, of which waited for: 15 -> 12; matrix products, arithmetic and copies ran while one was open for 0% -> 1% of each run, Pallas kernels for 10% -> 10%
where the time goes in v3:
time: 260 us; the launch traced here: 258 us
  waiting for transfers between devices  158 us (61%)
  starting transfers between devices  64.5 us (25%)
  Pallas kernels  31.6 us (12%)
  local copies, waits for them, and re-layouts  2.73 us (1%)
    ppermute x33, waiting for transfers between devices, on_device(): got[step[0]] = lax.ppermute(got[step[2]], ('row', 'col'), WAYS[step[1]])  158 us
    ppermute x33, starting transfers between devices, on_device(): got[step[0]] = lax.ppermute(got[step[2]], ('row', 'col'), WAYS[step[1]])  64.5 us
    pallas_call x7, Pallas kernels, call(): pl.pallas_call(functools.partial(kernel, plan), out_shape=jax.ShapeDtypeS...  31.6 us
  transfers between devices with their start and end apart: 33, of which 12 were waited for; matrix products, arithmetic and copies ran while one was open for 1% of the time, Pallas kernels for 10%

profile of v3, /device:TPU:1, one launch (start us, length us, event | category | flops | bytes accessed | tf_op | source)
XLA Modules:
  0.0 257.6 jit_solution(14482183800634775822)
XLA Ops:
  1.2 4.6 %collective-permute-start.4 = (bf16[256,896]{1,0:T(8,128)(2,1)S(1)}, bf16[256,896]{1,0:T(8,128)(2,1)S(1)}, u32[]{:S(2)}, u32[]{:S(2)}) collective-permute-start(bf16[256,896]{1,0:T(8,128)(2,1)S(1)} %slice.12.refs_8_.refs_4_.refs_2_), channel_id=1, source_target_pairs={{0,16},{1,49},{2,18},{3,51},{4,20},{5,53},{6,22},{7,55},{8,24},{9,... | collective-permute-start | bytes 1376264 | tf_op jit(solution)/shard_map/ppermute | solution.py:186
  10.1 4.9 %collective-permute-done.4.refs_10_.refs_6_.refs_4_ = bf16[256,896]{1,0:T(8,128)(2,1)S(1)} collective-permute-done((bf16[256,896]{1,0:T(8,128)(2,1)S(1)}, bf16[256,896]{1,0:T(8,128)(2,1)S(1)}, u32[]{:S(2)}, u32[]{:S(2)}) %collective-permute-start.4) | collective-permute-done | bytes 458784 | tf_op jit(solution)/shard_map/ppermute | solution.py:186
  15.0 2.9 %collective-permute-start = (bf16[96,8192]{1,0:T(8,128)(2,1)S(1)}, bf16[96,8192]{1,0:T(8,128)(2,1)S(1)}, u32[]{:S(2)}, u32[]{:S(2)}) collective-permute-start(bf16[96,8192]{1,0:T(8,128)(2,1)S(1)} %copy-done), channel_id=1, source_target_pairs={{0,2},{1,3},{2,0},{3,1},{4,6},{5,7},{6,4},{7,5},{8,10},{9,11},{10,... | collective-permute-start | bytes 4718600 | tf_op jit(solution)/shard_map/ppermute | solution.py:186
  18.0 3.5 %collective-permute-start.5 = (bf16[768,896]{1,0:T(8,128)(2,1)S(1)}, bf16[768,896]{1,0:T(8,128)(2,1)S(1)}, u32[]{:S(2)}, u32[]{:S(2)}) collective-permute-start(bf16[768,896]{1,0:T(8,128)(2,1)S(1)} %slice.13.refs_9_.refs_5_.refs_3_), channel_id=1, source_target_pairs={{0,16},{1,49},{2,18},{3,51},{4,20},{5,53},{6,22},{7,55},{8,24},{9,... | collective-permute-start | bytes 4128776 | tf_op jit(solution)/shard_map/ppermute | solution.py:186
  21.5 11.6 %collective-permute-done.12.refs_14_.refs_12_ = bf16[256,896]{1,0:T(8,128)(2,1)S(1)} collective-permute-done((bf16[256,896]{1,0:T(8,128)(2,1)S(1)}, bf16[256,896]{1,0:T(8,128)(2,1)S(1)}, u32[]{:S(2)}, u32[]{:S(2)}) %collective-permute-start.12) | collective-permute-done | bytes 458784 | tf_op jit(solution)/shard_map/ppermute | solution.py:186
  33.1 3.7 %collective-permute-start.8 = (bf16[256,896]{1,0:T(8,128)(2,1)S(1)}, bf16[256,896]{1,0:T(8,128)(2,1)S(1)}, u32[]{:S(2)}, u32[]{:S(2)}) collective-permute-start(bf16[256,896]{1,0:T(8,128)(2,1)S(1)} %collective-permute-done.4.refs_10_.refs_6_.refs_4_), channel_id=1, source_target_pairs={{0,16},{1,49},{2,18},{3,51},{4,20},{5,53},{6,22},{7,55},{8,24},{9,... | collective-permute-start | bytes 1376264 | tf_op jit(solution)/shard_map/ppermute | solution.py:186
  36.8 11.1 %collective-permute-done.11.refs_11_.refs_13_ = bf16[384,896]{1,0:T(8,128)(2,1)S(1)} collective-permute-done((bf16[384,896]{1,0:T(8,128)(2,1)S(1)}, bf16[384,896]{1,0:T(8,128)(2,1)S(1)}, u32[]{:S(2)}, u32[]{:S(2)}) %collective-permute-start.11) | collective-permute-done | bytes 688160 | tf_op jit(solution)/shard_map/ppermute | solution.py:186
  49.4 42.1 %collective-permute-done.13.refs_15_.refs_13_ = bf16[256,896]{1,0:T(8,128)(2,1)S(1)} collective-permute-done((bf16[256,896]{1,0:T(8,128)(2,1)S(1)}, bf16[256,896]{1,0:T(8,128)(2,1)S(1)}, u32[]{:S(2)}, u32[]{:S(2)}) %collective-permute-start.13) | collective-permute-done | bytes 458784 | tf_op jit(solution)/shard_map/ppermute | solution.py:186
  91.4 3.7 %collective-permute-start.14 = (bf16[384,896]{1,0:T(8,128)(2,1)S(1)}, bf16[384,896]{1,0:T(8,128)(2,1)S(1)}, u32[]{:S(2)}, u32[]{:S(2)}) collective-permute-start(bf16[384,896]{1,0:T(8,128)(2,1)S(1)} %collective-permute-done.10.refs_10_.refs_12_), channel_id=1, source_target_pairs={{0,16},{1,49},{2,18},{3,51},{4,20},{5,53},{6,22},{7,55},{8,24},{9,... | collective-permute-start | bytes 2064392 | tf_op jit(solution)/shard_map/ppermute | solution.py:186
  95.1 6.1 %collective-permute-done.16.refs_18_.refs_16_ = bf16[256,896]{1,0:T(8,128)(2,1)S(1)} collective-permute-done((bf16[256,896]{1,0:T(8,128)(2,1)S(1)}, bf16[256,896]{1,0:T(8,128)(2,1)S(1)}, u32[]{:S(2)}, u32[]{:S(2)}) %collective-permute-start.16) | collective-permute-done | bytes 458784 | tf_op jit(solution)/shard_map/ppermute | solution.py:186
  101.3 2.5 collective-permute-start.22
  103.7 2.6 %collective-permute-start.24 = (bf16[96,8192]{1,0:T(8,128)(2,1)S(1)}, bf16[96,8192]{1,0:T(8,128)(2,1)S(1)}, u32[]{:S(2)}, u32[]{:S(2)}) collective-permute-start(bf16[96,8192]{1,0:T(8,128)(2,1)S(1)} %copy-done), channel_id=1, source_target_pairs={{0,1},{1,0},{2,3},{3,2},{4,5},{5,4},{6,7},{7,6},{8,9},{9,8},{10,11... | collective-permute-start | bytes 4718600 | tf_op jit(solution)/shard_map/ppermute | solution.py:186
  106.5 2.7 %collective-permute-start.15 = (bf16[384,896]{1,0:T(8,128)(2,1)S(1)}, bf16[384,896]{1,0:T(8,128)(2,1)S(1)}, u32[]{:S(2)}, u32[]{:S(2)}) collective-permute-start(bf16[384,896]{1,0:T(8,128)(2,1)S(1)} %collective-permute-done.11.refs_11_.refs_13_), channel_id=1, source_target_pairs={{0,16},{1,49},{2,18},{3,51},{4,20},{5,53},{6,22},{7,55},{8,24},{9,... | collective-permute-start | bytes 2064392 | tf_op jit(solution)/shard_map/ppermute | solution.py:186
  109.2 7.9 %collective-permute-done.15.refs_17_.refs_15_ = bf16[384,896]{1,0:T(8,128)(2,1)S(1)} collective-permute-done((bf16[384,896]{1,0:T(8,128)(2,1)S(1)}, bf16[384,896]{1,0:T(8,128)(2,1)S(1)}, u32[]{:S(2)}, u32[]{:S(2)}) %collective-permute-start.15) | collective-permute-done | bytes 688160 | tf_op jit(solution)/shard_map/ppermute | solution.py:186
  118.5 16.6 %collective-permute-done.22.refs_1_ = bf16[96,8192]{1,0:T(8,128)(2,1)S(1)} collective-permute-done((bf16[96,8192]{1,0:T(8,128)(2,1)S(1)}, bf16[96,8192]{1,0:T(8,128)(2,1)S(1)}, u32[]{:S(2)}, u32[]{:S(2)}) %collective-permute-start.22) | collective-permute-done | bytes 1572896 | tf_op jit(solution)/shard_map/ppermute | solution.py:186
  135.1 6.4 %collective-permute-start.25 = (bf16[96,8192]{1,0:T(8,128)(2,1)S(1)}, bf16[96,8192]{1,0:T(8,128)(2,1)S(1)}, u32[]{:S(2)}, u32[]{:S(2)}) collective-permute-start(bf16[96,8192]{1,0:T(8,128)(2,1)S(1)} %collective-permute-done.22.refs_1_), channel_id=1, source_target_pairs={{0,1},{1,0},{2,3},{3,2},{4,5},{5,4},{6,7},{7,6},{8,9},{9,8},{10,11... | collective-permute-start | bytes 4718600 | tf_op jit(solution)/shard_map/ppermute | solution.py:186
  144.7 19.4 %collective-permute-done.1.refs_0_.refs_8_ = bf16[96,8192]{1,0:T(8,128)(2,1)S(1)} collective-permute-done((bf16[96,8192]{1,0:T(8,128)(2,1)S(1)}, bf16[96,8192]{1,0:T(8,128)(2,1)S(1)}, u32[]{:S(2)}, u32[]{:S(2)}) %collective-permute-start.1) | collective-permute-done | bytes 1572896 | tf_op jit(solution)/shard_map/ppermute | solution.py:186
  164.0 3.4 %collective-permute-start.2 = (bf16[96,8192]{1,0:T(8,128)(2,1)S(1)}, bf16[96,8192]{1,0:T(8,128)(2,1)S(1)}, u32[]{:S(2)}, u32[]{:S(2)}) collective-permute-start(bf16[96,8192]{1,0:T(8,128)(2,1)S(1)} %collective-permute-done.1.refs_0_.refs_8_), channel_id=1, source_target_pairs={{0,4},{1,13},{2,6},{3,15},{4,8},{5,1},{6,10},{7,3},{8,12},{9,5},{1... | collective-permute-start | bytes 4718600 | tf_op jit(solution)/shard_map/ppermute | solution.py:186
  167.5 3.3 %collective-permute-start.29 = (bf16[96,8192]{1,0:T(8,128)(2,1)S(1)}, bf16[96,8192]{1,0:T(8,128)(2,1)S(1)}, u32[]{:S(2)}, u32[]{:S(2)}) collective-permute-start(bf16[96,8192]{1,0:T(8,128)(2,1)S(1)} %collective-permute-done.1.refs_0_.refs_8_), channel_id=1, source_target_pairs={{0,1},{1,0},{2,3},{3,2},{4,5},{5,4},{6,7},{7,6},{8,9},{9,8},{10,11... | collective-permute-start | bytes 4718600 | tf_op jit(solution)/shard_map/ppermute | solution.py:186
  170.7 2.8 %collective-permute-start.9 = (bf16[768,896]{1,0:T(8,128)(2,1)S(1)}, bf16[768,896]{1,0:T(8,128)(2,1)S(1)}, u32[]{:S(2)}, u32[]{:S(2)}) collective-permute-start(bf16[768,896]{1,0:T(8,128)(2,1)S(1)} %collective-permute-done.5.refs_11_.refs_7_.refs_5_), channel_id=1, source_target_pairs={{0,16},{1,49},{2,18},{3,51},{4,20},{5,53},{6,22},{7,55},{8,24},{9,... | collective-permute-start | bytes 4128776 | tf_op jit(solution)/shard_map/ppermute | solution.py:186
  173.6 6.0 %collective-permute-done.28.refs_1_.refs_9_ = bf16[96,8192]{1,0:T(8,128)(2,1)S(1)} collective-permute-done((bf16[96,8192]{1,0:T(8,128)(2,1)S(1)}, bf16[96,8192]{1,0:T(8,128)(2,1)S(1)}, u32[]{:S(2)}, u32[]{:S(2)}) %collective-permute-start.28) | collective-permute-done | bytes 1572896 | tf_op jit(solution)/shard_map/ppermute | solution.py:186
  179.7 8.8 %collective-permute-done.31.refs_0_.refs_12_ = bf16[96,8192]{1,0:T(8,128)(2,1)S(1)} collective-permute-done((bf16[96,8192]{1,0:T(8,128)(2,1)S(1)}, bf16[96,8192]{1,0:T(8,128)(2,1)S(1)}, u32[]{:S(2)}, u32[]{:S(2)}) %collective-permute-start.31) | collective-permute-done | bytes 1572896 | tf_op jit(solution)/shard_map/ppermute | solution.py:186
  188.5 3.7 %collective-permute-start.32 = (bf16[96,8192]{1,0:T(8,128)(2,1)S(1)}, bf16[96,8192]{1,0:T(8,128)(2,1)S(1)}, u32[]{:S(2)}, u32[]{:S(2)}) collective-permute-start(bf16[96,8192]{1,0:T(8,128)(2,1)S(1)} %collective-permute-done.31.refs_0_.refs_12_), channel_id=1, source_target_pairs={{0,1},{1,0},{2,3},{3,2},{4,5},{5,4},{6,7},{7,6},{8,9},{9,8},{10,11... | collective-permute-start | bytes 4718600 | tf_op jit(solution)/shard_map/ppermute | solution.py:186
  192.2 13.2 %collective-permute-done.2.refs_0_ = bf16[96,8192]{1,0:T(8,128)(2,1)S(1)} collective-permute-done((bf16[96,8192]{1,0:T(8,128)(2,1)S(1)}, bf16[96,8192]{1,0:T(8,128)(2,1)S(1)}, u32[]{:S(2)}, u32[]{:S(2)}) %collective-permute-start.2) | collective-permute-done | bytes 1572896 | tf_op jit(solution)/shard_map/ppermute | solution.py:186
  205.4 3.7 %collective-permute-start.3 = (bf16[96,8192]{1,0:T(8,128)(2,1)S(1)}, bf16[96,8192]{1,0:T(8,128)(2,1)S(1)}, u32[]{:S(2)}, u32[]{:S(2)}) collective-permute-start(bf16[96,8192]{1,0:T(8,128)(2,1)S(1)} %collective-permute-done.2.refs_0_), channel_id=1, source_target_pairs={{0,1},{1,0},{2,3},{3,2},{4,5},{5,4},{6,7},{7,6},{8,9},{9,8},{10,11... | collective-permute-start | bytes 4718600 | tf_op jit(solution)/shard_map/ppermute | solution.py:186
  209.0 5.0 %shard_map.28.refs_12_ = f32[768,896]{1,0:T(8,128)S(1)} custom-call(bf16[96,8192]{1,0:T(8,128)(2,1)S(1)} %copy-done, bf16[96,8192]{1,0:T(8,128)(2,1)S(1)} %collective-permute-done.22.refs_1_, bf16[96,8192]{1,0:T(8,128)(2,1)S(1)} %collective-permute-done.23.refs_2_, bf16[96,8192]{1,0:T(8,128)(2,1)S(1)} %collective-permute-done.refs_3_, ...), custom_call_target="tpu_custom_call" | custom-call | flops 4227858432 | bytes 4718592 | tf_op jit(solution)/shard_map/pallas_call | solution.py:169
  215.1 3.3 %shard_map.29.refs_21_ = f32[768,896]{1,0:T(8,128)S(1)} custom-call(bf16[96,8192]{1,0:T(8,128)(2,1)S(1)} %copy-done, bf16[96,8192]{1,0:T(8,128)(2,1)S(1)} %collective-permute-done.22.refs_1_, bf16[96,8192]{1,0:T(8,128)(2,1)S(1)} %collective-permute-done.23.refs_2_, bf16[96,8192]{1,0:T(8,128)(2,1)S(1)} %collective-permute-done.refs_3_, ...), custom_call_target="tpu_custom_call" | custom-call | flops 2466250752 | bytes 2752512 | tf_op jit(solution)/shard_map/pallas_call | solution.py:169
  221.8 4.2 %shard_map.30.refs_22_ = f32[384,896]{1,0:T(8,128)S(1)} custom-call(bf16[96,8192]{1,0:T(8,128)(2,1)S(1)} %collective-permute-done.1.refs_0_.refs_8_, bf16[96,8192]{1,0:T(8,128)(2,1)S(1)} %collective-permute-done.28.refs_1_.refs_9_, bf16[96,8192]{1,0:T(8,128)(2,1)S(1)} %collective-permute-done.29.refs_2_.refs_10_, ...), custom_call_target="tpu_custom_call" | custom-call | flops 3347054592 | bytes 3735552 | tf_op jit(solution)/shard_map/pallas_call | solution.py:169
  229.9 10.7 %collective-permute-done.18.refs_20_.refs_18_ = bf16[384,896]{1,0:T(8,128)(2,1)S(1)} collective-permute-done((bf16[384,896]{1,0:T(8,128)(2,1)S(1)}, bf16[384,896]{1,0:T(8,128)(2,1)S(1)}, u32[]{:S(2)}, u32[]{:S(2)}) %collective-permute-start.18) | collective-permute-done | bytes 688160 | tf_op jit(solution)/shard_map/ppermute | solution.py:186
  240.6 7.8 %shard_map.32.refs_17_ = f32[1344,896]{1,0:T(8,128)S(1)} custom-call(bf16[96,8192]{1,0:T(8,128)(2,1)S(1)} %copy-done, bf16[96,8192]{1,0:T(8,128)(2,1)S(1)} %collective-permute-done.22.refs_1_, bf16[96,8192]{1,0:T(8,128)(2,1)S(1)} %collective-permute-done.23.refs_2_, bf16[96,8192]{1,0:T(8,128)(2,1)S(1)} %collective-permute-done.refs_3_, ...), custom_call_target="tpu_custom_call" | custom-call | flops 5549064192 | bytes 6193152 | tf_op jit(solution)/shard_map/pallas_call | solution.py:169
  248.4 4.5 %shard_map.33.refs_22_ = bf16[1536,896]{1,0:T(8,128)(2,1)} custom-call(bf16[96,8192]{1,0:T(8,128)(2,1)S(1)} %copy-done, bf16[96,8192]{1,0:T(8,128)(2,1)S(1)} %collective-permute-done.22.refs_1_, bf16[96,8192]{1,0:T(8,128)(2,1)S(1)} %collective-permute-done.23.refs_2_, bf16[96,8192]{1,0:T(8,128)(2,1)S(1)} %collective-permute-done.refs_3_, ...), custom_call_target="tpu_custom_call" | custom-call | flops 2466250752 | bytes 2752512 | tf_op jit(solution)/shard_map/pallas_call | solution.py:169
  252.9 4.6 %shard_map.34 = bf16[1536,896]{1,0:T(8,128)(2,1)} custom-call(bf16[96,8192]{1,0:T(8,128)(2,1)S(1)} %collective-permute-done.2.refs_0_, bf16[96,8192]{1,0:T(8,128)(2,1)S(1)} %collective-permute-done.3.refs_1_, bf16[256,896]{1,0:T(8,128)(2,1)S(1)} %slice.12.refs_8_.refs_4_.refs_2_, ...), custom_call_target="tpu_custom_call", output_to_operand_aliasing={{}: (22, {})} | custom-call | flops 2818572288 | bytes 3145728 | tf_op jit(solution)/shard_map/pallas_call | solution.py:169
  (48 shorter events, 20.1 us)
Async XLA Ops:
  1.2 13.8 %collective-permute-start.4 = (bf16[256,896]{1,0:T(8,128)(2,1)S(1)}, bf16[256,896]{1,0:T(8,128)(2,1)S(1)}, u32[]{:S(2)}, u32[]{:S(2)}) collective-permute-start(bf16[256,896]{1,0:T(8,128)(2,1)S(1)} %slice.12.refs_8_.refs_4_.refs_2_), channel_id=1, source_target_pairs={{0,16},{1,49},{2,18},{3,51},{4,20},{5,53},{6,22},{7,55},{8,24},{9,... | collective-permute-start | bytes 1376264 | tf_op jit(solution)/shard_map/ppermute | solution.py:186
  5.9 12.2 %collective-permute-start.6 = (bf16[256,896]{1,0:T(8,128)(2,1)S(1)}, bf16[256,896]{1,0:T(8,128)(2,1)S(1)}, u32[]{:S(2)}, u32[]{:S(2)}) collective-permute-start(bf16[256,896]{1,0:T(8,128)(2,1)S(1)} %slice.12.refs_8_.refs_4_.refs_2_), channel_id=1, source_target_pairs={{0,48},{1,17},{2,50},{3,19},{4,52},{5,21},{6,54},{7,23},{8,56},{9,... | collective-permute-start | bytes 1376264 | tf_op jit(solution)/shard_map/ppermute | solution.py:186
  7.3 25.9 %collective-permute-start.10 = (bf16[384,896]{1,0:T(8,128)(2,1)S(1)}, bf16[384,896]{1,0:T(8,128)(2,1)S(1)}, u32[]{:S(2)}, u32[]{:S(2)}) collective-permute-start(bf16[384,896]{1,0:T(8,128)(2,1)S(1)} %get-tuple-element.6), channel_id=1, source_target_pairs={{0,64},{1,65},{2,66},{3,67},{4,68},{5,69},{6,70},{7,71},{8,72},{9,... | collective-permute-start | bytes 2064392 | tf_op jit(solution)/shard_map/ppermute | solution.py:186
  8.7 24.5 %collective-permute-start.12 = (bf16[256,896]{1,0:T(8,128)(2,1)S(1)}, bf16[256,896]{1,0:T(8,128)(2,1)S(1)}, u32[]{:S(2)}, u32[]{:S(2)}) collective-permute-start(bf16[256,896]{1,0:T(8,128)(2,1)S(1)} %slice.12.refs_8_.refs_4_.refs_2_), channel_id=1, source_target_pairs={{0,64},{1,65},{2,66},{3,67},{4,68},{5,69},{6,70},{7,71},{8,72},{9,... | collective-permute-start | bytes 1376264 | tf_op jit(solution)/shard_map/ppermute | solution.py:186
  8.8 39.1 %collective-permute-start.11 = (bf16[384,896]{1,0:T(8,128)(2,1)S(1)}, bf16[384,896]{1,0:T(8,128)(2,1)S(1)}, u32[]{:S(2)}, u32[]{:S(2)}) collective-permute-start(bf16[384,896]{1,0:T(8,128)(2,1)S(1)} %get-tuple-element.5), channel_id=1, source_target_pairs={{0,64},{1,65},{2,66},{3,67},{4,68},{5,69},{6,70},{7,71},{8,72},{9,... | collective-permute-start | bytes 2064392 | tf_op jit(solution)/shard_map/ppermute | solution.py:186
  15.0 91.4 %collective-permute-start = (bf16[96,8192]{1,0:T(8,128)(2,1)S(1)}, bf16[96,8192]{1,0:T(8,128)(2,1)S(1)}, u32[]{:S(2)}, u32[]{:S(2)}) collective-permute-start(bf16[96,8192]{1,0:T(8,128)(2,1)S(1)} %copy-done), channel_id=1, source_target_pairs={{0,2},{1,3},{2,0},{3,1},{4,6},{5,7},{6,4},{7,5},{8,10},{9,11},{10,... | collective-permute-start | bytes 4718600 | tf_op jit(solution)/shard_map/ppermute | solution.py:186
  18.0 85.7 %collective-permute-start.5 = (bf16[768,896]{1,0:T(8,128)(2,1)S(1)}, bf16[768,896]{1,0:T(8,128)(2,1)S(1)}, u32[]{:S(2)}, u32[]{:S(2)}) collective-permute-start(bf16[768,896]{1,0:T(8,128)(2,1)S(1)} %slice.13.refs_9_.refs_5_.refs_3_), channel_id=1, source_target_pairs={{0,16},{1,49},{2,18},{3,51},{4,20},{5,53},{6,22},{7,55},{8,24},{9,... | collective-permute-start | bytes 4128776 | tf_op jit(solution)/shard_map/ppermute | solution.py:186
  33.1 70.6 %collective-permute-start.7 = (bf16[768,896]{1,0:T(8,128)(2,1)S(1)}, bf16[768,896]{1,0:T(8,128)(2,1)S(1)}, u32[]{:S(2)}, u32[]{:S(2)}) collective-permute-start(bf16[768,896]{1,0:T(8,128)(2,1)S(1)} %slice.13.refs_9_.refs_5_.refs_3_), channel_id=1, source_target_pairs={{0,48},{1,17},{2,50},{3,19},{4,52},{5,21},{6,54},{7,23},{8,56},{9,... | collective-permute-start | bytes 4128776 | tf_op jit(solution)/shard_map/ppermute | solution.py:186
  33.1 16.0 %collective-permute-start.8 = (bf16[256,896]{1,0:T(8,128)(2,1)S(1)}, bf16[256,896]{1,0:T(8,128)(2,1)S(1)}, u32[]{:S(2)}, u32[]{:S(2)}) collective-permute-start(bf16[256,896]{1,0:T(8,128)(2,1)S(1)} %collective-permute-done.4.refs_10_.refs_6_.refs_4_), channel_id=1, source_target_pairs={{0,16},{1,49},{2,18},{3,51},{4,20},{5,53},{6,22},{7,55},{8,24},{9,... | collective-permute-start | bytes 1376264 | tf_op jit(solution)/shard_map/ppermute | solution.py:186
  47.9 43.5 %collective-permute-start.13 = (bf16[256,896]{1,0:T(8,128)(2,1)S(1)}, bf16[256,896]{1,0:T(8,128)(2,1)S(1)}, u32[]{:S(2)}, u32[]{:S(2)}) collective-permute-start(bf16[256,896]{1,0:T(8,128)(2,1)S(1)} %collective-permute-done.4.refs_10_.refs_6_.refs_4_), channel_id=1, source_target_pairs={{0,64},{1,65},{2,66},{3,67},{4,68},{5,69},{6,70},{7,71},{8,72},{9,... | collective-permute-start | bytes 1376264 | tf_op jit(solution)/shard_map/ppermute | solution.py:186
  49.2 52.1 %collective-permute-start.16 = (bf16[256,896]{1,0:T(8,128)(2,1)S(1)}, bf16[256,896]{1,0:T(8,128)(2,1)S(1)}, u32[]{:S(2)}, u32[]{:S(2)}) collective-permute-start(bf16[256,896]{1,0:T(8,128)(2,1)S(1)} %collective-permute-done.6.refs_12_.refs_8_.refs_6_), channel_id=1, source_target_pairs={{0,64},{1,65},{2,66},{3,67},{4,68},{5,69},{6,70},{7,71},{8,72},{9,... | collective-permute-start | bytes 1376264 | tf_op jit(solution)/shard_map/ppermute | solution.py:186
  91.4 15.1 %collective-permute-start.14 = (bf16[384,896]{1,0:T(8,128)(2,1)S(1)}, bf16[384,896]{1,0:T(8,128)(2,1)S(1)}, u32[]{:S(2)}, u32[]{:S(2)}) collective-permute-start(bf16[384,896]{1,0:T(8,128)(2,1)S(1)} %collective-permute-done.10.refs_10_.refs_12_), channel_id=1, source_target_pairs={{0,16},{1,49},{2,18},{3,51},{4,20},{5,53},{6,22},{7,55},{8,24},{9,... | collective-permute-start | bytes 2064392 | tf_op jit(solution)/shard_map/ppermute | solution.py:186
  101.3 33.9 %collective-permute-start.22 = (bf16[96,8192]{1,0:T(8,128)(2,1)S(1)}, bf16[96,8192]{1,0:T(8,128)(2,1)S(1)}, u32[]{:S(2)}, u32[]{:S(2)}) collective-permute-start(bf16[96,8192]{1,0:T(8,128)(2,1)S(1)} %copy-done), channel_id=1, source_target_pairs={{0,4},{1,13},{2,6},{3,15},{4,8},{5,1},{6,10},{7,3},{8,12},{9,5},{1... | collective-permute-start | bytes 4718600 | tf_op jit(solution)/shard_map/ppermute | solution.py:186
  103.7 37.8 %collective-permute-start.23 = (bf16[96,8192]{1,0:T(8,128)(2,1)S(1)}, bf16[96,8192]{1,0:T(8,128)(2,1)S(1)}, u32[]{:S(2)}, u32[]{:S(2)}) collective-permute-start(bf16[96,8192]{1,0:T(8,128)(2,1)S(1)} %copy-done), channel_id=1, source_target_pairs={{0,12},{1,5},{2,14},{3,7},{4,0},{5,9},{6,2},{7,11},{8,4},{9,13},{1... | collective-permute-start | bytes 4718600 | tf_op jit(solution)/shard_map/ppermute | solution.py:186
  103.7 38.2 %collective-permute-start.24 = (bf16[96,8192]{1,0:T(8,128)(2,1)S(1)}, bf16[96,8192]{1,0:T(8,128)(2,1)S(1)}, u32[]{:S(2)}, u32[]{:S(2)}) collective-permute-start(bf16[96,8192]{1,0:T(8,128)(2,1)S(1)} %copy-done), channel_id=1, source_target_pairs={{0,1},{1,0},{2,3},{3,2},{4,5},{5,4},{6,7},{7,6},{8,9},{9,8},{10,11... | collective-permute-start | bytes 4718600 | tf_op jit(solution)/shard_map/ppermute | solution.py:186
  106.4 36.7 %collective-permute-start.27 = (bf16[96,8192]{1,0:T(8,128)(2,1)S(1)}, bf16[96,8192]{1,0:T(8,128)(2,1)S(1)}, u32[]{:S(2)}, u32[]{:S(2)}) collective-permute-start(bf16[96,8192]{1,0:T(8,128)(2,1)S(1)} %collective-permute-done.refs_3_), channel_id=1, source_target_pairs={{0,1},{1,0},{2,3},{3,2},{4,5},{5,4},{6,7},{7,6},{8,9},{9,8},{10,11... | collective-permute-start | bytes 4718600 | tf_op jit(solution)/shard_map/ppermute | solution.py:186
  117.0 47.0 %collective-permute-start.1 = (bf16[96,8192]{1,0:T(8,128)(2,1)S(1)}, bf16[96,8192]{1,0:T(8,128)(2,1)S(1)}, u32[]{:S(2)}, u32[]{:S(2)}) collective-permute-start(bf16[96,8192]{1,0:T(8,128)(2,1)S(1)} %collective-permute-done.refs_3_), channel_id=1, source_target_pairs={{0,4},{1,13},{2,6},{3,15},{4,8},{5,1},{6,10},{7,3},{8,12},{9,5},{1... | collective-permute-start | bytes 4718600 | tf_op jit(solution)/shard_map/ppermute | solution.py:186
  135.1 32.3 %collective-permute-start.25 = (bf16[96,8192]{1,0:T(8,128)(2,1)S(1)}, bf16[96,8192]{1,0:T(8,128)(2,1)S(1)}, u32[]{:S(2)}, u32[]{:S(2)}) collective-permute-start(bf16[96,8192]{1,0:T(8,128)(2,1)S(1)} %collective-permute-done.22.refs_1_), channel_id=1, source_target_pairs={{0,1},{1,0},{2,3},{3,2},{4,5},{5,4},{6,7},{7,6},{8,9},{9,8},{10,11... | collective-permute-start | bytes 4718600 | tf_op jit(solution)/shard_map/ppermute | solution.py:186
  141.5 29.2 %collective-permute-start.26 = (bf16[96,8192]{1,0:T(8,128)(2,1)S(1)}, bf16[96,8192]{1,0:T(8,128)(2,1)S(1)}, u32[]{:S(2)}, u32[]{:S(2)}) collective-permute-start(bf16[96,8192]{1,0:T(8,128)(2,1)S(1)} %collective-permute-done.23.refs_2_), channel_id=1, source_target_pairs={{0,1},{1,0},{2,3},{3,2},{4,5},{5,4},{6,7},{7,6},{8,9},{9,8},{10,11... | collective-permute-start | bytes 4718600 | tf_op jit(solution)/shard_map/ppermute | solution.py:186
  141.9 37.6 %collective-permute-start.28 = (bf16[96,8192]{1,0:T(8,128)(2,1)S(1)}, bf16[96,8192]{1,0:T(8,128)(2,1)S(1)}, u32[]{:S(2)}, u32[]{:S(2)}) collective-permute-start(bf16[96,8192]{1,0:T(8,128)(2,1)S(1)} %collective-permute-done.refs_3_), channel_id=1, source_target_pairs={{0,12},{1,5},{2,14},{3,7},{4,0},{5,9},{6,2},{7,11},{8,4},{9,13},{1... | collective-permute-start | bytes 4718600 | tf_op jit(solution)/shard_map/ppermute | solution.py:186
  143.1 45.4 %collective-permute-start.31 = (bf16[96,8192]{1,0:T(8,128)(2,1)S(1)}, bf16[96,8192]{1,0:T(8,128)(2,1)S(1)}, u32[]{:S(2)}, u32[]{:S(2)}) collective-permute-start(bf16[96,8192]{1,0:T(8,128)(2,1)S(1)} %collective-permute-done.22.refs_1_), channel_id=1, source_target_pairs={{0,4},{1,13},{2,6},{3,15},{4,8},{5,1},{6,10},{7,3},{8,12},{9,5},{1... | collective-permute-start | bytes 4718600 | tf_op jit(solution)/shard_map/ppermute | solution.py:186
  164.0 41.3 %collective-permute-start.2 = (bf16[96,8192]{1,0:T(8,128)(2,1)S(1)}, bf16[96,8192]{1,0:T(8,128)(2,1)S(1)}, u32[]{:S(2)}, u32[]{:S(2)}) collective-permute-start(bf16[96,8192]{1,0:T(8,128)(2,1)S(1)} %collective-permute-done.1.refs_0_.refs_8_), channel_id=1, source_target_pairs={{0,4},{1,13},{2,6},{3,15},{4,8},{5,1},{6,10},{7,3},{8,12},{9,5},{1... | collective-permute-start | bytes 4718600 | tf_op jit(solution)/shard_map/ppermute | solution.py:186
  167.5 46.7 %collective-permute-start.29 = (bf16[96,8192]{1,0:T(8,128)(2,1)S(1)}, bf16[96,8192]{1,0:T(8,128)(2,1)S(1)}, u32[]{:S(2)}, u32[]{:S(2)}) collective-permute-start(bf16[96,8192]{1,0:T(8,128)(2,1)S(1)} %collective-permute-done.1.refs_0_.refs_8_), channel_id=1, source_target_pairs={{0,1},{1,0},{2,3},{3,2},{4,5},{5,4},{6,7},{7,6},{8,9},{9,8},{10,11... | collective-permute-start | bytes 4718600 | tf_op jit(solution)/shard_map/ppermute | solution.py:186
  170.7 43.3 %collective-permute-start.9 = (bf16[768,896]{1,0:T(8,128)(2,1)S(1)}, bf16[768,896]{1,0:T(8,128)(2,1)S(1)}, u32[]{:S(2)}, u32[]{:S(2)}) collective-permute-start(bf16[768,896]{1,0:T(8,128)(2,1)S(1)} %collective-permute-done.5.refs_11_.refs_7_.refs_5_), channel_id=1, source_target_pairs={{0,16},{1,49},{2,18},{3,51},{4,20},{5,53},{6,22},{7,55},{8,24},{9,... | collective-permute-start | bytes 4128776 | tf_op jit(solution)/shard_map/ppermute | solution.py:186
  179.5 38.9 %collective-permute-start.30 = (bf16[96,8192]{1,0:T(8,128)(2,1)S(1)}, bf16[96,8192]{1,0:T(8,128)(2,1)S(1)}, u32[]{:S(2)}, u32[]{:S(2)}) collective-permute-start(bf16[96,8192]{1,0:T(8,128)(2,1)S(1)} %collective-permute-done.28.refs_1_.refs_9_), channel_id=1, source_target_pairs={{0,1},{1,0},{2,3},{3,2},{4,5},{5,4},{6,7},{7,6},{8,9},{9,8},{10,11... | collective-permute-start | bytes 4718600 | tf_op jit(solution)/shard_map/ppermute | solution.py:186
  188.5 31.9 %collective-permute-start.32 = (bf16[96,8192]{1,0:T(8,128)(2,1)S(1)}, bf16[96,8192]{1,0:T(8,128)(2,1)S(1)}, u32[]{:S(2)}, u32[]{:S(2)}) collective-permute-start(bf16[96,8192]{1,0:T(8,128)(2,1)S(1)} %collective-permute-done.31.refs_0_.refs_12_), channel_id=1, source_target_pairs={{0,1},{1,0},{2,3},{3,2},{4,5},{5,4},{6,7},{7,6},{8,9},{9,8},{10,11... | collective-permute-start | bytes 4718600 | tf_op jit(solution)/shard_map/ppermute | solution.py:186
  205.4 47.5 %collective-permute-start.3 = (bf16[96,8192]{1,0:T(8,128)(2,1)S(1)}, bf16[96,8192]{1,0:T(8,128)(2,1)S(1)}, u32[]{:S(2)}, u32[]{:S(2)}) collective-permute-start(bf16[96,8192]{1,0:T(8,128)(2,1)S(1)} %collective-permute-done.2.refs_0_), channel_id=1, source_target_pairs={{0,1},{1,0},{2,3},{3,2},{4,5},{5,4},{6,7},{7,6},{8,9},{9,8},{10,11... | collective-permute-start | bytes 4718600 | tf_op jit(solution)/shard_map/ppermute | solution.py:186
  214.1 14.2 %collective-permute-start.17 = (bf16[384,896]{1,0:T(8,128)(2,1)S(1)}, bf16[384,896]{1,0:T(8,128)(2,1)S(1)}, u32[]{:S(2)}, u32[]{:S(2)}) collective-permute-start(bf16[384,896]{1,0:T(8,128)(2,1)S(1)} %collective-permute-done.10.refs_10_.refs_12_), channel_id=1, source_target_pairs={{0,48},{1,17},{2,50},{3,19},{4,52},{5,21},{6,54},{7,23},{8,56},{9,... | collective-permute-start | bytes 2064392 | tf_op jit(solution)/shard_map/ppermute | solution.py:186
  214.2 26.4 %collective-permute-start.18 = (bf16[384,896]{1,0:T(8,128)(2,1)S(1)}, bf16[384,896]{1,0:T(8,128)(2,1)S(1)}, u32[]{:S(2)}, u32[]{:S(2)}) collective-permute-start(bf16[384,896]{1,0:T(8,128)(2,1)S(1)} %collective-permute-done.11.refs_11_.refs_13_), channel_id=1, source_target_pairs={{0,48},{1,17},{2,50},{3,19},{4,52},{5,21},{6,54},{7,23},{8,56},{9,... | collective-permute-start | bytes 2064392 | tf_op jit(solution)/shard_map/ppermute | solution.py:186
  218.4 30.0 %collective-permute-start.20 = (bf16[384,896]{1,0:T(8,128)(2,1)S(1)}, bf16[384,896]{1,0:T(8,128)(2,1)S(1)}, u32[]{:S(2)}, u32[]{:S(2)}) collective-permute-start(bf16[384,896]{1,0:T(8,128)(2,1)S(1)} %collective-permute-done.14.refs_16_.refs_14_), channel_id=1, source_target_pairs={{0,16},{1,49},{2,18},{3,51},{4,20},{5,53},{6,22},{7,55},{8,24},{9,... | collective-permute-start | bytes 2064392 | tf_op jit(solution)/shard_map/ppermute | solution.py:186
  220.4 28.0 %collective-permute-start.21 = (bf16[384,896]{1,0:T(8,128)(2,1)S(1)}, bf16[384,896]{1,0:T(8,128)(2,1)S(1)}, u32[]{:S(2)}, u32[]{:S(2)}) collective-permute-start(bf16[384,896]{1,0:T(8,128)(2,1)S(1)} %collective-permute-done.15.refs_17_.refs_15_), channel_id=1, source_target_pairs={{0,16},{1,49},{2,18},{3,51},{4,20},{5,53},{6,22},{7,55},{8,24},{9,... | collective-permute-start | bytes 2064392 | tf_op jit(solution)/shard_map/ppermute | solution.py:186
  228.3 20.1 %collective-permute-start.19 = (bf16[256,896]{1,0:T(8,128)(2,1)S(1)}, bf16[256,896]{1,0:T(8,128)(2,1)S(1)}, u32[]{:S(2)}, u32[]{:S(2)}) collective-permute-start(bf16[256,896]{1,0:T(8,128)(2,1)S(1)} %collective-permute-done.8.refs_8_.refs_10_), channel_id=1, source_target_pairs={{0,64},{1,65},{2,66},{3,67},{4,68},{5,69},{6,70},{7,71},{8,72},{9,... | collective-permute-start | bytes 1376264 | tf_op jit(solution)/shard_map/ppermute | solution.py:186
  (3 other events, 42.2 us)

commit v4 on v0

v4 whole, which is shorter than its diff:
```python
import functools
import itertools

import jax
import jax.numpy as jnp
from jax import lax
from jax.experimental import pallas as pl
from jax.experimental.pallas import tpu as pltpu
from jax.sharding import PartitionSpec as P

N = 896
KB = 1024
ROWS = 96


F = 256
HA, HB = 512, 256


def way(fn):
    at = lambda yl, z, x, yh, c: (yl * 4 + z % 4) * 16 + x % 4 * 4 + yh * 2 + c
    places = itertools.product(range(2), range(4), range(4), range(2), range(2))
    return [(at(*p), at(*fn(*p))) for p in places]


WAYS = {
    "zP": way(lambda yl, z, x, yh, c: (yl, z + 1 - 2 * c, x, yh, c)),
    "zM": way(lambda yl, z, x, yh, c: (yl, z - 1 + 2 * c, x, yh, c)),
    "xP": way(lambda yl, z, x, yh, c: (yl, z, x + 1 - 2 * c, yh, c)),
    "xM": way(lambda yl, z, x, yh, c: (yl, z, x - 1 + 2 * c, yh, c)),
    "yl": way(lambda yl, z, x, yh, c: (1 - yl, z, x, yh, c)),
    "yh": way(lambda yl, z, x, yh, c: (yl, z, x, 1 - yh, c)),
    "co": way(lambda yl, z, x, yh, c: (yl, z, x, yh, 1 - c)),
}

STEPS = [
    ("t1", "yh", "t"), ("FP", "zP", "F"), ("FM", "zM", "F"), ("tP", "xP", "t"), ("tM", "xM", "t"),
    ("SP", "zP", "S"), ("SM", "zM", "S"), ("ct", "co", "t"),
    ("FD", "zP", "FP"),
    ("S1a", "yl", "Sa"), ("S1b", "yl", "Sb"),
    ("t1P", "xP", "t1"), ("t1M", "xM", "t1"), ("ct1", "co", "t1"), ("ctP", "co", "tP"), ("ctM", "co", "tM"), ("tD", "xP", "tP"),
    ("SD", "zP", "SP"),
    ("kA",),
    ("F1", "yl", "F"), ("F1P", "yl", "FP"), ("F1M", "yl", "FM"),
    ("S1aP", "zP", "S1a"), ("S1aM", "zM", "S1a"), ("F1D", "yl", "FD"),
    ("S1bP", "zP", "S1b"), ("S1bM", "zM", "S1b"),
    ("kB",),
    ("kS",),
    ("t1Da", "xP", "t1Pa"), ("t1Db", "xP", "t1Pb"), ("ct1P", "co", "t1P"), ("ct1M", "co", "t1M"),
    ("kC",),
    ("S1aD", "zP", "S1aP"),
    ("ctD", "co", "tD"),
    ("kD",),
    ("S1bD", "zP", "S1bP"),
    ("kE",),
    ("ct1Da", "co", "t1Da"),
    ("kI",),
    ("kK",),
    ("kJ",),
    ("ct1Db", "co", "t1Db"),
    ("kF",),
    ("kG",),
]
A = ["t", "tP", "tM", "t1", "ct", "ctP", "ctM", "ct1"]
B1 = ["t1P", "t1M", "ct1P", "ct1M"]
D0 = ["tD", "ctD"]
B2 = ["t1D", "ct1D"]

W0 = [(b, 0, [(f"F{k}", F), (f"S{k}", KB - F)]) for b, k in enumerate(("", "P", "M"))]
WD = [(3, 0, [("FD", F), ("SD", KB - F)])]
S1 = [(4, F, [("S1a", HA), ("S1b", HB)])]
W1 = [(4, 0, [("F1", F)]), (5, 0, [("F1P", F), ("S1aP", HA)]), (6, F, [("S1aM", HA)])]
W2 = [(5, F + HA, [("S1bP", HB)]), (6, 0, [("F1M", F)]), (6, F + HA, [("S1bM", HB)])]
W3, W4, W5 = [(7, F, [("S1aD", HA)])], [(7, 0, [("F1D", F)])], [(7, F + HA, [("S1bD", HB)])]

ALL = A + B1 + D0 + B2
B2_AT = ROWS * len(A + B1 + D0)


def piece_of(name, block):
    return name + "ab"[block // 4] if name in B2 else name


KERNELS = {
    "kA": [(0, 768, W0)],
    "kB": [(0, 768, WD + S1)],
    "kC": [(768, 1152, W0 + WD + S1)],
    "kD": [(0, 1152, W1)],
    "kE": [(1152, 1344, W0 + WD + S1 + W1)],
    "kI": [(0, 1344, W2)],
    "kJ": [(0, 1344, W3)],
    "kF": [(0, 1344, W4)],
    "kK": [(1344, 1536, W0 + WD)],
    "kG": [(0, 1344, W5), (1344, 1536, S1 + W1 + W2 + W3 + W4 + W5)],
}
TILE = 384
VMEM, LAST_VMEM = 2, 6


def sum_of(parts):
    return functools.reduce(lambda a, b: a + b, parts)


def kernel(plan, *refs):
    row, col = lax.axis_index("row"), lax.axis_index("col")
    yl, z, x, yh, core = row // 4, row % 4, col // 4, col // 2 % 2, col % 2
    far = lambda name, c: 3 - 2 * c if "P" in name else 1 + 2 * c if "M" in name else 2 if "D" in name else 0
    block_at = [((yl ^ one) * 4 + (z + far(k, core)) % 4) * KB for one in range(2) for k in ("", "P", "M", "D")]
    n_t, n_w = len(plan["t"]), len(plan["w"])
    t_refs, w_refs, refs = refs[:n_t], refs[n_t : n_t + n_w], refs[n_t + n_w :]
    sums_ref, refs = (refs[0], refs[1:]) if plan["taken"] else (None, refs)
    out_ref, *rest = refs

    def product(r, e, piece):
        block, k, arrays = piece
        total = None
        for name, rows in arrays:
            at = block_at[block] + k
            if r >= B2_AT:
                at = at - (yl ^ (block // 4)) * (4 * KB)
            cols = pl.ds(pl.multiple_of(at, 128), rows)
            lhs = [t_refs[plan["t"].index(piece_of(n, block))][:, cols] for n in ALL[r // ROWS : e // ROWS]]
            lhs = jnp.concatenate(lhs, axis=0)
            part = jnp.dot(lhs, w_refs[plan["w"].index(name)][...], preferred_element_type=jnp.float32)
            total = part if total is None else total + part
            k += rows
        return total

    started = []
    for lo, hi, blocks in plan["groups"]:
        for r in range(lo, hi, TILE):
            e = min(hi, r + TILE)
            at = pl.ds(r, e - r)
            total = sum_of([product(r, e, block) for block in blocks])
            if blocks[0] not in W0:
                total = total + sums_ref[at]
            if not plan["last"]:
                out_ref[at] = total
                continue
            res, sem = rest
            res[at] = total.astype(jnp.bfloat16)
            for q in range(r // ROWS, e // ROWS):
                c = core ^ ("c" in ALL[q])
                place = (x + far(ALL[q], c)) % 4 * 4 + (yh ^ ("1" in ALL[q])) * 2 + c
                to = out_ref.at[pl.ds(pl.multiple_of(place * ROWS, 16), ROWS)]
                started.append(pltpu.make_async_copy(res.at[pl.ds(q * ROWS, ROWS)], to, sem.at[q]))
                started[-1].start()
    for copy in started:
        copy.wait()


def call(name, got, sums):
    groups, last = KERNELS[name], name == "kG"
    names, arrays = [], []
    for lo, hi, blocks in groups:
        for n in ALL[lo // ROWS : hi // ROWS]:
            names += [p for p in dict.fromkeys(piece_of(n, b[0]) for b in blocks) if p not in names]
    for _, _, blocks in groups:
        for block in blocks:
            arrays += [a for a, _ in block[2] if a not in arrays]
    plan = {"t": names, "w": arrays, "taken": sums is not None, "groups": groups, "last": last}
    flops = sum(2 * (hi - lo) * rows * N for lo, hi, blocks in groups for b in blocks for _, rows in b[2])
    vmem = pl.BlockSpec(memory_space=pltpu.VMEM)
    ins = [got[n] for n in names + arrays] + ([] if sums is None else [sums])
    ins = [pltpu.with_memory_space_constraint(v, pltpu.MemorySpace.VMEM) for v in ins]
    shape = (len(ALL) * ROWS, N)
    return pl.pallas_call(
        functools.partial(kernel, plan),
        out_shape=jax.ShapeDtypeStruct(shape, jnp.bfloat16) if last else pltpu.MemorySpace.VMEM(shape, jnp.float32),
        in_specs=[vmem] * len(ins),
        out_specs=pl.BlockSpec(memory_space=pltpu.HBM) if last else vmem,
        input_output_aliases={} if last or sums is None else {len(ins) - 1: 0},
        scratch_shapes=[pltpu.VMEM(shape, jnp.bfloat16), pltpu.SemaphoreType.DMA((len(ALL),))] if last else [],
        compiler_params=pltpu.CompilerParams(vmem_limit_bytes=(LAST_VMEM if last else VMEM) * 2**20),
        cost_estimate=pl.CostEstimate(flops=flops, bytes_accessed=flops // 1000, transcendentals=0),
    )(*ins)


def halves(whole, own, other):
    yl = lax.axis_index("row") // 4
    own[...] = whole[:, pl.ds(pl.multiple_of(yl * (4 * KB), 4 * KB), 4 * KB)]
    other[...] = whole[:, pl.ds(pl.multiple_of((1 - yl) * (4 * KB), 4 * KB), 4 * KB)]


def cut(whole):
    vmem = pl.BlockSpec(memory_space=pltpu.VMEM)
    return pl.pallas_call(
        halves,
        out_shape=[pltpu.MemorySpace.VMEM((ROWS, 4 * KB), jnp.bfloat16)] * 2,
        in_specs=[vmem],
        out_specs=[vmem, vmem],
        compiler_params=pltpu.CompilerParams(vmem_limit_bytes=VMEM * 2**20),
        name="kS",
    )(pltpu.with_memory_space_constraint(whole, pltpu.MemorySpace.VMEM))


def on_device(tokens, up_weight):
    got = {"t": tokens, "F": up_weight[:F], "S": up_weight[F:], "Sa": up_weight[F : F + HA], "Sb": up_weight[F + HA :]}
    sums = None
    for step in STEPS:
        if len(step) == 3:
            got[step[0]] = lax.ppermute(got[step[2]], ("row", "col"), WAYS[step[1]])
        elif step == ("kS",):
            got["t1Pa"], got["t1Pb"] = cut(got["t1P"])
        else:
            sums = call(step[0], got, sums)
    return sums


def solution(mesh):
    return jax.shard_map(
        on_device, mesh=mesh, in_specs=(P(("row", "col"), None), P("row", "col")), out_specs=P("row", "col"), check_vma=False
    )
```

time: 353 us -> 210 us (0.59)
  waiting for transfers between devices: 307 us -> 125 us
  starting transfers between devices: 0.04 us -> 51.6 us
  matrix products: 32.5 us -> 0 us
  Pallas kernels: 0 us -> 30.8 us
  between operations: 13.4 us -> 0.4 us
    all_gather x2 -> x0, waiting for transfers between devices: 305 us -> none  [the longest x1 155 us: on_device(): w_column = lax.all_gather(up_weight, 'row', axis=0, tiled=True)]
    ppermute x0 -> x35, waiting for transfers between devices: none -> 125 us  [on_device(): got[step[0]] = lax.ppermute(got[step[2]], ('row', 'col'), WAYS[step[1]])]
    ppermute x0 -> x35, starting transfers between devices: none -> 51.6 us  [on_device(): got[step[0]] = lax.ppermute(got[step[2]], ('row', 'col'), WAYS[step[1]])]
    dot_general x1 -> x0, matrix products: 32.5 us -> none  [on_device(): jnp.dot(lax.all_gather(tokens, 'col', axis=0, tiled=True), w_column, pref...]
    pallas_call x0 -> x11, Pallas kernels: none -> 30.8 us  [the longest x10 30.7 us: call(): pl.pallas_call(functools.partial(kernel, plan), out_shape=jax.ShapeDtypeS...]
  transfers between devices with their start and end apart: 2 -> 35, of which waited for: 2 -> 13; matrix products, arithmetic and copies ran while one was open for 0% -> 0% of each run, Pallas kernels for 0% -> 13%
where the time goes in v4:
time: 210 us
  waiting for transfers between devices  125 us (60%)
  starting transfers between devices  51.6 us (25%)
  Pallas kernels  30.8 us (15%)
    ppermute x35, waiting for transfers between devices, on_device(): got[step[0]] = lax.ppermute(got[step[2]], ('row', 'col'), WAYS[step[1]])  125 us
    ppermute x35, starting transfers between devices, on_device(): got[step[0]] = lax.ppermute(got[step[2]], ('row', 'col'), WAYS[step[1]])  51.6 us
    pallas_call x10, Pallas kernels, call(): pl.pallas_call(functools.partial(kernel, plan), out_shape=jax.ShapeDtypeS...  30.7 us
  transfers between devices with their start and end apart: 35, of which 13 were waited for; matrix products, arithmetic and copies ran while one was open for 0% of the time, Pallas kernels for 13%

profile of v4, /device:TPU:1, one launch (start us, length us, event | category | flops | bytes accessed | tf_op | source)
XLA Modules:
  0.0 209.5 jit_solution(1318093140745724574)
XLA Ops:
  1.4 4.6 %collective-permute-start.20 = (bf16[256,896]{1,0:T(8,128)(2,1)S(1)}, bf16[256,896]{1,0:T(8,128)(2,1)S(1)}, u32[]{:S(2)}, u32[]{:S(2)}) collective-permute-start(bf16[256,896]{1,0:T(8,128)(2,1)S(1)} %get-tuple-element.9.refs_8_.refs_4_.refs_2_), channel_id=1, source_target_pairs={{0,16},{1,49},{2,18},{3,51},{4,20},{5,53},{6,22},{7,55},{8,24},{9,... | collective-permute-start | bytes 1376264 | tf_op jit(solution)/shard_map/ppermute | solution.py:202
  9.1 6.1 %collective-permute-done.20.refs_10_.refs_6_.refs_4_ = bf16[256,896]{1,0:T(8,128)(2,1)S(1)} collective-permute-done((bf16[256,896]{1,0:T(8,128)(2,1)S(1)}, bf16[256,896]{1,0:T(8,128)(2,1)S(1)}, u32[]{:S(2)}, u32[]{:S(2)}) %collective-permute-start.20) | collective-permute-done | bytes 458784 | tf_op jit(solution)/shard_map/ppermute | solution.py:202
  15.1 3.4 %collective-permute-start.32 = (bf16[768,896]{1,0:T(8,128)(2,1)S(1)}, bf16[768,896]{1,0:T(8,128)(2,1)S(1)}, u32[]{:S(2)}, u32[]{:S(2)}) collective-permute-start(bf16[768,896]{1,0:T(8,128)(2,1)S(1)} %slice.15.refs_9_.refs_5_.refs_3_), channel_id=1, source_target_pairs={{0,16},{1,49},{2,18},{3,51},{4,20},{5,53},{6,22},{7,55},{8,24},{9,... | collective-permute-start | bytes 4128776 | tf_op jit(solution)/shard_map/ppermute | solution.py:202
  18.6 18.3 %collective-permute-done.15.refs_11_.refs_13_.refs_18_ = bf16[256,896]{1,0:T(8,128)(2,1)S(1)} collective-permute-done((bf16[256,896]{1,0:T(8,128)(2,1)S(1)}, bf16[256,896]{1,0:T(8,128)(2,1)S(1)}, u32[]{:S(2)}, u32[]{:S(2)}) %collective-permute-start.15) | collective-permute-done | bytes 458784 | tf_op jit(solution)/shard_map/ppermute | solution.py:202
  38.2 8.5 %collective-permute-done.19.refs_12_.refs_19_ = bf16[256,896]{1,0:T(8,128)(2,1)S(1)} collective-permute-done((bf16[256,896]{1,0:T(8,128)(2,1)S(1)}, bf16[256,896]{1,0:T(8,128)(2,1)S(1)}, u32[]{:S(2)}, u32[]{:S(2)}) %collective-permute-start.19) | collective-permute-done | bytes 458784 | tf_op jit(solution)/shard_map/ppermute | solution.py:202
  48.0 2.6 %collective-permute-start.2 = (bf16[96,8192]{1,0:T(8,128)(2,1)S(1)}, bf16[96,8192]{1,0:T(8,128)(2,1)S(1)}, u32[]{:S(2)}, u32[]{:S(2)}) collective-permute-start(bf16[96,8192]{1,0:T(8,128)(2,1)S(1)} %copy-done), channel_id=1, source_target_pairs={{0,2},{1,3},{2,0},{3,1},{4,6},{5,7},{6,4},{7,5},{8,10},{9,11},{10,... | collective-permute-start | bytes 4718600 | tf_op jit(solution)/shard_map/ppermute | solution.py:202
  50.7 2.5 %collective-permute-start = (bf16[96,8192]{1,0:T(8,128)(2,1)S(1)}, bf16[96,8192]{1,0:T(8,128)(2,1)S(1)}, u32[]{:S(2)}, u32[]{:S(2)}) collective-permute-start(bf16[96,8192]{1,0:T(8,128)(2,1)S(1)} %copy-done), channel_id=1, source_target_pairs={{0,4},{1,13},{2,6},{3,15},{4,8},{5,1},{6,10},{7,3},{8,12},{9,5},{1... | collective-permute-start | bytes 4718600 | tf_op jit(solution)/shard_map/ppermute | solution.py:202
  53.1 3.4 %collective-permute-done.21.refs_13_.refs_20_ = bf16[256,896]{1,0:T(8,128)(2,1)S(1)} collective-permute-done((bf16[256,896]{1,0:T(8,128)(2,1)S(1)}, bf16[256,896]{1,0:T(8,128)(2,1)S(1)}, u32[]{:S(2)}, u32[]{:S(2)}) %collective-permute-start.21) | collective-permute-done | bytes 458784 | tf_op jit(solution)/shard_map/ppermute | solution.py:202
  56.6 9.8 %collective-permute-done.25.refs_15_.refs_24_ = bf16[256,896]{1,0:T(8,128)(2,1)S(1)} collective-permute-done((bf16[256,896]{1,0:T(8,128)(2,1)S(1)}, bf16[256,896]{1,0:T(8,128)(2,1)S(1)}, u32[]{:S(2)}, u32[]{:S(2)}) %collective-permute-start.25) | collective-permute-done | bytes 458784 | tf_op jit(solution)/shard_map/ppermute | solution.py:202
  66.4 3.7 %collective-permute-start.16 = (bf16[256,896]{1,0:T(8,128)(2,1)S(1)}, bf16[256,896]{1,0:T(8,128)(2,1)S(1)}, u32[]{:S(2)}, u32[]{:S(2)}) collective-permute-start(bf16[256,896]{1,0:T(8,128)(2,1)S(1)} %collective-permute-done.15.refs_11_.refs_13_.refs_18_), channel_id=1, source_target_pairs={{0,16},{1,49},{2,18},{3,51},{4,20},{5,53},{6,22},{7,55},{8,24},{9,... | collective-permute-start | bytes 1376264 | tf_op jit(solution)/shard_map/ppermute | solution.py:202
  70.1 10.3 %collective-permute-done.16.refs_14_.refs_23_ = bf16[256,896]{1,0:T(8,128)(2,1)S(1)} collective-permute-done((bf16[256,896]{1,0:T(8,128)(2,1)S(1)}, bf16[256,896]{1,0:T(8,128)(2,1)S(1)}, u32[]{:S(2)}, u32[]{:S(2)}) %collective-permute-start.16) | collective-permute-done | bytes 458784 | tf_op jit(solution)/shard_map/ppermute | solution.py:202
  81.6 2.7 %collective-permute-start.3 = (bf16[96,8192]{1,0:T(8,128)(2,1)S(1)}, bf16[96,8192]{1,0:T(8,128)(2,1)S(1)}, u32[]{:S(2)}, u32[]{:S(2)}) collective-permute-start(bf16[96,8192]{1,0:T(8,128)(2,1)S(1)} %copy-done), channel_id=1, source_target_pairs={{0,1},{1,0},{2,3},{3,2},{4,5},{5,4},{6,7},{7,6},{8,9},{9,8},{10,11... | collective-permute-start | bytes 4718600 | tf_op jit(solution)/shard_map/ppermute | solution.py:202
  85.8 16.8 %collective-permute-done.2.refs_3_ = bf16[96,8192]{1,0:T(8,128)(2,1)S(1)} collective-permute-done((bf16[96,8192]{1,0:T(8,128)(2,1)S(1)}, bf16[96,8192]{1,0:T(8,128)(2,1)S(1)}, u32[]{:S(2)}, u32[]{:S(2)}) %collective-permute-start.2) | collective-permute-done | bytes 1572896 | tf_op jit(solution)/shard_map/ppermute | solution.py:202
  102.5 3.7 %collective-permute-start.22 = (bf16[512,896]{1,0:T(8,128)(2,1)S(1)}, bf16[512,896]{1,0:T(8,128)(2,1)S(1)}, u32[]{:S(2)}, u32[]{:S(2)}) collective-permute-start(bf16[512,896]{1,0:T(8,128)(2,1)S(1)} %collective-permute-done.18.refs_10_.refs_12_.refs_17_), channel_id=1, source_target_pairs={{0,16},{1,49},{2,18},{3,51},{4,20},{5,53},{6,22},{7,55},{8,24},{9,... | collective-permute-start | bytes 2752520 | tf_op jit(solution)/shard_map/ppermute | solution.py:202
  106.2 2.5 %collective-permute-start.7 = (bf16[96,8192]{1,0:T(8,128)(2,1)S(1)}, bf16[96,8192]{1,0:T(8,128)(2,1)S(1)}, u32[]{:S(2)}, u32[]{:S(2)}) collective-permute-start(bf16[96,8192]{1,0:T(8,128)(2,1)S(1)} %collective-permute-done.2.refs_3_), channel_id=1, source_target_pairs={{0,4},{1,13},{2,6},{3,15},{4,8},{5,1},{6,10},{7,3},{8,12},{9,5},{1... | collective-permute-start | bytes 4718600 | tf_op jit(solution)/shard_map/ppermute | solution.py:202
  108.8 7.8 %collective-permute-done.22.refs_14_.refs_21_ = bf16[512,896]{1,0:T(8,128)(2,1)S(1)} collective-permute-done((bf16[512,896]{1,0:T(8,128)(2,1)S(1)}, bf16[512,896]{1,0:T(8,128)(2,1)S(1)}, u32[]{:S(2)}, u32[]{:S(2)}) %collective-permute-start.22) | collective-permute-done | bytes 917536 | tf_op jit(solution)/shard_map/ppermute | solution.py:202
  116.6 2.5 %collective-permute-start.4 = (bf16[96,8192]{1,0:T(8,128)(2,1)S(1)}, bf16[96,8192]{1,0:T(8,128)(2,1)S(1)}, u32[]{:S(2)}, u32[]{:S(2)}) collective-permute-start(bf16[96,8192]{1,0:T(8,128)(2,1)S(1)} %collective-permute-done.refs_1_), channel_id=1, source_target_pairs={{0,1},{1,0},{2,3},{3,2},{4,5},{5,4},{6,7},{7,6},{8,9},{9,8},{10,11... | collective-permute-start | bytes 4718600 | tf_op jit(solution)/shard_map/ppermute | solution.py:202
  119.0 2.5 %collective-permute-start.11 = (bf16[96,8192]{1,0:T(8,128)(2,1)S(1)}, bf16[96,8192]{1,0:T(8,128)(2,1)S(1)}, u32[]{:S(2)}, u32[]{:S(2)}) collective-permute-start(bf16[96,8192]{1,0:T(8,128)(2,1)S(1)} %collective-permute-done.refs_1_), channel_id=1, source_target_pairs={{0,4},{1,13},{2,6},{3,15},{4,8},{5,1},{6,10},{7,3},{8,12},{9,5},{1... | collective-permute-start | bytes 4718600 | tf_op jit(solution)/shard_map/ppermute | solution.py:202
  121.5 20.1 %collective-permute-done.7.whole.refs_0_.refs_8_ = bf16[96,8192]{1,0:T(8,128)(2,1)S(1)} collective-permute-done((bf16[96,8192]{1,0:T(8,128)(2,1)S(1)}, bf16[96,8192]{1,0:T(8,128)(2,1)S(1)}, u32[]{:S(2)}, u32[]{:S(2)}) %collective-permute-start.7) | collective-permute-done | bytes 1572896 | tf_op jit(solution)/shard_map/ppermute | solution.py:202
  143.6 2.8 %collective-permute-done.8.refs_1_.refs_9_ = bf16[96,8192]{1,0:T(8,128)(2,1)S(1)} collective-permute-done((bf16[96,8192]{1,0:T(8,128)(2,1)S(1)}, bf16[96,8192]{1,0:T(8,128)(2,1)S(1)}, u32[]{:S(2)}, u32[]{:S(2)}) %collective-permute-start.8) | collective-permute-done | bytes 1572896 | tf_op jit(solution)/shard_map/ppermute | solution.py:202
  148.4 11.5 %collective-permute-done.11.refs_0_.refs_12_ = bf16[96,8192]{1,0:T(8,128)(2,1)S(1)} collective-permute-done((bf16[96,8192]{1,0:T(8,128)(2,1)S(1)}, bf16[96,8192]{1,0:T(8,128)(2,1)S(1)}, u32[]{:S(2)}, u32[]{:S(2)}) %collective-permute-start.11) | collective-permute-done | bytes 1572896 | tf_op jit(solution)/shard_map/ppermute | solution.py:202
  159.9 2.2 %collective-permute-start.12 = (bf16[96,8192]{1,0:T(8,128)(2,1)S(1)}, bf16[96,8192]{1,0:T(8,128)(2,1)S(1)}, u32[]{:S(2)}, u32[]{:S(2)}) collective-permute-start(bf16[96,8192]{1,0:T(8,128)(2,1)S(1)} %collective-permute-done.11.refs_0_.refs_12_), channel_id=1, source_target_pairs={{0,1},{1,0},{2,3},{3,2},{4,5},{5,4},{6,7},{7,6},{8,9},{9,8},{10,11... | collective-permute-start | bytes 4718600 | tf_op jit(solution)/shard_map/ppermute | solution.py:202
  162.1 6.2 %collective-permute-done.30.refs_0_ = bf16[96,4096]{1,0:T(8,128)(2,1)S(1)} collective-permute-done((bf16[96,4096]{1,0:T(8,128)(2,1)S(1)}, bf16[96,4096]{1,0:T(8,128)(2,1)S(1)}, u32[]{:S(2)}, u32[]{:S(2)}) %collective-permute-start.30) | collective-permute-done | bytes 786464 | tf_op jit(solution)/shard_map/ppermute | solution.py:202
  168.3 3.1 %collective-permute-start.13 = (bf16[96,4096]{1,0:T(8,128)(2,1)S(1)}, bf16[96,4096]{1,0:T(8,128)(2,1)S(1)}, u32[]{:S(2)}, u32[]{:S(2)}) collective-permute-start(bf16[96,4096]{1,0:T(8,128)(2,1)S(1)} %get-tuple-element.7), channel_id=1, source_target_pairs={{0,4},{1,13},{2,6},{3,15},{4,8},{5,1},{6,10},{7,3},{8,12},{9,5},{1... | collective-permute-start | bytes 2359304 | tf_op jit(solution)/shard_map/ppermute | solution.py:202
  171.4 5.0 %shard_map.28.refs_12_ = f32[1536,896]{1,0:T(8,128)S(1)} custom-call(bf16[96,8192]{1,0:T(8,128)(2,1)S(1)} %copy-done, bf16[96,8192]{1,0:T(8,128)(2,1)S(1)} %collective-permute-done.refs_1_, bf16[96,8192]{1,0:T(8,128)(2,1)S(1)} %collective-permute-done.1.refs_2_, bf16[96,8192]{1,0:T(8,128)(2,1)S(1)} %collective-permute-done.2.refs_3_, ...), custom_call_target="tpu_custom_call" | custom-call | flops 4227858432 | bytes 4227858 | tf_op jit(solution)/shard_map/pallas_call | solution.py:167
  176.4 3.3 %shard_map.29.refs_14_ = f32[1536,896]{1,0:T(8,128)S(1)} custom-call(bf16[96,8192]{1,0:T(8,128)(2,1)S(1)} %copy-done, bf16[96,8192]{1,0:T(8,128)(2,1)S(1)} %collective-permute-done.refs_1_, bf16[96,8192]{1,0:T(8,128)(2,1)S(1)} %collective-permute-done.1.refs_2_, ...), custom_call_target="tpu_custom_call", output_to_operand_aliasing={{}: (12, {})} | custom-call | flops 2466250752 | bytes 2466250 | tf_op jit(solution)/shard_map/pallas_call | solution.py:167
  181.2 4.0 %shard_map.30.refs_16_ = f32[1536,896]{1,0:T(8,128)S(1)} custom-call(bf16[96,8192]{1,0:T(8,128)(2,1)S(1)} %collective-permute-done.7.whole.refs_0_.refs_8_, bf16[96,8192]{1,0:T(8,128)(2,1)S(1)} %collective-permute-done.8.refs_1_.refs_9_, bf16[96,8192]{1,0:T(8,128)(2,1)S(1)} %collective-permute-done.9.refs_2_.refs_10_, ...), custom_call_target="tpu_custom_call", output_to_operand_aliasing={{}: (14, {})} | custom-call | flops 3347054592 | bytes 3347054 | tf_op jit(solution)/shard_map/pallas_call | solution.py:167
  187.3 4.4 %shard_map.31.refs_16_ = f32[1536,896]{1,0:T(8,128)S(1)} custom-call(bf16[96,8192]{1,0:T(8,128)(2,1)S(1)} %copy-done, bf16[96,8192]{1,0:T(8,128)(2,1)S(1)} %collective-permute-done.refs_1_, bf16[96,8192]{1,0:T(8,128)(2,1)S(1)} %collective-permute-done.1.refs_2_, ...), custom_call_target="tpu_custom_call", output_to_operand_aliasing={{}: (16, {})} | custom-call | flops 3170893824 | bytes 3170893 | tf_op jit(solution)/shard_map/pallas_call | solution.py:167
  191.8 2.8 %shard_map.32.refs_17_ = f32[1536,896]{1,0:T(8,128)S(1)} custom-call(bf16[96,8192]{1,0:T(8,128)(2,1)S(1)} %collective-permute-done.11.refs_0_.refs_12_, bf16[96,8192]{1,0:T(8,128)(2,1)S(1)} %collective-permute-done.12.refs_1_.refs_13_, bf16[256,896]{1,0:T(8,128)(2,1)S(1)} %get-tuple-element.9.refs_8_.refs_4_.refs_2_, ...), custom_call_target="tpu_custom_call", output_to_operand_aliasing={{}: (16, {})} | custom-call | flops 2202009600 | bytes 2202009 | tf_op jit(solution)/shard_map/pallas_call | solution.py:167
  194.5 3.5 %collective-permute-done.26.refs_16_.refs_25_ = bf16[256,896]{1,0:T(8,128)(2,1)S(1)} collective-permute-done((bf16[256,896]{1,0:T(8,128)(2,1)S(1)}, bf16[256,896]{1,0:T(8,128)(2,1)S(1)}, u32[]{:S(2)}, u32[]{:S(2)}) %collective-permute-start.26) | collective-permute-done | bytes 458784 | tf_op jit(solution)/shard_map/ppermute | solution.py:202
  198.1 2.9 %shard_map.33.refs_10_ = f32[1536,896]{1,0:T(8,128)S(1)} custom-call(bf16[96,8192]{1,0:T(8,128)(2,1)S(1)} %copy-done, bf16[96,8192]{1,0:T(8,128)(2,1)S(1)} %collective-permute-done.refs_1_, bf16[96,8192]{1,0:T(8,128)(2,1)S(1)} %collective-permute-done.1.refs_2_, ...), custom_call_target="tpu_custom_call", output_to_operand_aliasing={{}: (17, {})} | custom-call | flops 1849688064 | bytes 1849688 | tf_op jit(solution)/shard_map/pallas_call | solution.py:167
  205.9 3.5 %shard_map.37 = bf16[1536,896]{1,0:T(8,128)(2,1)} custom-call(bf16[96,8192]{1,0:T(8,128)(2,1)S(1)} %copy-done, bf16[96,8192]{1,0:T(8,128)(2,1)S(1)} %collective-permute-done.refs_1_, bf16[96,8192]{1,0:T(8,128)(2,1)S(1)} %collective-permute-done.1.refs_2_, bf16[96,8192]{1,0:T(8,128)(2,1)S(1)} %collective-permute-done.2.refs_3_, ...), custom_call_target="tpu_custom_call" | custom-call | flops 2025848832 | bytes 2025848 | tf_op jit(solution)/shard_map/pallas_call | solution.py:167
  (56 shorter events, 22.1 us)
Async XLA Ops:
  1.4 13.8 %collective-permute-start.20 = (bf16[256,896]{1,0:T(8,128)(2,1)S(1)}, bf16[256,896]{1,0:T(8,128)(2,1)S(1)}, u32[]{:S(2)}, u32[]{:S(2)}) collective-permute-start(bf16[256,896]{1,0:T(8,128)(2,1)S(1)} %get-tuple-element.9.refs_8_.refs_4_.refs_2_), channel_id=1, source_target_pairs={{0,16},{1,49},{2,18},{3,51},{4,20},{5,53},{6,22},{7,55},{8,24},{9,... | collective-permute-start | bytes 1376264 | tf_op jit(solution)/shard_map/ppermute | solution.py:202
  6.1 44.5 %collective-permute-start.18 = (bf16[512,896]{1,0:T(8,128)(2,1)S(1)}, bf16[512,896]{1,0:T(8,128)(2,1)S(1)}, u32[]{:S(2)}, u32[]{:S(2)}) collective-permute-start(bf16[512,896]{1,0:T(8,128)(2,1)S(1)} %slice.13), channel_id=1, source_target_pairs={{0,64},{1,65},{2,66},{3,67},{4,68},{5,69},{6,70},{7,71},{8,72},{9,... | collective-permute-start | bytes 2752520 | tf_op jit(solution)/shard_map/ppermute | solution.py:202
  7.5 29.4 %collective-permute-start.15 = (bf16[256,896]{1,0:T(8,128)(2,1)S(1)}, bf16[256,896]{1,0:T(8,128)(2,1)S(1)}, u32[]{:S(2)}, u32[]{:S(2)}) collective-permute-start(bf16[256,896]{1,0:T(8,128)(2,1)S(1)} %get-tuple-element.10), channel_id=1, source_target_pairs={{0,64},{1,65},{2,66},{3,67},{4,68},{5,69},{6,70},{7,71},{8,72},{9,... | collective-permute-start | bytes 1376264 | tf_op jit(solution)/shard_map/ppermute | solution.py:202
  7.7 39.1 %collective-permute-start.19 = (bf16[256,896]{1,0:T(8,128)(2,1)S(1)}, bf16[256,896]{1,0:T(8,128)(2,1)S(1)}, u32[]{:S(2)}, u32[]{:S(2)}) collective-permute-start(bf16[256,896]{1,0:T(8,128)(2,1)S(1)} %get-tuple-element.9.refs_8_.refs_4_.refs_2_), channel_id=1, source_target_pairs={{0,64},{1,65},{2,66},{3,67},{4,68},{5,69},{6,70},{7,71},{8,72},{9,... | collective-permute-start | bytes 1376264 | tf_op jit(solution)/shard_map/ppermute | solution.py:202
  15.1 66.5 %collective-permute-start.32 = (bf16[768,896]{1,0:T(8,128)(2,1)S(1)}, bf16[768,896]{1,0:T(8,128)(2,1)S(1)}, u32[]{:S(2)}, u32[]{:S(2)}) collective-permute-start(bf16[768,896]{1,0:T(8,128)(2,1)S(1)} %slice.15.refs_9_.refs_5_.refs_3_), channel_id=1, source_target_pairs={{0,16},{1,49},{2,18},{3,51},{4,20},{5,53},{6,22},{7,55},{8,24},{9,... | collective-permute-start | bytes 4128776 | tf_op jit(solution)/shard_map/ppermute | solution.py:202
  18.6 29.5 %collective-permute-start.28 = (bf16[256,896]{1,0:T(8,128)(2,1)S(1)}, bf16[256,896]{1,0:T(8,128)(2,1)S(1)}, u32[]{:S(2)}, u32[]{:S(2)}) collective-permute-start(bf16[256,896]{1,0:T(8,128)(2,1)S(1)} %collective-permute-done.20.refs_10_.refs_6_.refs_4_), channel_id=1, source_target_pairs={{0,16},{1,49},{2,18},{3,51},{4,20},{5,53},{6,22},{7,55},{8,24},{9,... | collective-permute-start | bytes 1376264 | tf_op jit(solution)/shard_map/ppermute | solution.py:202
  36.9 19.7 %collective-permute-start.21 = (bf16[256,896]{1,0:T(8,128)(2,1)S(1)}, bf16[256,896]{1,0:T(8,128)(2,1)S(1)}, u32[]{:S(2)}, u32[]{:S(2)}) collective-permute-start(bf16[256,896]{1,0:T(8,128)(2,1)S(1)} %collective-permute-done.20.refs_10_.refs_6_.refs_4_), channel_id=1, source_target_pairs={{0,64},{1,65},{2,66},{3,67},{4,68},{5,69},{6,70},{7,71},{8,72},{9,... | collective-permute-start | bytes 1376264 | tf_op jit(solution)/shard_map/ppermute | solution.py:202
  46.7 19.7 %collective-permute-start.25 = (bf16[256,896]{1,0:T(8,128)(2,1)S(1)}, bf16[256,896]{1,0:T(8,128)(2,1)S(1)}, u32[]{:S(2)}, u32[]{:S(2)}) collective-permute-start(bf16[256,896]{1,0:T(8,128)(2,1)S(1)} %collective-permute-done.24.refs_12_.refs_8_.refs_6_), channel_id=1, source_target_pairs={{0,64},{1,65},{2,66},{3,67},{4,68},{5,69},{6,70},{7,71},{8,72},{9,... | collective-permute-start | bytes 1376264 | tf_op jit(solution)/shard_map/ppermute | solution.py:202
  48.0 54.5 %collective-permute-start.2 = (bf16[96,8192]{1,0:T(8,128)(2,1)S(1)}, bf16[96,8192]{1,0:T(8,128)(2,1)S(1)}, u32[]{:S(2)}, u32[]{:S(2)}) collective-permute-start(bf16[96,8192]{1,0:T(8,128)(2,1)S(1)} %copy-done), channel_id=1, source_target_pairs={{0,2},{1,3},{2,0},{3,1},{4,6},{5,7},{6,4},{7,5},{8,10},{9,11},{10,... | collective-permute-start | bytes 4718600 | tf_op jit(solution)/shard_map/ppermute | solution.py:202
  50.7 55.6 %collective-permute-start = (bf16[96,8192]{1,0:T(8,128)(2,1)S(1)}, bf16[96,8192]{1,0:T(8,128)(2,1)S(1)}, u32[]{:S(2)}, u32[]{:S(2)}) collective-permute-start(bf16[96,8192]{1,0:T(8,128)(2,1)S(1)} %copy-done), channel_id=1, source_target_pairs={{0,4},{1,13},{2,6},{3,15},{4,8},{5,1},{6,10},{7,3},{8,12},{9,5},{1... | collective-permute-start | bytes 4718600 | tf_op jit(solution)/shard_map/ppermute | solution.py:202
  56.6 27.8 %collective-permute-start.33 = (bf16[768,896]{1,0:T(8,128)(2,1)S(1)}, bf16[768,896]{1,0:T(8,128)(2,1)S(1)}, u32[]{:S(2)}, u32[]{:S(2)}) collective-permute-start(bf16[768,896]{1,0:T(8,128)(2,1)S(1)} %slice.15.refs_9_.refs_5_.refs_3_), channel_id=1, source_target_pairs={{0,48},{1,17},{2,50},{3,19},{4,52},{5,21},{6,54},{7,23},{8,56},{9,... | collective-permute-start | bytes 4128776 | tf_op jit(solution)/shard_map/ppermute | solution.py:202
  66.4 14.0 %collective-permute-start.16 = (bf16[256,896]{1,0:T(8,128)(2,1)S(1)}, bf16[256,896]{1,0:T(8,128)(2,1)S(1)}, u32[]{:S(2)}, u32[]{:S(2)}) collective-permute-start(bf16[256,896]{1,0:T(8,128)(2,1)S(1)} %collective-permute-done.15.refs_11_.refs_13_.refs_18_), channel_id=1, source_target_pairs={{0,16},{1,49},{2,18},{3,51},{4,20},{5,53},{6,22},{7,55},{8,24},{9,... | collective-permute-start | bytes 1376264 | tf_op jit(solution)/shard_map/ppermute | solution.py:202
  80.4 25.8 %collective-permute-start.1 = (bf16[96,8192]{1,0:T(8,128)(2,1)S(1)}, bf16[96,8192]{1,0:T(8,128)(2,1)S(1)}, u32[]{:S(2)}, u32[]{:S(2)}) collective-permute-start(bf16[96,8192]{1,0:T(8,128)(2,1)S(1)} %copy-done), channel_id=1, source_target_pairs={{0,12},{1,5},{2,14},{3,7},{4,0},{5,9},{6,2},{7,11},{8,4},{9,13},{1... | collective-permute-start | bytes 4718600 | tf_op jit(solution)/shard_map/ppermute | solution.py:202
  81.6 27.2 %collective-permute-start.3 = (bf16[96,8192]{1,0:T(8,128)(2,1)S(1)}, bf16[96,8192]{1,0:T(8,128)(2,1)S(1)}, u32[]{:S(2)}, u32[]{:S(2)}) collective-permute-start(bf16[96,8192]{1,0:T(8,128)(2,1)S(1)} %copy-done), channel_id=1, source_target_pairs={{0,1},{1,0},{2,3},{3,2},{4,5},{5,4},{6,7},{7,6},{8,9},{9,8},{10,11... | collective-permute-start | bytes 4718600 | tf_op jit(solution)/shard_map/ppermute | solution.py:202
  84.3 34.7 %collective-permute-start.34 = (bf16[768,896]{1,0:T(8,128)(2,1)S(1)}, bf16[768,896]{1,0:T(8,128)(2,1)S(1)}, u32[]{:S(2)}, u32[]{:S(2)}) collective-permute-start(bf16[768,896]{1,0:T(8,128)(2,1)S(1)} %collective-permute-done.32.refs_11_.refs_7_.refs_5_), channel_id=1, source_target_pairs={{0,16},{1,49},{2,18},{3,51},{4,20},{5,53},{6,22},{7,55},{8,24},{9,... | collective-permute-start | bytes 4128776 | tf_op jit(solution)/shard_map/ppermute | solution.py:202
  102.5 14.0 %collective-permute-start.22 = (bf16[512,896]{1,0:T(8,128)(2,1)S(1)}, bf16[512,896]{1,0:T(8,128)(2,1)S(1)}, u32[]{:S(2)}, u32[]{:S(2)}) collective-permute-start(bf16[512,896]{1,0:T(8,128)(2,1)S(1)} %collective-permute-done.18.refs_10_.refs_12_.refs_17_), channel_id=1, source_target_pairs={{0,16},{1,49},{2,18},{3,51},{4,20},{5,53},{6,22},{7,55},{8,24},{9,... | collective-permute-start | bytes 2752520 | tf_op jit(solution)/shard_map/ppermute | solution.py:202
  106.2 15.3 %collective-permute-start.6 = (bf16[96,8192]{1,0:T(8,128)(2,1)S(1)}, bf16[96,8192]{1,0:T(8,128)(2,1)S(1)}, u32[]{:S(2)}, u32[]{:S(2)}) collective-permute-start(bf16[96,8192]{1,0:T(8,128)(2,1)S(1)} %collective-permute-done.2.refs_3_), channel_id=1, source_target_pairs={{0,1},{1,0},{2,3},{3,2},{4,5},{5,4},{6,7},{7,6},{8,9},{9,8},{10,11... | collective-permute-start | bytes 4718600 | tf_op jit(solution)/shard_map/ppermute | solution.py:202
  106.2 35.4 %collective-permute-start.7 = (bf16[96,8192]{1,0:T(8,128)(2,1)S(1)}, bf16[96,8192]{1,0:T(8,128)(2,1)S(1)}, u32[]{:S(2)}, u32[]{:S(2)}) collective-permute-start(bf16[96,8192]{1,0:T(8,128)(2,1)S(1)} %collective-permute-done.2.refs_3_), channel_id=1, source_target_pairs={{0,4},{1,13},{2,6},{3,15},{4,8},{5,1},{6,10},{7,3},{8,12},{9,5},{1... | collective-permute-start | bytes 4718600 | tf_op jit(solution)/shard_map/ppermute | solution.py:202
  108.8 37.6 %collective-permute-start.8 = (bf16[96,8192]{1,0:T(8,128)(2,1)S(1)}, bf16[96,8192]{1,0:T(8,128)(2,1)S(1)}, u32[]{:S(2)}, u32[]{:S(2)}) collective-permute-start(bf16[96,8192]{1,0:T(8,128)(2,1)S(1)} %collective-permute-done.2.refs_3_), channel_id=1, source_target_pairs={{0,12},{1,5},{2,14},{3,7},{4,0},{5,9},{6,2},{7,11},{8,4},{9,13},{1... | collective-permute-start | bytes 4718600 | tf_op jit(solution)/shard_map/ppermute | solution.py:202
  116.6 30.0 %collective-permute-start.4 = (bf16[96,8192]{1,0:T(8,128)(2,1)S(1)}, bf16[96,8192]{1,0:T(8,128)(2,1)S(1)}, u32[]{:S(2)}, u32[]{:S(2)}) collective-permute-start(bf16[96,8192]{1,0:T(8,128)(2,1)S(1)} %collective-permute-done.refs_1_), channel_id=1, source_target_pairs={{0,1},{1,0},{2,3},{3,2},{4,5},{5,4},{6,7},{7,6},{8,9},{9,8},{10,11... | collective-permute-start | bytes 4718600 | tf_op jit(solution)/shard_map/ppermute | solution.py:202
  119.0 40.8 %collective-permute-start.11 = (bf16[96,8192]{1,0:T(8,128)(2,1)S(1)}, bf16[96,8192]{1,0:T(8,128)(2,1)S(1)}, u32[]{:S(2)}, u32[]{:S(2)}) collective-permute-start(bf16[96,8192]{1,0:T(8,128)(2,1)S(1)} %collective-permute-done.refs_1_), channel_id=1, source_target_pairs={{0,4},{1,13},{2,6},{3,15},{4,8},{5,1},{6,10},{7,3},{8,12},{9,5},{1... | collective-permute-start | bytes 4718600 | tf_op jit(solution)/shard_map/ppermute | solution.py:202
  121.5 40.6 %collective-permute-start.5 = (bf16[96,8192]{1,0:T(8,128)(2,1)S(1)}, bf16[96,8192]{1,0:T(8,128)(2,1)S(1)}, u32[]{:S(2)}, u32[]{:S(2)}) collective-permute-start(bf16[96,8192]{1,0:T(8,128)(2,1)S(1)} %collective-permute-done.1.refs_2_), channel_id=1, source_target_pairs={{0,1},{1,0},{2,3},{3,2},{4,5},{5,4},{6,7},{7,6},{8,9},{9,8},{10,11... | collective-permute-start | bytes 4718600 | tf_op jit(solution)/shard_map/ppermute | solution.py:202
  141.6 38.1 %collective-permute-start.9 = (bf16[96,8192]{1,0:T(8,128)(2,1)S(1)}, bf16[96,8192]{1,0:T(8,128)(2,1)S(1)}, u32[]{:S(2)}, u32[]{:S(2)}) collective-permute-start(bf16[96,8192]{1,0:T(8,128)(2,1)S(1)} %collective-permute-done.7.whole.refs_0_.refs_8_), channel_id=1, source_target_pairs={{0,1},{1,0},{2,3},{3,2},{4,5},{5,4},{6,7},{7,6},{8,9},{9,8},{10,11... | collective-permute-start | bytes 4718600 | tf_op jit(solution)/shard_map/ppermute | solution.py:202
  146.4 34.8 %collective-permute-start.10 = (bf16[96,8192]{1,0:T(8,128)(2,1)S(1)}, bf16[96,8192]{1,0:T(8,128)(2,1)S(1)}, u32[]{:S(2)}, u32[]{:S(2)}) collective-permute-start(bf16[96,8192]{1,0:T(8,128)(2,1)S(1)} %collective-permute-done.8.refs_1_.refs_9_), channel_id=1, source_target_pairs={{0,1},{1,0},{2,3},{3,2},{4,5},{5,4},{6,7},{7,6},{8,9},{9,8},{10,11... | collective-permute-start | bytes 4718600 | tf_op jit(solution)/shard_map/ppermute | solution.py:202
  146.5 21.7 %collective-permute-start.30 = (bf16[96,4096]{1,0:T(8,128)(2,1)S(1)}, bf16[96,4096]{1,0:T(8,128)(2,1)S(1)}, u32[]{:S(2)}, u32[]{:S(2)}) collective-permute-start(bf16[96,4096]{1,0:T(8,128)(2,1)S(1)} %get-tuple-element.8), channel_id=1, source_target_pairs={{0,4},{1,13},{2,6},{3,15},{4,8},{5,1},{6,10},{7,3},{8,12},{9,5},{1... | collective-permute-start | bytes 2359304 | tf_op jit(solution)/shard_map/ppermute | solution.py:202
  159.9 31.8 %collective-permute-start.12 = (bf16[96,8192]{1,0:T(8,128)(2,1)S(1)}, bf16[96,8192]{1,0:T(8,128)(2,1)S(1)}, u32[]{:S(2)}, u32[]{:S(2)}) collective-permute-start(bf16[96,8192]{1,0:T(8,128)(2,1)S(1)} %collective-permute-done.11.refs_0_.refs_12_), channel_id=1, source_target_pairs={{0,1},{1,0},{2,3},{3,2},{4,5},{5,4},{6,7},{7,6},{8,9},{9,8},{10,11... | collective-permute-start | bytes 4718600 | tf_op jit(solution)/shard_map/ppermute | solution.py:202
  162.1 23.2 %collective-permute-start.23 = (bf16[512,896]{1,0:T(8,128)(2,1)S(1)}, bf16[512,896]{1,0:T(8,128)(2,1)S(1)}, u32[]{:S(2)}, u32[]{:S(2)}) collective-permute-start(bf16[512,896]{1,0:T(8,128)(2,1)S(1)} %collective-permute-done.18.refs_10_.refs_12_.refs_17_), channel_id=1, source_target_pairs={{0,48},{1,17},{2,50},{3,19},{4,52},{5,21},{6,54},{7,23},{8,56},{9,... | collective-permute-start | bytes 2752520 | tf_op jit(solution)/shard_map/ppermute | solution.py:202
  168.3 17.1 %collective-permute-start.13 = (bf16[96,4096]{1,0:T(8,128)(2,1)S(1)}, bf16[96,4096]{1,0:T(8,128)(2,1)S(1)}, u32[]{:S(2)}, u32[]{:S(2)}) collective-permute-start(bf16[96,4096]{1,0:T(8,128)(2,1)S(1)} %get-tuple-element.7), channel_id=1, source_target_pairs={{0,4},{1,13},{2,6},{3,15},{4,8},{5,1},{6,10},{7,3},{8,12},{9,5},{1... | collective-permute-start | bytes 2359304 | tf_op jit(solution)/shard_map/ppermute | solution.py:202
  179.8 23.1 %collective-permute-start.27 = (bf16[512,896]{1,0:T(8,128)(2,1)S(1)}, bf16[512,896]{1,0:T(8,128)(2,1)S(1)}, u32[]{:S(2)}, u32[]{:S(2)}) collective-permute-start(bf16[512,896]{1,0:T(8,128)(2,1)S(1)} %collective-permute-done.22.refs_14_.refs_21_), channel_id=1, source_target_pairs={{0,16},{1,49},{2,18},{3,51},{4,20},{5,53},{6,22},{7,55},{8,24},{9,... | collective-permute-start | bytes 2752520 | tf_op jit(solution)/shard_map/ppermute | solution.py:202
  181.2 19.8 %collective-permute-start.31 = (bf16[96,4096]{1,0:T(8,128)(2,1)S(1)}, bf16[96,4096]{1,0:T(8,128)(2,1)S(1)}, u32[]{:S(2)}, u32[]{:S(2)}) collective-permute-start(bf16[96,4096]{1,0:T(8,128)(2,1)S(1)} %collective-permute-done.30.refs_0_), channel_id=1, source_target_pairs={{0,1},{1,0},{2,3},{3,2},{4,5},{5,4},{6,7},{7,6},{8,9},{9,8},{10,11... | collective-permute-start | bytes 2359304 | tf_op jit(solution)/shard_map/ppermute | solution.py:202
  185.4 20.4 %collective-permute-start.14 = (bf16[96,4096]{1,0:T(8,128)(2,1)S(1)}, bf16[96,4096]{1,0:T(8,128)(2,1)S(1)}, u32[]{:S(2)}, u32[]{:S(2)}) collective-permute-start(bf16[96,4096]{1,0:T(8,128)(2,1)S(1)} %collective-permute-done.13.refs_14_), channel_id=1, source_target_pairs={{0,1},{1,0},{2,3},{3,2},{4,5},{5,4},{6,7},{7,6},{8,9},{9,8},{10,11... | collective-permute-start | bytes 2359304 | tf_op jit(solution)/shard_map/ppermute | solution.py:202
  191.7 13.0 %collective-permute-start.29 = (bf16[256,896]{1,0:T(8,128)(2,1)S(1)}, bf16[256,896]{1,0:T(8,128)(2,1)S(1)}, u32[]{:S(2)}, u32[]{:S(2)}) collective-permute-start(bf16[256,896]{1,0:T(8,128)(2,1)S(1)} %collective-permute-done.28.refs_8_.refs_10_), channel_id=1, source_target_pairs={{0,64},{1,65},{2,66},{3,67},{4,68},{5,69},{6,70},{7,71},{8,72},{9,... | collective-permute-start | bytes 1376264 | tf_op jit(solution)/shard_map/ppermute | solution.py:202
  (5 other events, 81.1 us)

commit v5 on v4

--- a/solution.py
+++ b/solution.py
@@ -34,31 +34,31 @@
 }
 
 STEPS = [
-    ("t1", "yh", "t"), ("FP", "zP", "F"), ("FM", "zM", "F"), ("tP", "xP", "t"), ("tM", "xM", "t"),
-    ("SP", "zP", "S"), ("SM", "zM", "S"), ("ct", "co", "t"),
-    ("FD", "zP", "FP"),
+    ("t1", "yh", "t"), ("WP", "zP", "w"), ("tP", "xP", "t"), ("WM", "zM", "w"), ("tM", "xM", "t"), ("ct", "co", "t"),
     ("S1a", "yl", "Sa"), ("S1b", "yl", "Sb"),
-    ("t1P", "xP", "t1"), ("t1M", "xM", "t1"), ("ct1", "co", "t1"), ("ctP", "co", "tP"), ("ctM", "co", "tM"), ("tD", "xP", "tP"),
-    ("SD", "zP", "SP"),
+    ("t1P", "xP", "t1"), ("t1M", "xM", "t1"), ("WD", "zP", "WP"),
+    ("ct1", "co", "t1"), ("ctP", "co", "tP"), ("ctM", "co", "tM"), ("tD", "xP", "tP"),
     ("kA",),
     ("F1", "yl", "F"), ("F1P", "yl", "FP"), ("F1M", "yl", "FM"),
-    ("S1aP", "zP", "S1a"), ("S1aM", "zM", "S1a"), ("F1D", "yl", "FD"),
+    ("S1aP", "zP", "S1a"), ("S1aM", "zM", "S1a"),
+    ("kB",),
     ("S1bP", "zP", "S1b"), ("S1bM", "zM", "S1b"),
-    ("kB",),
+    ("kC",),
     ("kS",),
-    ("t1Da", "xP", "t1Pa"), ("t1Db", "xP", "t1Pb"), ("ct1P", "co", "t1P"), ("ct1M", "co", "t1M"),
-    ("kC",),
+    ("t1Da", "xP", "t1Pa"), ("t1Db", "xP", "t1Pb"), ("ct1P", "co", "t1P"), ("ct1M", "co", "t1M"), ("F1D", "yl", "FD"),
+    ("kD",),
+    ("kF",),
+    ("kE",),
     ("S1aD", "zP", "S1aP"),
-    ("ctD", "co", "tD"),
-    ("kD",),
-    ("S1bD", "zP", "S1bP"),
-    ("kE",),
+    ("kH",),
+    ("ctD", "co", "tD"), ("S1bD", "zP", "S1bP"),
+    ("kJ",),
+    ("kI",),
     ("ct1Da", "co", "t1Da"),
-    ("kI",),
+    ("kL",),
+    ("ct1Db", "co", "t1Db"),
     ("kK",),
-    ("kJ",),
-    ("ct1Db", "co", "t1Db"),
-    ("kF",),
+    ("kM",),
     ("kG",),
 ]
 A = ["t", "tP", "tM", "t1", "ct", "ctP", "ctM", "ct1"]
@@ -66,35 +66,38 @@
 D0 = ["tD", "ctD"]
 B2 = ["t1D", "ct1D"]
 
-W0 = [(b, 0, [(f"F{k}", F), (f"S{k}", KB - F)]) for b, k in enumerate(("", "P", "M"))]
-WD = [(3, 0, [("FD", F), ("SD", KB - F)])]
-S1 = [(4, F, [("S1a", HA), ("S1b", HB)])]
-W1 = [(4, 0, [("F1", F)]), (5, 0, [("F1P", F), ("S1aP", HA)]), (6, F, [("S1aM", HA)])]
-W2 = [(5, F + HA, [("S1bP", HB)]), (6, 0, [("F1M", F)]), (6, F + HA, [("S1bM", HB)])]
-W3, W4, W5 = [(7, F, [("S1aD", HA)])], [(7, 0, [("F1D", F)])], [(7, F + HA, [("S1bD", HB)])]
+W0 = [(0, 0, [("w", 0, KB)]), (1, 0, [("WP", 0, KB)]), (2, 0, [("WM", 0, KB)])]
+WD = [(3, 0, [("WD", 0, KB)])]
+S1 = [(4, F, [("S1a", 0, HA), ("S1b", 0, HB)])]
+W1 = [(4, 0, [("F1", 0, F)]), (5, 0, [("F1P", 0, F), ("S1aP", 0, HA)]), (6, F, [("S1aM", 0, HA)])]
+W2 = [(5, F + HA, [("S1bP", 0, HB)]), (6, 0, [("F1M", 0, F)]), (6, F + HA, [("S1bM", 0, HB)])]
+W3, W4, W5 = [(7, F, [("S1aD", 0, HA)])], [(7, 0, [("F1D", 0, F)])], [(7, F + HA, [("S1bD", 0, HB)])]
 
 ALL = A + B1 + D0 + B2
 B2_AT = ROWS * len(A + B1 + D0)
 
 
 def piece_of(name, block):
-    return name + "ab"[block // 4] if name in B2 else name
+    return name if name not in B2 else name + "b" if block in (5, 6) else name + "a"
 
 
 KERNELS = {
     "kA": [(0, 768, W0)],
-    "kB": [(0, 768, WD + S1)],
-    "kC": [(768, 1152, W0 + WD + S1)],
-    "kD": [(0, 1152, W1)],
-    "kE": [(1152, 1344, W0 + WD + S1 + W1)],
-    "kI": [(0, 1344, W2)],
-    "kJ": [(0, 1344, W3)],
-    "kF": [(0, 1344, W4)],
-    "kK": [(1344, 1536, W0 + WD)],
-    "kG": [(0, 1344, W5), (1344, 1536, S1 + W1 + W2 + W3 + W4 + W5)],
+    "kB": [(0, 768, [(4, F, [("S1a", 0, HA)])])],
+    "kC": [(0, 768, WD + [(4, F + HA, [("S1b", 0, HB)])])],
+    "kD": [(768, 960, W0 + WD + S1)],
+    "kE": [(0, 768, W1[::2])],
+    "kF": [(960, 1152, W0 + WD + S1)],
+    "kH": [(0, 768, W1[1:2]), (768, 1152, W1)],
+    "kI": [(1152, 1344, W0 + WD + S1 + W1 + W2)],
+    "kJ": [(0, 1152, W2)],
+    "kL": [(0, 1344, W3)],
+    "kK": [(1344, 1536, W0 + WD + S1 + W1[:1] + W3)],
+    "kM": [(0, 1344, W4), (1344, 1536, W4)],
+    "kG": [(0, 1344, W5), (1344, 1536, W5 + W1[1:] + W2)],
 }
 TILE = 384
-VMEM, LAST_VMEM = 2, 6
+VMEM, LAST_VMEM = 4, 6
 
 
 def sum_of(parts):
@@ -106,6 +109,8 @@
     yl, z, x, yh, core = row // 4, row % 4, col // 4, col // 2 % 2, col % 2
     far = lambda name, c: 3 - 2 * c if "P" in name else 1 + 2 * c if "M" in name else 2 if "D" in name else 0
     block_at = [((yl ^ one) * 4 + (z + far(k, core)) % 4) * KB for one in range(2) for k in ("", "P", "M", "D")]
+    block_in_piece = [block_at[b] - yl * (4 * KB) for b in range(4)]
+    block_in_piece += [4 * KB, (far("P", core) - 1) // 2 * KB, (far("M", core) - 1) // 2 * KB, 5 * KB]
     n_t, n_w = len(plan["t"]), len(plan["w"])
     t_refs, w_refs, refs = refs[:n_t], refs[n_t : n_t + n_w], refs[n_t + n_w :]
     sums_ref, refs = (refs[0], refs[1:]) if plan["taken"] else (None, refs)
@@ -114,14 +119,12 @@
     def product(r, e, piece):
         block, k, arrays = piece
         total = None
-        for name, rows in arrays:
-            at = block_at[block] + k
-            if r >= B2_AT:
-                at = at - (yl ^ (block // 4)) * (4 * KB)
+        for name, first, rows in arrays:
+            at = (block_at[block] if r < B2_AT else block_in_piece[block]) + k
             cols = pl.ds(pl.multiple_of(at, 128), rows)
             lhs = [t_refs[plan["t"].index(piece_of(n, block))][:, cols] for n in ALL[r // ROWS : e // ROWS]]
             lhs = jnp.concatenate(lhs, axis=0)
-            part = jnp.dot(lhs, w_refs[plan["w"].index(name)][...], preferred_element_type=jnp.float32)
+            part = jnp.dot(lhs, w_refs[plan["w"].index(name)][first : first + rows], preferred_element_type=jnp.float32)
             total = part if total is None else total + part
             k += rows
         return total
@@ -157,9 +160,9 @@
             names += [p for p in dict.fromkeys(piece_of(n, b[0]) for b in blocks) if p not in names]
     for _, _, blocks in groups:
         for block in blocks:
-            arrays += [a for a, _ in block[2] if a not in arrays]
+            arrays += [a for a, _, _ in block[2] if a not in arrays]
     plan = {"t": names, "w": arrays, "taken": sums is not None, "groups": groups, "last": last}
-    flops = sum(2 * (hi - lo) * rows * N for lo, hi, blocks in groups for b in blocks for _, rows in b[2])
+    flops = sum(2 * (hi - lo) * rows * N for lo, hi, blocks in groups for b in blocks for _, _, rows in b[2])
     vmem = pl.BlockSpec(memory_space=pltpu.VMEM)
     ins = [got[n] for n in names + arrays] + ([] if sums is None else [sums])
     ins = [pltpu.with_memory_space_constraint(v, pltpu.MemorySpace.VMEM) for v in ins]
@@ -176,32 +179,43 @@
     )(*ins)
 
 
-def halves(whole, own, other):
-    yl = lax.axis_index("row") // 4
-    own[...] = whole[:, pl.ds(pl.multiple_of(yl * (4 * KB), 4 * KB), 4 * KB)]
-    other[...] = whole[:, pl.ds(pl.multiple_of((1 - yl) * (4 * KB), 4 * KB), 4 * KB)]
-
-
-def cut(whole):
+def two_pieces(whole, a, b):
+    row = lax.axis_index("row")
+    yl, z = row // 4, row % 4
+    columns = lambda block, n: whole[:, pl.ds(pl.multiple_of(block * KB, KB), n * KB)]
+    a[:, : 4 * KB] = columns(yl * 4, 4)
+    a[:, 4 * KB : 5 * KB] = columns((1 - yl) * 4 + z, 1)
+    a[:, 5 * KB :] = columns((1 - yl) * 4 + (z + 2) % 4, 1)
+    b[:, :KB] = columns((1 - yl) * 4 + (z + 1) % 4, 1)
+    b[:, KB:] = columns((1 - yl) * 4 + (z + 3) % 4, 1)
+
+
+def first_rows(whole, out):
+    out[...] = whole[:F]
+
+
+def cut(whole, body, shapes):
     vmem = pl.BlockSpec(memory_space=pltpu.VMEM)
     return pl.pallas_call(
-        halves,
-        out_shape=[pltpu.MemorySpace.VMEM((ROWS, 4 * KB), jnp.bfloat16)] * 2,
+        body,
+        out_shape=[pltpu.MemorySpace.VMEM(shape, jnp.bfloat16) for shape in shapes],
         in_specs=[vmem],
-        out_specs=[vmem, vmem],
+        out_specs=[vmem] * len(shapes),
         compiler_params=pltpu.CompilerParams(vmem_limit_bytes=VMEM * 2**20),
         name="kS",
     )(pltpu.with_memory_space_constraint(whole, pltpu.MemorySpace.VMEM))
 
 
 def on_device(tokens, up_weight):
-    got = {"t": tokens, "F": up_weight[:F], "S": up_weight[F:], "Sa": up_weight[F : F + HA], "Sb": up_weight[F + HA :]}
+    got = {"t": tokens, "w": up_weight, "F": up_weight[:F], "Sa": up_weight[F : F + HA], "Sb": up_weight[F + HA :]}
     sums = None
     for step in STEPS:
+        if len(step) == 3 and step[2] in ("FP", "FM", "FD"):
+            (got[step[2]],) = cut(got["W" + step[2][1]], first_rows, [(F, N)])
         if len(step) == 3:
             got[step[0]] = lax.ppermute(got[step[2]], ("row", "col"), WAYS[step[1]])
         elif step == ("kS",):
-            got["t1Pa"], got["t1Pb"] = cut(got["t1P"])
+            got["t1Pa"], got["t1Pb"] = cut(got["t1P"], two_pieces, [(ROWS, 6 * KB), (ROWS, 2 * KB)])
         else:
             sums = call(step[0], got, sums)
     return sums

time: 210 us -> 233 us (1.11)
  waiting for transfers between devices: 125 us -> 152 us
  starting transfers between devices: 51.6 us -> 47.4 us
    ppermute x35 -> x32, waiting for transfers between devices: 125 us -> 152 us  [on_device(): got[step[0]] = lax.ppermute(got[step[2]], ('row', 'col'), WAYS[step[1]])]
    ppermute x35 -> x32, starting transfers between devices: 51.6 us -> 47.4 us  [on_device(): got[step[0]] = lax.ppermute(got[step[2]], ('row', 'col'), WAYS[step[1]])]
    pallas_call x10 -> x13, Pallas kernels: 30.7 us -> 31 us  [call(): pl.pallas_call(functools.partial(kernel, plan), out_shape=jax.ShapeDtypeS...]
  transfers between devices with their start and end apart: 35 -> 32, of which waited for: 13 -> 10; matrix products, arithmetic and copies ran while one was open for 0% -> 1% of each run, Pallas kernels for 13% -> 12%
where the time goes in v5:
time: 233 us
  waiting for transfers between devices  152 us (65%)
  starting transfers between devices  47.4 us (20%)
  Pallas kernels  31.2 us (13%)
  local copies, waits for them, and re-layouts  2.49 us (1%)
    ppermute x32, waiting for transfers between devices, on_device(): got[step[0]] = lax.ppermute(got[step[2]], ('row', 'col'), WAYS[step[1]])  152 us
    ppermute x32, starting transfers between devices, on_device(): got[step[0]] = lax.ppermute(got[step[2]], ('row', 'col'), WAYS[step[1]])  47.4 us
    pallas_call x13, Pallas kernels, call(): pl.pallas_call(functools.partial(kernel, plan), out_shape=jax.ShapeDtypeS...  31 us
  transfers between devices with their start and end apart: 32, of which 10 were waited for; matrix products, arithmetic and copies ran while one was open for 1% of the time, Pallas kernels for 12%

profile of v5, /device:TPU:1, one launch (start us, length us, event | category | flops | bytes accessed | tf_op | source)
XLA Modules:
  0.0 233.3 jit_solution(11286513731827759469)
XLA Ops:
  0.0 3.7 %collective-permute-start.2 = (bf16[96,8192]{1,0:T(8,128)(2,1)}, bf16[96,8192]{1,0:T(8,128)(2,1)S(1)}, u32[]{:S(2)}, u32[]{:S(2)}) collective-permute-start(bf16[96,8192]{1,0:T(8,128)(2,1)} %refs_0_.17), channel_id=1, source_target_pairs={{0,2},{1,3},{2,0},{3,1},{4,6},{5,7},{6,4},{7,5},{8,10},{9,11},{10,... | collective-permute-start | bytes 4718600 | tf_op jit(solution)/shard_map/ppermute | solution.py:216
  8.2 59.4 %collective-permute-done.17.refs_9_.refs_7_ = bf16[256,896]{1,0:T(8,128)(2,1)S(1)} collective-permute-done((bf16[256,896]{1,0:T(8,128)(2,1)S(1)}, bf16[256,896]{1,0:T(8,128)(2,1)S(1)}, u32[]{:S(2)}, u32[]{:S(2)}) %collective-permute-start.17) | collective-permute-done | bytes 458784 | tf_op jit(solution)/shard_map/ppermute | solution.py:216
  67.7 3.8 %collective-permute-start.18 = (bf16[256,896]{1,0:T(8,128)(2,1)S(1)}, bf16[256,896]{1,0:T(8,128)(2,1)S(1)}, u32[]{:S(2)}, u32[]{:S(2)}) collective-permute-start(bf16[256,896]{1,0:T(8,128)(2,1)S(1)} %collective-permute-done.17.refs_9_.refs_7_), channel_id=1, source_target_pairs={{0,16},{1,49},{2,18},{3,51},{4,20},{5,53},{6,22},{7,55},{8,24},{9,... | collective-permute-start | bytes 1376264 | tf_op jit(solution)/shard_map/ppermute | solution.py:216
  71.4 6.1 %collective-permute-done.30.refs_8_.refs_14_ = bf16[256,896]{1,0:T(8,128)(2,1)S(1)} collective-permute-done((bf16[256,896]{1,0:T(8,128)(2,1)S(1)}, bf16[256,896]{1,0:T(8,128)(2,1)S(1)}, u32[]{:S(2)}, u32[]{:S(2)}) %collective-permute-start.30) | collective-permute-done | bytes 458784 | tf_op jit(solution)/shard_map/ppermute | solution.py:216
  77.5 3.8 %collective-permute-start.20 = (bf16[1024,896]{1,0:T(8,128)(2,1)S(1)}, bf16[1024,896]{1,0:T(8,128)(2,1)S(1)}, u32[]{:S(2)}, u32[]{:S(2)}) collective-permute-start(bf16[1024,896]{1,0:T(8,128)(2,1)S(1)} %copy-done.1), channel_id=1, source_target_pairs={{0,16},{1,49},{2,18},{3,51},{4,20},{5,53},{6,22},{7,55},{8,24},{9,... | collective-permute-start | bytes 5505032 | tf_op jit(solution)/shard_map/ppermute | solution.py:216
  81.2 2.5 %collective-permute-start = (bf16[96,8192]{1,0:T(8,128)(2,1)S(1)}, bf16[96,8192]{1,0:T(8,128)(2,1)S(1)}, u32[]{:S(2)}, u32[]{:S(2)}) collective-permute-start(bf16[96,8192]{1,0:T(8,128)(2,1)S(1)} %copy-done), channel_id=1, source_target_pairs={{0,4},{1,13},{2,6},{3,15},{4,8},{5,1},{6,10},{7,3},{8,12},{9,5},{1... | collective-permute-start | bytes 4718600 | tf_op jit(solution)/shard_map/ppermute | solution.py:216
  85.0 3.3 %collective-permute-start.3 = (bf16[96,8192]{1,0:T(8,128)(2,1)S(1)}, bf16[96,8192]{1,0:T(8,128)(2,1)S(1)}, u32[]{:S(2)}, u32[]{:S(2)}) collective-permute-start(bf16[96,8192]{1,0:T(8,128)(2,1)S(1)} %copy-done), channel_id=1, source_target_pairs={{0,1},{1,0},{2,3},{3,2},{4,5},{5,4},{6,7},{7,6},{8,9},{9,8},{10,11... | collective-permute-start | bytes 4718600 | tf_op jit(solution)/shard_map/ppermute | solution.py:216
  88.3 24.9 %collective-permute-done.refs_1_ = bf16[96,8192]{1,0:T(8,128)(2,1)S(1)} collective-permute-done((bf16[96,8192]{1,0:T(8,128)(2,1)S(1)}, bf16[96,8192]{1,0:T(8,128)(2,1)S(1)}, u32[]{:S(2)}, u32[]{:S(2)}) %collective-permute-start) | collective-permute-done | bytes 1572896 | tf_op jit(solution)/shard_map/ppermute | solution.py:216
  113.2 3.9 %collective-permute-start.6 = (bf16[96,8192]{1,0:T(8,128)(2,1)S(1)}, bf16[96,8192]{1,0:T(8,128)(2,1)S(1)}, u32[]{:S(2)}, u32[]{:S(2)}) collective-permute-start(bf16[96,8192]{1,0:T(8,128)(2,1)S(1)} %collective-permute-done.2.refs_3_), channel_id=1, source_target_pairs={{0,1},{1,0},{2,3},{3,2},{4,5},{5,4},{6,7},{7,6},{8,9},{9,8},{10,11... | collective-permute-start | bytes 4718600 | tf_op jit(solution)/shard_map/ppermute | solution.py:216
  117.1 1.6 collective-permute-done.1.refs_2_
  121.4 2.8 %collective-permute-done.25.whole.refs_10_.refs_4_ = bf16[1024,896]{1,0:T(8,128)(2,1)S(1)} collective-permute-done((bf16[1024,896]{1,0:T(8,128)(2,1)S(1)}, bf16[1024,896]{1,0:T(8,128)(2,1)S(1)}, u32[]{:S(2)}, u32[]{:S(2)}) %collective-permute-start.25) | collective-permute-done | bytes 1835040 | tf_op jit(solution)/shard_map/ppermute | solution.py:216
  124.2 2.5 %collective-permute-start.7 = (bf16[96,8192]{1,0:T(8,128)(2,1)S(1)}, bf16[96,8192]{1,0:T(8,128)(2,1)S(1)}, u32[]{:S(2)}, u32[]{:S(2)}) collective-permute-start(bf16[96,8192]{1,0:T(8,128)(2,1)S(1)} %collective-permute-done.2.refs_3_), channel_id=1, source_target_pairs={{0,4},{1,13},{2,6},{3,15},{4,8},{5,1},{6,10},{7,3},{8,12},{9,5},{1... | collective-permute-start | bytes 4718600 | tf_op jit(solution)/shard_map/ppermute | solution.py:216
  126.7 15.8 %collective-permute-done.24.refs_9_.refs_15_.refs_11_.refs_21_ = bf16[512,896]{1,0:T(8,128)(2,1)S(1)} collective-permute-done((bf16[512,896]{1,0:T(8,128)(2,1)S(1)}, bf16[512,896]{1,0:T(8,128)(2,1)S(1)}, u32[]{:S(2)}, u32[]{:S(2)}) %collective-permute-start.24) | collective-permute-done | bytes 917536 | tf_op jit(solution)/shard_map/ppermute | solution.py:216
  142.5 2.6 %collective-permute-start.8 = (bf16[96,8192]{1,0:T(8,128)(2,1)S(1)}, bf16[96,8192]{1,0:T(8,128)(2,1)S(1)}, u32[]{:S(2)}, u32[]{:S(2)}) collective-permute-start(bf16[96,8192]{1,0:T(8,128)(2,1)S(1)} %collective-permute-done.2.refs_3_), channel_id=1, source_target_pairs={{0,12},{1,5},{2,14},{3,7},{4,0},{5,9},{6,2},{7,11},{8,4},{9,13},{1... | collective-permute-start | bytes 4718600 | tf_op jit(solution)/shard_map/ppermute | solution.py:216
  145.9 1.9 collective-permute-start.11
  147.8 31.2 %collective-permute-done.8.refs_1_.refs_9_ = bf16[96,8192]{1,0:T(8,128)(2,1)S(1)} collective-permute-done((bf16[96,8192]{1,0:T(8,128)(2,1)S(1)}, bf16[96,8192]{1,0:T(8,128)(2,1)S(1)}, u32[]{:S(2)}, u32[]{:S(2)}) %collective-permute-start.8) | collective-permute-done | bytes 1572896 | tf_op jit(solution)/shard_map/ppermute | solution.py:216
  179.2 2.8 %collective-permute-start.13 = (bf16[96,6144]{1,0:T(8,128)(2,1)S(1)}, bf16[96,6144]{1,0:T(8,128)(2,1)S(1)}, u32[]{:S(2)}, u32[]{:S(2)}) collective-permute-start(bf16[96,6144]{1,0:T(8,128)(2,1)S(1)} %get-tuple-element.7), channel_id=1, source_target_pairs={{0,4},{1,13},{2,6},{3,15},{4,8},{5,1},{6,10},{7,3},{8,12},{9,5},{1... | collective-permute-start | bytes 3538952 | tf_op jit(solution)/shard_map/ppermute | solution.py:216
  183.3 5.0 %shard_map.28.refs_9_ = f32[1536,896]{1,0:T(8,128)S(1)} custom-call(bf16[96,8192]{1,0:T(8,128)(2,1)S(1)} %copy-done, bf16[96,8192]{1,0:T(8,128)(2,1)S(1)} %collective-permute-done.refs_1_, bf16[96,8192]{1,0:T(8,128)(2,1)S(1)} %collective-permute-done.1.refs_2_, bf16[96,8192]{1,0:T(8,128)(2,1)S(1)} %collective-permute-done.2.refs_3_, ...), custom_call_target="tpu_custom_call" | custom-call | flops 4227858432 | bytes 4227858 | tf_op jit(solution)/shard_map/pallas_call | solution.py:170
  189.5 5.6 %collective-permute-done.13.refs_0_.refs_14_ = bf16[96,6144]{1,0:T(8,128)(2,1)S(1)} collective-permute-done((bf16[96,6144]{1,0:T(8,128)(2,1)S(1)}, bf16[96,6144]{1,0:T(8,128)(2,1)S(1)}, u32[]{:S(2)}, u32[]{:S(2)}) %collective-permute-start.13) | collective-permute-done | bytes 1179680 | tf_op jit(solution)/shard_map/ppermute | solution.py:216
  195.1 2.1 collective-permute-start.15
  197.1 2.4 %shard_map.30.refs_8_ = f32[1536,896]{1,0:T(8,128)S(1)} custom-call(bf16[96,8192]{1,0:T(8,128)(2,1)S(1)} %copy-done, bf16[96,8192]{1,0:T(8,128)(2,1)S(1)} %collective-permute-done.refs_1_, bf16[96,8192]{1,0:T(8,128)(2,1)S(1)} %collective-permute-done.1.refs_2_, bf16[96,8192]{1,0:T(8,128)(2,1)S(1)} %collective-permute-done.2.refs_3_, ...), custom_call_target="tpu_custom_call", output_to_operand_aliasing={{}: (10, {})} | custom-call | flops 1761607680 | bytes 1761607 | tf_op jit(solution)/shard_map/pallas_call | solution.py:170
  200.7 3.0 %collective-permute-start.31 = (bf16[512,896]{1,0:T(8,128)(2,1)S(1)}, bf16[512,896]{1,0:T(8,128)(2,1)S(1)}, u32[]{:S(2)}, u32[]{:S(2)}) collective-permute-start(bf16[512,896]{1,0:T(8,128)(2,1)S(1)} %collective-permute-done.23.refs_13_.refs_10_.refs_20_), channel_id=1, source_target_pairs={{0,16},{1,49},{2,18},{3,51},{4,20},{5,53},{6,22},{7,55},{8,24},{9,... | collective-permute-start | bytes 2752520 | tf_op jit(solution)/shard_map/ppermute | solution.py:216
  203.7 2.1 shard_map.31.refs_8_
  206.2 2.1 shard_map.32.refs_10_
  209.8 2.9 %shard_map.34.refs_15_ = f32[1536,896]{1,0:T(8,128)S(1)} custom-call(bf16[96,8192]{1,0:T(8,128)(2,1)S(1)} %copy-done, bf16[96,8192]{1,0:T(8,128)(2,1)S(1)} %collective-permute-done.refs_1_, bf16[96,8192]{1,0:T(8,128)(2,1)S(1)} %collective-permute-done.1.refs_2_, ...), custom_call_target="tpu_custom_call", output_to_operand_aliasing={{}: (16, {})} | custom-call | flops 2113929216 | bytes 2113929 | tf_op jit(solution)/shard_map/pallas_call | solution.py:170
  212.8 1.9 collective-permute-start.19
  214.7 2.4 %shard_map.35.refs_15_ = f32[1536,896]{1,0:T(8,128)S(1)} custom-call(bf16[96,8192]{1,0:T(8,128)(2,1)S(1)} %copy-done, bf16[96,8192]{1,0:T(8,128)(2,1)S(1)} %collective-permute-done.refs_1_, bf16[96,8192]{1,0:T(8,128)(2,1)S(1)} %collective-permute-done.1.refs_2_, ...), custom_call_target="tpu_custom_call", output_to_operand_aliasing={{}: (15, {})} | custom-call | flops 1585446912 | bytes 1585446 | tf_op jit(solution)/shard_map/pallas_call | solution.py:170
  218.6 3.0 %shard_map.36.refs_15_ = f32[1536,896]{1,0:T(8,128)S(1)} custom-call(bf16[96,8192]{1,0:T(8,128)(2,1)S(1)} %collective-permute-done.11.refs_0_.refs_12_, bf16[96,8192]{1,0:T(8,128)(2,1)S(1)} %collective-permute-done.12.refs_1_.refs_13_, bf16[1024,896]{1,0:T(8,128)(2,1)S(1)} %copy-done.1, ...), custom_call_target="tpu_custom_call", output_to_operand_aliasing={{}: (15, {})} | custom-call | flops 2466250752 | bytes 2466250 | tf_op jit(solution)/shard_map/pallas_call | solution.py:170
  221.6 1.8 shard_map.37.refs_10_
  223.5 2.4 %shard_map.38.refs_17_ = f32[1536,896]{1,0:T(8,128)S(1)} custom-call(bf16[96,6144]{1,0:T(8,128)(2,1)S(1)} %collective-permute-done.13.refs_0_.refs_14_, bf16[96,6144]{1,0:T(8,128)(2,1)S(1)} %collective-permute-done.15.refs_1_.refs_15_.refs_16_, bf16[1024,896]{1,0:T(8,128)(2,1)S(1)} %copy-done.1, ...), custom_call_target="tpu_custom_call", output_to_operand_aliasing={{}: (10, {})} | custom-call | flops 1937768448 | bytes 1937768 | tf_op jit(solution)/shard_map/pallas_call | solution.py:170
  225.9 3.1 %collective-permute-done.29.refs_16_ = bf16[256,896]{1,0:T(8,128)(2,1)S(1)} collective-permute-done((bf16[256,896]{1,0:T(8,128)(2,1)S(1)}, bf16[256,896]{1,0:T(8,128)(2,1)S(1)}, u32[]{:S(2)}, u32[]{:S(2)}) %collective-permute-start.29) | collective-permute-done | bytes 458784 | tf_op jit(solution)/shard_map/ppermute | solution.py:216
  230.4 2.7 %shard_map.40 = bf16[1536,896]{1,0:T(8,128)(2,1)} custom-call(bf16[96,8192]{1,0:T(8,128)(2,1)S(1)} %copy-done, bf16[96,8192]{1,0:T(8,128)(2,1)S(1)} %collective-permute-done.refs_1_, bf16[96,8192]{1,0:T(8,128)(2,1)S(1)} %collective-permute-done.1.refs_2_, bf16[96,8192]{1,0:T(8,128)(2,1)S(1)} %collective-permute-done.2.refs_3_, ...), custom_call_target="tpu_custom_call" | custom-call | flops 1409286144 | bytes 1409286 | tf_op jit(solution)/shard_map/pallas_call | solution.py:170
  (55 shorter events, 17.7 us)
Async XLA Ops:
  0.0 88.3 %collective-permute-start.2 = (bf16[96,8192]{1,0:T(8,128)(2,1)}, bf16[96,8192]{1,0:T(8,128)(2,1)S(1)}, u32[]{:S(2)}, u32[]{:S(2)}) collective-permute-start(bf16[96,8192]{1,0:T(8,128)(2,1)} %refs_0_.17), channel_id=1, source_target_pairs={{0,2},{1,3},{2,0},{3,1},{4,6},{5,7},{6,4},{7,5},{8,10},{9,11},{10,... | collective-permute-start | bytes 4718600 | tf_op jit(solution)/shard_map/ppermute | solution.py:216
  5.0 76.3 %collective-permute-start.22 = (bf16[512,896]{1,0:T(8,128)(2,1)S(1)}, bf16[512,896]{1,0:T(8,128)(2,1)S(1)}, u32[]{:S(2)}, u32[]{:S(2)}) collective-permute-start(bf16[512,896]{1,0:T(8,128)(2,1)S(1)} %slice.10), channel_id=1, source_target_pairs={{0,64},{1,65},{2,66},{3,67},{4,68},{5,69},{6,70},{7,71},{8,72},{9,... | collective-permute-start | bytes 2752520 | tf_op jit(solution)/shard_map/ppermute | solution.py:216
  6.7 60.9 %collective-permute-start.17 = (bf16[256,896]{1,0:T(8,128)(2,1)S(1)}, bf16[256,896]{1,0:T(8,128)(2,1)S(1)}, u32[]{:S(2)}, u32[]{:S(2)}) collective-permute-start(bf16[256,896]{1,0:T(8,128)(2,1)S(1)} %get-tuple-element.10), channel_id=1, source_target_pairs={{0,64},{1,65},{2,66},{3,67},{4,68},{5,69},{6,70},{7,71},{8,72},{9,... | collective-permute-start | bytes 1376264 | tf_op jit(solution)/shard_map/ppermute | solution.py:216
  7.9 69.6 %collective-permute-start.30 = (bf16[256,896]{1,0:T(8,128)(2,1)S(1)}, bf16[256,896]{1,0:T(8,128)(2,1)S(1)}, u32[]{:S(2)}, u32[]{:S(2)}) collective-permute-start(bf16[256,896]{1,0:T(8,128)(2,1)S(1)} %get-tuple-element.9), channel_id=1, source_target_pairs={{0,64},{1,65},{2,66},{3,67},{4,68},{5,69},{6,70},{7,71},{8,72},{9,... | collective-permute-start | bytes 1376264 | tf_op jit(solution)/shard_map/ppermute | solution.py:216
  67.7 16.1 %collective-permute-start.18 = (bf16[256,896]{1,0:T(8,128)(2,1)S(1)}, bf16[256,896]{1,0:T(8,128)(2,1)S(1)}, u32[]{:S(2)}, u32[]{:S(2)}) collective-permute-start(bf16[256,896]{1,0:T(8,128)(2,1)S(1)} %collective-permute-done.17.refs_9_.refs_7_), channel_id=1, source_target_pairs={{0,16},{1,49},{2,18},{3,51},{4,20},{5,53},{6,22},{7,55},{8,24},{9,... | collective-permute-start | bytes 1376264 | tf_op jit(solution)/shard_map/ppermute | solution.py:216
  71.4 13.6 %collective-permute-start.27 = (bf16[256,896]{1,0:T(8,128)(2,1)S(1)}, bf16[256,896]{1,0:T(8,128)(2,1)S(1)}, u32[]{:S(2)}, u32[]{:S(2)}) collective-permute-start(bf16[256,896]{1,0:T(8,128)(2,1)S(1)} %collective-permute-done.17.refs_9_.refs_7_), channel_id=1, source_target_pairs={{0,48},{1,17},{2,50},{3,19},{4,52},{5,21},{6,54},{7,23},{8,56},{9,... | collective-permute-start | bytes 1376264 | tf_op jit(solution)/shard_map/ppermute | solution.py:216
  77.5 42.3 %collective-permute-start.20 = (bf16[1024,896]{1,0:T(8,128)(2,1)S(1)}, bf16[1024,896]{1,0:T(8,128)(2,1)S(1)}, u32[]{:S(2)}, u32[]{:S(2)}) collective-permute-start(bf16[1024,896]{1,0:T(8,128)(2,1)S(1)} %copy-done.1), channel_id=1, source_target_pairs={{0,16},{1,49},{2,18},{3,51},{4,20},{5,53},{6,22},{7,55},{8,24},{9,... | collective-permute-start | bytes 5505032 | tf_op jit(solution)/shard_map/ppermute | solution.py:216
  81.2 31.9 %collective-permute-start = (bf16[96,8192]{1,0:T(8,128)(2,1)S(1)}, bf16[96,8192]{1,0:T(8,128)(2,1)S(1)}, u32[]{:S(2)}, u32[]{:S(2)}) collective-permute-start(bf16[96,8192]{1,0:T(8,128)(2,1)S(1)} %copy-done), channel_id=1, source_target_pairs={{0,4},{1,13},{2,6},{3,15},{4,8},{5,1},{6,10},{7,3},{8,12},{9,5},{1... | collective-permute-start | bytes 4718600 | tf_op jit(solution)/shard_map/ppermute | solution.py:216
  83.7 35.0 %collective-permute-start.1 = (bf16[96,8192]{1,0:T(8,128)(2,1)S(1)}, bf16[96,8192]{1,0:T(8,128)(2,1)S(1)}, u32[]{:S(2)}, u32[]{:S(2)}) collective-permute-start(bf16[96,8192]{1,0:T(8,128)(2,1)S(1)} %copy-done), channel_id=1, source_target_pairs={{0,12},{1,5},{2,14},{3,7},{4,0},{5,9},{6,2},{7,11},{8,4},{9,13},{1... | collective-permute-start | bytes 4718600 | tf_op jit(solution)/shard_map/ppermute | solution.py:216
  85.0 33.7 %collective-permute-start.3 = (bf16[96,8192]{1,0:T(8,128)(2,1)S(1)}, bf16[96,8192]{1,0:T(8,128)(2,1)S(1)}, u32[]{:S(2)}, u32[]{:S(2)}) collective-permute-start(bf16[96,8192]{1,0:T(8,128)(2,1)S(1)} %copy-done), channel_id=1, source_target_pairs={{0,1},{1,0},{2,3},{3,2},{4,5},{5,4},{6,7},{7,6},{8,9},{9,8},{10,11... | collective-permute-start | bytes 4718600 | tf_op jit(solution)/shard_map/ppermute | solution.py:216
  88.3 35.9 %collective-permute-start.25 = (bf16[1024,896]{1,0:T(8,128)(2,1)S(1)}, bf16[1024,896]{1,0:T(8,128)(2,1)S(1)}, u32[]{:S(2)}, u32[]{:S(2)}) collective-permute-start(bf16[1024,896]{1,0:T(8,128)(2,1)S(1)} %copy-done.1), channel_id=1, source_target_pairs={{0,48},{1,17},{2,50},{3,19},{4,52},{5,21},{6,54},{7,23},{8,56},{9,... | collective-permute-start | bytes 5505032 | tf_op jit(solution)/shard_map/ppermute | solution.py:216
  113.2 31.9 %collective-permute-start.6 = (bf16[96,8192]{1,0:T(8,128)(2,1)S(1)}, bf16[96,8192]{1,0:T(8,128)(2,1)S(1)}, u32[]{:S(2)}, u32[]{:S(2)}) collective-permute-start(bf16[96,8192]{1,0:T(8,128)(2,1)S(1)} %collective-permute-done.2.refs_3_), channel_id=1, source_target_pairs={{0,1},{1,0},{2,3},{3,2},{4,5},{5,4},{6,7},{7,6},{8,9},{9,8},{10,11... | collective-permute-start | bytes 4718600 | tf_op jit(solution)/shard_map/ppermute | solution.py:216
  118.7 27.2 %collective-permute-start.4 = (bf16[96,8192]{1,0:T(8,128)(2,1)S(1)}, bf16[96,8192]{1,0:T(8,128)(2,1)S(1)}, u32[]{:S(2)}, u32[]{:S(2)}) collective-permute-start(bf16[96,8192]{1,0:T(8,128)(2,1)S(1)} %collective-permute-done.refs_1_), channel_id=1, source_target_pairs={{0,1},{1,0},{2,3},{3,2},{4,5},{5,4},{6,7},{7,6},{8,9},{9,8},{10,11... | collective-permute-start | bytes 4718600 | tf_op jit(solution)/shard_map/ppermute | solution.py:216
  118.7 23.8 %collective-permute-start.24 = (bf16[512,896]{1,0:T(8,128)(2,1)S(1)}, bf16[512,896]{1,0:T(8,128)(2,1)S(1)}, u32[]{:S(2)}, u32[]{:S(2)}) collective-permute-start(bf16[512,896]{1,0:T(8,128)(2,1)S(1)} %collective-permute-done.22.refs_8_.refs_6_), channel_id=1, source_target_pairs={{0,48},{1,17},{2,50},{3,19},{4,52},{5,21},{6,54},{7,23},{8,56},{9,... | collective-permute-start | bytes 2752520 | tf_op jit(solution)/shard_map/ppermute | solution.py:216
  119.8 25.3 %collective-permute-start.23 = (bf16[512,896]{1,0:T(8,128)(2,1)S(1)}, bf16[512,896]{1,0:T(8,128)(2,1)S(1)}, u32[]{:S(2)}, u32[]{:S(2)}) collective-permute-start(bf16[512,896]{1,0:T(8,128)(2,1)S(1)} %collective-permute-done.22.refs_8_.refs_6_), channel_id=1, source_target_pairs={{0,16},{1,49},{2,18},{3,51},{4,20},{5,53},{6,22},{7,55},{8,24},{9,... | collective-permute-start | bytes 2752520 | tf_op jit(solution)/shard_map/ppermute | solution.py:216
  124.2 23.6 %collective-permute-start.7 = (bf16[96,8192]{1,0:T(8,128)(2,1)S(1)}, bf16[96,8192]{1,0:T(8,128)(2,1)S(1)}, u32[]{:S(2)}, u32[]{:S(2)}) collective-permute-start(bf16[96,8192]{1,0:T(8,128)(2,1)S(1)} %collective-permute-done.2.refs_3_), channel_id=1, source_target_pairs={{0,4},{1,13},{2,6},{3,15},{4,8},{5,1},{6,10},{7,3},{8,12},{9,5},{1... | collective-permute-start | bytes 4718600 | tf_op jit(solution)/shard_map/ppermute | solution.py:216
  142.5 36.5 %collective-permute-start.8 = (bf16[96,8192]{1,0:T(8,128)(2,1)S(1)}, bf16[96,8192]{1,0:T(8,128)(2,1)S(1)}, u32[]{:S(2)}, u32[]{:S(2)}) collective-permute-start(bf16[96,8192]{1,0:T(8,128)(2,1)S(1)} %collective-permute-done.2.refs_3_), channel_id=1, source_target_pairs={{0,12},{1,5},{2,14},{3,7},{4,0},{5,9},{6,2},{7,11},{8,4},{9,13},{1... | collective-permute-start | bytes 4718600 | tf_op jit(solution)/shard_map/ppermute | solution.py:216
  145.1 34.1 %collective-permute-start.5 = (bf16[96,8192]{1,0:T(8,128)(2,1)S(1)}, bf16[96,8192]{1,0:T(8,128)(2,1)S(1)}, u32[]{:S(2)}, u32[]{:S(2)}) collective-permute-start(bf16[96,8192]{1,0:T(8,128)(2,1)S(1)} %collective-permute-done.1.refs_2_), channel_id=1, source_target_pairs={{0,1},{1,0},{2,3},{3,2},{4,5},{5,4},{6,7},{7,6},{8,9},{9,8},{10,11... | collective-permute-start | bytes 4718600 | tf_op jit(solution)/shard_map/ppermute | solution.py:216
  145.1 36.9 %collective-permute-start.28 = (bf16[1024,896]{1,0:T(8,128)(2,1)S(1)}, bf16[1024,896]{1,0:T(8,128)(2,1)S(1)}, u32[]{:S(2)}, u32[]{:S(2)}) collective-permute-start(bf16[1024,896]{1,0:T(8,128)(2,1)S(1)} %collective-permute-done.20.whole.refs_9_.refs_3_), channel_id=1, source_target_pairs={{0,16},{1,49},{2,18},{3,51},{4,20},{5,53},{6,22},{7,55},{8,24},{9,... | collective-permute-start | bytes 5505032 | tf_op jit(solution)/shard_map/ppermute | solution.py:216
  145.9 36.0 %collective-permute-start.11 = (bf16[96,8192]{1,0:T(8,128)(2,1)S(1)}, bf16[96,8192]{1,0:T(8,128)(2,1)S(1)}, u32[]{:S(2)}, u32[]{:S(2)}) collective-permute-start(bf16[96,8192]{1,0:T(8,128)(2,1)S(1)} %collective-permute-done.refs_1_), channel_id=1, source_target_pairs={{0,4},{1,13},{2,6},{3,15},{4,8},{5,1},{6,10},{7,3},{8,12},{9,5},{1... | collective-permute-start | bytes 4718600 | tf_op jit(solution)/shard_map/ppermute | solution.py:216
  147.8 52.9 %collective-permute-start.9 = (bf16[96,8192]{1,0:T(8,128)(2,1)S(1)}, bf16[96,8192]{1,0:T(8,128)(2,1)S(1)}, u32[]{:S(2)}, u32[]{:S(2)}) collective-permute-start(bf16[96,8192]{1,0:T(8,128)(2,1)S(1)} %collective-permute-done.7.whole.refs_0_.refs_8_), channel_id=1, source_target_pairs={{0,1},{1,0},{2,3},{3,2},{4,5},{5,4},{6,7},{7,6},{8,9},{9,8},{10,11... | collective-permute-start | bytes 4718600 | tf_op jit(solution)/shard_map/ppermute | solution.py:216
  179.0 26.8 %collective-permute-start.10 = (bf16[96,8192]{1,0:T(8,128)(2,1)S(1)}, bf16[96,8192]{1,0:T(8,128)(2,1)S(1)}, u32[]{:S(2)}, u32[]{:S(2)}) collective-permute-start(bf16[96,8192]{1,0:T(8,128)(2,1)S(1)} %collective-permute-done.8.refs_1_.refs_9_), channel_id=1, source_target_pairs={{0,1},{1,0},{2,3},{3,2},{4,5},{5,4},{6,7},{7,6},{8,9},{9,8},{10,11... | collective-permute-start | bytes 4718600 | tf_op jit(solution)/shard_map/ppermute | solution.py:216
  179.2 15.9 %collective-permute-start.13 = (bf16[96,6144]{1,0:T(8,128)(2,1)S(1)}, bf16[96,6144]{1,0:T(8,128)(2,1)S(1)}, u32[]{:S(2)}, u32[]{:S(2)}) collective-permute-start(bf16[96,6144]{1,0:T(8,128)(2,1)S(1)} %get-tuple-element.7), channel_id=1, source_target_pairs={{0,4},{1,13},{2,6},{3,15},{4,8},{5,1},{6,10},{7,3},{8,12},{9,5},{1... | collective-permute-start | bytes 3538952 | tf_op jit(solution)/shard_map/ppermute | solution.py:216
  181.9 35.2 %collective-permute-start.12 = (bf16[96,8192]{1,0:T(8,128)(2,1)S(1)}, bf16[96,8192]{1,0:T(8,128)(2,1)S(1)}, u32[]{:S(2)}, u32[]{:S(2)}) collective-permute-start(bf16[96,8192]{1,0:T(8,128)(2,1)S(1)} %collective-permute-done.11.refs_0_.refs_12_), channel_id=1, source_target_pairs={{0,1},{1,0},{2,3},{3,2},{4,5},{5,4},{6,7},{7,6},{8,9},{9,8},{10,11... | collective-permute-start | bytes 4718600 | tf_op jit(solution)/shard_map/ppermute | solution.py:216
  182.0 17.5 %collective-permute-start.21 = (bf16[256,896]{1,0:T(8,128)(2,1)S(1)}, bf16[256,896]{1,0:T(8,128)(2,1)S(1)}, u32[]{:S(2)}, u32[]{:S(2)}) collective-permute-start(bf16[256,896]{1,0:T(8,128)(2,1)S(1)} %kS.5), channel_id=1, source_target_pairs={{0,64},{1,65},{2,66},{3,67},{4,68},{5,69},{6,70},{7,71},{8,72},{9,... | collective-permute-start | bytes 1376264 | tf_op jit(solution)/shard_map/ppermute | solution.py:216
  195.1 28.4 %collective-permute-start.15 = (bf16[96,6144]{1,0:T(8,128)(2,1)S(1)}, bf16[96,6144]{1,0:T(8,128)(2,1)S(1)}, u32[]{:S(2)}, u32[]{:S(2)}) collective-permute-start(bf16[96,6144]{1,0:T(8,128)(2,1)S(1)} %collective-permute-done.13.refs_0_.refs_14_), channel_id=1, source_target_pairs={{0,1},{1,0},{2,3},{3,2},{4,5},{5,4},{6,7},{7,6},{8,9},{9,8},{10,11... | collective-permute-start | bytes 3538952 | tf_op jit(solution)/shard_map/ppermute | solution.py:216
  199.5 13.2 %collective-permute-start.26 = (bf16[256,896]{1,0:T(8,128)(2,1)S(1)}, bf16[256,896]{1,0:T(8,128)(2,1)S(1)}, u32[]{:S(2)}, u32[]{:S(2)}) collective-permute-start(bf16[256,896]{1,0:T(8,128)(2,1)S(1)} %kS.6), channel_id=1, source_target_pairs={{0,64},{1,65},{2,66},{3,67},{4,68},{5,69},{6,70},{7,71},{8,72},{9,... | collective-permute-start | bytes 1376264 | tf_op jit(solution)/shard_map/ppermute | solution.py:216
  200.7 20.9 %collective-permute-start.31 = (bf16[512,896]{1,0:T(8,128)(2,1)S(1)}, bf16[512,896]{1,0:T(8,128)(2,1)S(1)}, u32[]{:S(2)}, u32[]{:S(2)}) collective-permute-start(bf16[512,896]{1,0:T(8,128)(2,1)S(1)} %collective-permute-done.23.refs_13_.refs_10_.refs_20_), channel_id=1, source_target_pairs={{0,16},{1,49},{2,18},{3,51},{4,20},{5,53},{6,22},{7,55},{8,24},{9,... | collective-permute-start | bytes 2752520 | tf_op jit(solution)/shard_map/ppermute | solution.py:216
  205.9 8.8 %collective-permute-start.14 = (bf16[96,2048]{1,0:T(8,128)(2,1)S(1)}, bf16[96,2048]{1,0:T(8,128)(2,1)S(1)}, u32[]{:S(2)}, u32[]{:S(2)}) collective-permute-start(bf16[96,2048]{1,0:T(8,128)(2,1)S(1)} %get-tuple-element.8), channel_id=1, source_target_pairs={{0,4},{1,13},{2,6},{3,15},{4,8},{5,1},{6,10},{7,3},{8,12},{9,5},{1... | collective-permute-start | bytes 1179656 | tf_op jit(solution)/shard_map/ppermute | solution.py:216
  212.8 17.6 %collective-permute-start.19 = (bf16[256,896]{1,0:T(8,128)(2,1)S(1)}, bf16[256,896]{1,0:T(8,128)(2,1)S(1)}, u32[]{:S(2)}, u32[]{:S(2)}) collective-permute-start(bf16[256,896]{1,0:T(8,128)(2,1)S(1)} %collective-permute-done.18.refs_12_.refs_22_), channel_id=1, source_target_pairs={{0,16},{1,49},{2,18},{3,51},{4,20},{5,53},{6,22},{7,55},{8,24},{9,... | collective-permute-start | bytes 1376264 | tf_op jit(solution)/shard_map/ppermute | solution.py:216
  214.7 15.7 %collective-permute-start.16 = (bf16[96,2048]{1,0:T(8,128)(2,1)S(1)}, bf16[96,2048]{1,0:T(8,128)(2,1)S(1)}, u32[]{:S(2)}, u32[]{:S(2)}) collective-permute-start(bf16[96,2048]{1,0:T(8,128)(2,1)S(1)} %collective-permute-done.14.refs_15_), channel_id=1, source_target_pairs={{0,1},{1,0},{2,3},{3,2},{4,5},{5,4},{6,7},{7,6},{8,9},{9,8},{10,11... | collective-permute-start | bytes 1179656 | tf_op jit(solution)/shard_map/ppermute | solution.py:216
  217.2 11.9 %collective-permute-start.29 = (bf16[256,896]{1,0:T(8,128)(2,1)S(1)}, bf16[256,896]{1,0:T(8,128)(2,1)S(1)}, u32[]{:S(2)}, u32[]{:S(2)}) collective-permute-start(bf16[256,896]{1,0:T(8,128)(2,1)S(1)} %kS.7), channel_id=1, source_target_pairs={{0,64},{1,65},{2,66},{3,67},{4,68},{5,69},{6,70},{7,71},{8,72},{9,... | collective-permute-start | bytes 1376264 | tf_op jit(solution)/shard_map/ppermute | solution.py:216
  (2 other events, 158.7 us)

commit v6 on v5

--- a/solution.py
+++ b/solution.py
@@ -53,11 +53,11 @@
     ("kH",),
     ("ctD", "co", "tD"), ("S1bD", "zP", "S1bP"),
     ("kJ",),
+    ("ct1Da", "co", "t1Da"),
     ("kI",),
-    ("ct1Da", "co", "t1Da"),
+    ("kK",),
     ("kL",),
     ("ct1Db", "co", "t1Db"),
-    ("kK",),
     ("kM",),
     ("kG",),
 ]
@@ -78,7 +78,7 @@
 
 
 def piece_of(name, block):
-    return name if name not in B2 else name + "b" if block in (5, 6) else name + "a"
+    return name if name not in B2 else name + "b" if block > 4 else name + "a"
 
 
 KERNELS = {
@@ -92,9 +92,9 @@
     "kI": [(1152, 1344, W0 + WD + S1 + W1 + W2)],
     "kJ": [(0, 1152, W2)],
     "kL": [(0, 1344, W3)],
-    "kK": [(1344, 1536, W0 + WD + S1 + W1[:1] + W3)],
-    "kM": [(0, 1344, W4), (1344, 1536, W4)],
-    "kG": [(0, 1344, W5), (1344, 1536, W5 + W1[1:] + W2)],
+    "kK": [(1344, 1536, W0 + WD + S1 + W1[:1])],
+    "kM": [(0, 1344, W4)],
+    "kG": [(0, 1344, W5), (1344, 1536, W1[1:] + W2 + W3 + W4 + W5)],
 }
 TILE = 384
 VMEM, LAST_VMEM = 4, 6
@@ -110,7 +110,7 @@
     far = lambda name, c: 3 - 2 * c if "P" in name else 1 + 2 * c if "M" in name else 2 if "D" in name else 0
     block_at = [((yl ^ one) * 4 + (z + far(k, core)) % 4) * KB for one in range(2) for k in ("", "P", "M", "D")]
     block_in_piece = [block_at[b] - yl * (4 * KB) for b in range(4)]
-    block_in_piece += [4 * KB, (far("P", core) - 1) // 2 * KB, (far("M", core) - 1) // 2 * KB, 5 * KB]
+    block_in_piece += [4 * KB, (far("P", core) - 1) // 2 * KB, (far("M", core) - 1) // 2 * KB, 2 * KB]
     n_t, n_w = len(plan["t"]), len(plan["w"])
     t_refs, w_refs, refs = refs[:n_t], refs[n_t : n_t + n_w], refs[n_t + n_w :]
     sums_ref, refs = (refs[0], refs[1:]) if plan["taken"] else (None, refs)
@@ -184,10 +184,10 @@
     yl, z = row // 4, row % 4
     columns = lambda block, n: whole[:, pl.ds(pl.multiple_of(block * KB, KB), n * KB)]
     a[:, : 4 * KB] = columns(yl * 4, 4)
-    a[:, 4 * KB : 5 * KB] = columns((1 - yl) * 4 + z, 1)
-    a[:, 5 * KB :] = columns((1 - yl) * 4 + (z + 2) % 4, 1)
+    a[:, 4 * KB :] = columns((1 - yl) * 4 + z, 1)
     b[:, :KB] = columns((1 - yl) * 4 + (z + 1) % 4, 1)
-    b[:, KB:] = columns((1 - yl) * 4 + (z + 3) % 4, 1)
+    b[:, KB : 2 * KB] = columns((1 - yl) * 4 + (z + 3) % 4, 1)
+    b[:, 2 * KB :] = columns((1 - yl) * 4 + (z + 2) % 4, 1)
 
 
 def first_rows(whole, out):
@@ -215,7 +215,7 @@
         if len(step) == 3:
             got[step[0]] = lax.ppermute(got[step[2]], ("row", "col"), WAYS[step[1]])
         elif step == ("kS",):
-            got["t1Pa"], got["t1Pb"] = cut(got["t1P"], two_pieces, [(ROWS, 6 * KB), (ROWS, 2 * KB)])
+            got["t1Pa"], got["t1Pb"] = cut(got["t1P"], two_pieces, [(ROWS, 5 * KB), (ROWS, 3 * KB)])
         else:
             sums = call(step[0], got, sums)
     return sums

time: 233 us -> 231 us (level)
  transfers between devices with their start and end apart: 32 -> 32, of which waited for: 10 -> 11; matrix products, arithmetic and copies ran while one was open for 1% -> 1% of each run, Pallas kernels for 12% -> 12%
where the time goes in v6:
time: 231 us
  waiting for transfers between devices  150 us (65%)
  starting transfers between devices  46.5 us (20%)
  Pallas kernels  31.1 us (13%)
  local copies, waits for them, and re-layouts  2.49 us (1%)
    ppermute x32, waiting for transfers between devices, on_device(): got[step[0]] = lax.ppermute(got[step[2]], ('row', 'col'), WAYS[step[1]])  150 us
    ppermute x32, starting transfers between devices, on_device(): got[step[0]] = lax.ppermute(got[step[2]], ('row', 'col'), WAYS[step[1]])  46.5 us
    pallas_call x13, Pallas kernels, call(): pl.pallas_call(functools.partial(kernel, plan), out_shape=jax.ShapeDtypeS...  30.9 us
  transfers between devices with their start and end apart: 32, of which 11 were waited for; matrix products, arithmetic and copies ran while one was open for 1% of the time, Pallas kernels for 12%

profile of v6, /device:TPU:1, one launch (start us, length us, event | category | flops | bytes accessed | tf_op | source)
XLA Modules:
  0.0 231.0 jit_solution(826267426150952934)
XLA Ops:
  0.0 3.7 %collective-permute-start.2 = (bf16[96,8192]{1,0:T(8,128)(2,1)}, bf16[96,8192]{1,0:T(8,128)(2,1)S(1)}, u32[]{:S(2)}, u32[]{:S(2)}) collective-permute-start(bf16[96,8192]{1,0:T(8,128)(2,1)} %refs_0_.17), channel_id=1, source_target_pairs={{0,2},{1,3},{2,0},{3,1},{4,6},{5,7},{6,4},{7,5},{8,10},{9,11},{10,... | collective-permute-start | bytes 4718600 | tf_op jit(solution)/shard_map/ppermute | solution.py:216
  8.2 59.4 %collective-permute-done.15.refs_9_.refs_7_ = bf16[256,896]{1,0:T(8,128)(2,1)S(1)} collective-permute-done((bf16[256,896]{1,0:T(8,128)(2,1)S(1)}, bf16[256,896]{1,0:T(8,128)(2,1)S(1)}, u32[]{:S(2)}, u32[]{:S(2)}) %collective-permute-start.15) | collective-permute-done | bytes 458784 | tf_op jit(solution)/shard_map/ppermute | solution.py:216
  67.7 3.8 %collective-permute-start.16 = (bf16[256,896]{1,0:T(8,128)(2,1)S(1)}, bf16[256,896]{1,0:T(8,128)(2,1)S(1)}, u32[]{:S(2)}, u32[]{:S(2)}) collective-permute-start(bf16[256,896]{1,0:T(8,128)(2,1)S(1)} %collective-permute-done.15.refs_9_.refs_7_), channel_id=1, source_target_pairs={{0,16},{1,49},{2,18},{3,51},{4,20},{5,53},{6,22},{7,55},{8,24},{9,... | collective-permute-start | bytes 1376264 | tf_op jit(solution)/shard_map/ppermute | solution.py:216
  71.4 6.1 %collective-permute-done.31.refs_8_.refs_14_ = bf16[256,896]{1,0:T(8,128)(2,1)S(1)} collective-permute-done((bf16[256,896]{1,0:T(8,128)(2,1)S(1)}, bf16[256,896]{1,0:T(8,128)(2,1)S(1)}, u32[]{:S(2)}, u32[]{:S(2)}) %collective-permute-start.31) | collective-permute-done | bytes 458784 | tf_op jit(solution)/shard_map/ppermute | solution.py:216
  77.5 2.5 %collective-permute-start = (bf16[96,8192]{1,0:T(8,128)(2,1)S(1)}, bf16[96,8192]{1,0:T(8,128)(2,1)S(1)}, u32[]{:S(2)}, u32[]{:S(2)}) collective-permute-start(bf16[96,8192]{1,0:T(8,128)(2,1)S(1)} %copy-done), channel_id=1, source_target_pairs={{0,4},{1,13},{2,6},{3,15},{4,8},{5,1},{6,10},{7,3},{8,12},{9,5},{1... | collective-permute-start | bytes 4718600 | tf_op jit(solution)/shard_map/ppermute | solution.py:216
  80.0 5.6 %collective-permute-start.3 = (bf16[96,8192]{1,0:T(8,128)(2,1)S(1)}, bf16[96,8192]{1,0:T(8,128)(2,1)S(1)}, u32[]{:S(2)}, u32[]{:S(2)}) collective-permute-start(bf16[96,8192]{1,0:T(8,128)(2,1)S(1)} %copy-done), channel_id=1, source_target_pairs={{0,1},{1,0},{2,3},{3,2},{4,5},{5,4},{6,7},{7,6},{8,9},{9,8},{10,11... | collective-permute-start | bytes 4718600 | tf_op jit(solution)/shard_map/ppermute | solution.py:216
  87.0 24.7 %collective-permute-done.refs_1_ = bf16[96,8192]{1,0:T(8,128)(2,1)S(1)} collective-permute-done((bf16[96,8192]{1,0:T(8,128)(2,1)S(1)}, bf16[96,8192]{1,0:T(8,128)(2,1)S(1)}, u32[]{:S(2)}, u32[]{:S(2)}) %collective-permute-start) | collective-permute-done | bytes 1572896 | tf_op jit(solution)/shard_map/ppermute | solution.py:216
  111.7 5.3 %collective-permute-start.6 = (bf16[96,8192]{1,0:T(8,128)(2,1)S(1)}, bf16[96,8192]{1,0:T(8,128)(2,1)S(1)}, u32[]{:S(2)}, u32[]{:S(2)}) collective-permute-start(bf16[96,8192]{1,0:T(8,128)(2,1)S(1)} %collective-permute-done.2.refs_3_), channel_id=1, source_target_pairs={{0,1},{1,0},{2,3},{3,2},{4,5},{5,4},{6,7},{7,6},{8,9},{9,8},{10,11... | collective-permute-start | bytes 4718600 | tf_op jit(solution)/shard_map/ppermute | solution.py:216
  117.1 1.6 collective-permute-start.22
  118.7 8.2 %collective-permute-done.18.whole.refs_9_.refs_3_ = bf16[1024,896]{1,0:T(8,128)(2,1)S(1)} collective-permute-done((bf16[1024,896]{1,0:T(8,128)(2,1)S(1)}, bf16[1024,896]{1,0:T(8,128)(2,1)S(1)}, u32[]{:S(2)}, u32[]{:S(2)}) %collective-permute-start.18) | collective-permute-done | bytes 1835040 | tf_op jit(solution)/shard_map/ppermute | solution.py:216
  127.0 2.2 collective-permute-done.23.whole.refs_10_.refs_4_
  129.2 1.7 collective-permute-start.7
  130.9 13.2 %collective-permute-done.22.refs_9_.refs_15_.refs_11_.refs_19_ = bf16[512,896]{1,0:T(8,128)(2,1)S(1)} collective-permute-done((bf16[512,896]{1,0:T(8,128)(2,1)S(1)}, bf16[512,896]{1,0:T(8,128)(2,1)S(1)}, u32[]{:S(2)}, u32[]{:S(2)}) %collective-permute-start.22) | collective-permute-done | bytes 917536 | tf_op jit(solution)/shard_map/ppermute | solution.py:216
  144.5 2.7 %collective-permute-done.21.refs_13_.refs_10_.refs_18_ = bf16[512,896]{1,0:T(8,128)(2,1)S(1)} collective-permute-done((bf16[512,896]{1,0:T(8,128)(2,1)S(1)}, bf16[512,896]{1,0:T(8,128)(2,1)S(1)}, u32[]{:S(2)}, u32[]{:S(2)}) %collective-permute-start.21) | collective-permute-done | bytes 917536 | tf_op jit(solution)/shard_map/ppermute | solution.py:216
  147.3 2.1 collective-permute-start.5
  149.6 1.9 collective-permute-start.11
  151.5 2.8 %collective-permute-start.9 = (bf16[96,8192]{1,0:T(8,128)(2,1)S(1)}, bf16[96,8192]{1,0:T(8,128)(2,1)S(1)}, u32[]{:S(2)}, u32[]{:S(2)}) collective-permute-start(bf16[96,8192]{1,0:T(8,128)(2,1)S(1)} %collective-permute-done.7.whole.refs_0_.refs_8_), channel_id=1, source_target_pairs={{0,1},{1,0},{2,3},{3,2},{4,5},{5,4},{6,7},{7,6},{8,9},{9,8},{10,11... | collective-permute-start | bytes 4718600 | tf_op jit(solution)/shard_map/ppermute | solution.py:216
  154.3 27.4 %collective-permute-done.8.refs_1_.refs_9_ = bf16[96,8192]{1,0:T(8,128)(2,1)S(1)} collective-permute-done((bf16[96,8192]{1,0:T(8,128)(2,1)S(1)}, bf16[96,8192]{1,0:T(8,128)(2,1)S(1)}, u32[]{:S(2)}, u32[]{:S(2)}) %collective-permute-start.8) | collective-permute-done | bytes 1572896 | tf_op jit(solution)/shard_map/ppermute | solution.py:216
  181.8 1.9 collective-permute-start.29
  186.5 5.0 %shard_map.28.refs_9_ = f32[1536,896]{1,0:T(8,128)S(1)} custom-call(bf16[96,8192]{1,0:T(8,128)(2,1)S(1)} %copy-done, bf16[96,8192]{1,0:T(8,128)(2,1)S(1)} %collective-permute-done.refs_1_, bf16[96,8192]{1,0:T(8,128)(2,1)S(1)} %collective-permute-done.1.refs_2_, bf16[96,8192]{1,0:T(8,128)(2,1)S(1)} %collective-permute-done.2.refs_3_, ...), custom_call_target="tpu_custom_call" | custom-call | flops 4227858432 | bytes 4227858 | tf_op jit(solution)/shard_map/pallas_call | solution.py:170
  192.6 2.4 %shard_map.30.refs_8_ = f32[1536,896]{1,0:T(8,128)S(1)} custom-call(bf16[96,8192]{1,0:T(8,128)(2,1)S(1)} %copy-done, bf16[96,8192]{1,0:T(8,128)(2,1)S(1)} %collective-permute-done.refs_1_, bf16[96,8192]{1,0:T(8,128)(2,1)S(1)} %collective-permute-done.1.refs_2_, bf16[96,8192]{1,0:T(8,128)(2,1)S(1)} %collective-permute-done.2.refs_3_, ...), custom_call_target="tpu_custom_call", output_to_operand_aliasing={{}: (10, {})} | custom-call | flops 1761607680 | bytes 1761607 | tf_op jit(solution)/shard_map/pallas_call | solution.py:170
  195.0 2.5 %collective-permute-done.19.refs_12_.refs_9_.refs_17_ = bf16[256,896]{1,0:T(8,128)(2,1)S(1)} collective-permute-done((bf16[256,896]{1,0:T(8,128)(2,1)S(1)}, bf16[256,896]{1,0:T(8,128)(2,1)S(1)}, u32[]{:S(2)}, u32[]{:S(2)}) %collective-permute-start.19) | collective-permute-done | bytes 458784 | tf_op jit(solution)/shard_map/ppermute | solution.py:216
  200.0 2.1 shard_map.31.refs_8_
  202.2 3.2 %collective-permute-start.26 = (bf16[512,896]{1,0:T(8,128)(2,1)S(1)}, bf16[512,896]{1,0:T(8,128)(2,1)S(1)}, u32[]{:S(2)}, u32[]{:S(2)}) collective-permute-start(bf16[512,896]{1,0:T(8,128)(2,1)S(1)} %collective-permute-done.21.refs_13_.refs_10_.refs_18_), channel_id=1, source_target_pairs={{0,16},{1,49},{2,18},{3,51},{4,20},{5,53},{6,22},{7,55},{8,24},{9,... | collective-permute-start | bytes 2752520 | tf_op jit(solution)/shard_map/ppermute | solution.py:216
  205.4 2.1 shard_map.32.refs_10_
  209.1 2.9 %shard_map.34.refs_15_ = f32[1536,896]{1,0:T(8,128)S(1)} custom-call(bf16[96,8192]{1,0:T(8,128)(2,1)S(1)} %copy-done, bf16[96,8192]{1,0:T(8,128)(2,1)S(1)} %collective-permute-done.refs_1_, bf16[96,8192]{1,0:T(8,128)(2,1)S(1)} %collective-permute-done.1.refs_2_, ...), custom_call_target="tpu_custom_call", output_to_operand_aliasing={{}: (16, {})} | custom-call | flops 2113929216 | bytes 2113929 | tf_op jit(solution)/shard_map/pallas_call | solution.py:170
  212.2 2.5 %shard_map.35.refs_15_ = f32[1536,896]{1,0:T(8,128)S(1)} custom-call(bf16[96,8192]{1,0:T(8,128)(2,1)S(1)} %copy-done, bf16[96,8192]{1,0:T(8,128)(2,1)S(1)} %collective-permute-done.refs_1_, bf16[96,8192]{1,0:T(8,128)(2,1)S(1)} %collective-permute-done.1.refs_2_, ...), custom_call_target="tpu_custom_call", output_to_operand_aliasing={{}: (15, {})} | custom-call | flops 1585446912 | bytes 1585446 | tf_op jit(solution)/shard_map/pallas_call | solution.py:170
  215.6 3.0 %shard_map.36.refs_9_ = f32[1536,896]{1,0:T(8,128)S(1)} custom-call(bf16[96,8192]{1,0:T(8,128)(2,1)S(1)} %collective-permute-done.11.refs_0_.refs_12_, bf16[96,8192]{1,0:T(8,128)(2,1)S(1)} %collective-permute-done.12.refs_1_.refs_13_, bf16[1024,896]{1,0:T(8,128)(2,1)S(1)} %copy-done.1, ...), custom_call_target="tpu_custom_call", output_to_operand_aliasing={{}: (15, {})} | custom-call | flops 2466250752 | bytes 2466250 | tf_op jit(solution)/shard_map/pallas_call | solution.py:170
  218.6 2.2 shard_map.37.refs_15_
  220.9 1.9 shard_map.38.refs_15_
  222.7 3.9 %collective-permute-done.28.refs_14_.refs_24_ = bf16[256,896]{1,0:T(8,128)(2,1)S(1)} collective-permute-done((bf16[256,896]{1,0:T(8,128)(2,1)S(1)}, bf16[256,896]{1,0:T(8,128)(2,1)S(1)}, u32[]{:S(2)}, u32[]{:S(2)}) %collective-permute-start.28) | collective-permute-done | bytes 458784 | tf_op jit(solution)/shard_map/ppermute | solution.py:216
  227.7 3.0 %shard_map.40 = bf16[1536,896]{1,0:T(8,128)(2,1)} custom-call(bf16[96,8192]{1,0:T(8,128)(2,1)S(1)} %copy-done, bf16[96,8192]{1,0:T(8,128)(2,1)S(1)} %collective-permute-done.refs_1_, bf16[96,8192]{1,0:T(8,128)(2,1)S(1)} %collective-permute-done.1.refs_2_, bf16[96,8192]{1,0:T(8,128)(2,1)S(1)} %collective-permute-done.2.refs_3_, ...), custom_call_target="tpu_custom_call" | custom-call | flops 1673527296 | bytes 1673527 | tf_op jit(solution)/shard_map/pallas_call | solution.py:170
  (55 shorter events, 17.0 us)
Async XLA Ops:
  0.0 86.0 %collective-permute-start.2 = (bf16[96,8192]{1,0:T(8,128)(2,1)}, bf16[96,8192]{1,0:T(8,128)(2,1)S(1)}, u32[]{:S(2)}, u32[]{:S(2)}) collective-permute-start(bf16[96,8192]{1,0:T(8,128)(2,1)} %refs_0_.17), channel_id=1, source_target_pairs={{0,2},{1,3},{2,0},{3,1},{4,6},{5,7},{6,4},{7,5},{8,10},{9,11},{10,... | collective-permute-start | bytes 4718600 | tf_op jit(solution)/shard_map/ppermute | solution.py:216
  5.0 75.0 %collective-permute-start.20 = (bf16[512,896]{1,0:T(8,128)(2,1)S(1)}, bf16[512,896]{1,0:T(8,128)(2,1)S(1)}, u32[]{:S(2)}, u32[]{:S(2)}) collective-permute-start(bf16[512,896]{1,0:T(8,128)(2,1)S(1)} %slice.10), channel_id=1, source_target_pairs={{0,64},{1,65},{2,66},{3,67},{4,68},{5,69},{6,70},{7,71},{8,72},{9,... | collective-permute-start | bytes 2752520 | tf_op jit(solution)/shard_map/ppermute | solution.py:216
  6.7 60.9 %collective-permute-start.15 = (bf16[256,896]{1,0:T(8,128)(2,1)S(1)}, bf16[256,896]{1,0:T(8,128)(2,1)S(1)}, u32[]{:S(2)}, u32[]{:S(2)}) collective-permute-start(bf16[256,896]{1,0:T(8,128)(2,1)S(1)} %get-tuple-element.10), channel_id=1, source_target_pairs={{0,64},{1,65},{2,66},{3,67},{4,68},{5,69},{6,70},{7,71},{8,72},{9,... | collective-permute-start | bytes 1376264 | tf_op jit(solution)/shard_map/ppermute | solution.py:216
  7.9 69.6 %collective-permute-start.31 = (bf16[256,896]{1,0:T(8,128)(2,1)S(1)}, bf16[256,896]{1,0:T(8,128)(2,1)S(1)}, u32[]{:S(2)}, u32[]{:S(2)}) collective-permute-start(bf16[256,896]{1,0:T(8,128)(2,1)S(1)} %get-tuple-element.9), channel_id=1, source_target_pairs={{0,64},{1,65},{2,66},{3,67},{4,68},{5,69},{6,70},{7,71},{8,72},{9,... | collective-permute-start | bytes 1376264 | tf_op jit(solution)/shard_map/ppermute | solution.py:216
  67.7 12.3 %collective-permute-start.16 = (bf16[256,896]{1,0:T(8,128)(2,1)S(1)}, bf16[256,896]{1,0:T(8,128)(2,1)S(1)}, u32[]{:S(2)}, u32[]{:S(2)}) collective-permute-start(bf16[256,896]{1,0:T(8,128)(2,1)S(1)} %collective-permute-done.15.refs_9_.refs_7_), channel_id=1, source_target_pairs={{0,16},{1,49},{2,18},{3,51},{4,20},{5,53},{6,22},{7,55},{8,24},{9,... | collective-permute-start | bytes 1376264 | tf_op jit(solution)/shard_map/ppermute | solution.py:216
  71.4 14.1 %collective-permute-start.25 = (bf16[256,896]{1,0:T(8,128)(2,1)S(1)}, bf16[256,896]{1,0:T(8,128)(2,1)S(1)}, u32[]{:S(2)}, u32[]{:S(2)}) collective-permute-start(bf16[256,896]{1,0:T(8,128)(2,1)S(1)} %collective-permute-done.15.refs_9_.refs_7_), channel_id=1, source_target_pairs={{0,48},{1,17},{2,50},{3,19},{4,52},{5,21},{6,54},{7,23},{8,56},{9,... | collective-permute-start | bytes 1376264 | tf_op jit(solution)/shard_map/ppermute | solution.py:216
  77.5 34.2 %collective-permute-start = (bf16[96,8192]{1,0:T(8,128)(2,1)S(1)}, bf16[96,8192]{1,0:T(8,128)(2,1)S(1)}, u32[]{:S(2)}, u32[]{:S(2)}) collective-permute-start(bf16[96,8192]{1,0:T(8,128)(2,1)S(1)} %copy-done), channel_id=1, source_target_pairs={{0,4},{1,13},{2,6},{3,15},{4,8},{5,1},{6,10},{7,3},{8,12},{9,5},{1... | collective-permute-start | bytes 4718600 | tf_op jit(solution)/shard_map/ppermute | solution.py:216
  80.0 37.1 %collective-permute-start.1 = (bf16[96,8192]{1,0:T(8,128)(2,1)S(1)}, bf16[96,8192]{1,0:T(8,128)(2,1)S(1)}, u32[]{:S(2)}, u32[]{:S(2)}) collective-permute-start(bf16[96,8192]{1,0:T(8,128)(2,1)S(1)} %copy-done), channel_id=1, source_target_pairs={{0,12},{1,5},{2,14},{3,7},{4,0},{5,9},{6,2},{7,11},{8,4},{9,13},{1... | collective-permute-start | bytes 4718600 | tf_op jit(solution)/shard_map/ppermute | solution.py:216
  80.0 37.1 %collective-permute-start.3 = (bf16[96,8192]{1,0:T(8,128)(2,1)S(1)}, bf16[96,8192]{1,0:T(8,128)(2,1)S(1)}, u32[]{:S(2)}, u32[]{:S(2)}) collective-permute-start(bf16[96,8192]{1,0:T(8,128)(2,1)S(1)} %copy-done), channel_id=1, source_target_pairs={{0,1},{1,0},{2,3},{3,2},{4,5},{5,4},{6,7},{7,6},{8,9},{9,8},{10,11... | collective-permute-start | bytes 4718600 | tf_op jit(solution)/shard_map/ppermute | solution.py:216
  85.6 41.4 %collective-permute-start.18 = (bf16[1024,896]{1,0:T(8,128)(2,1)S(1)}, bf16[1024,896]{1,0:T(8,128)(2,1)S(1)}, u32[]{:S(2)}, u32[]{:S(2)}) collective-permute-start(bf16[1024,896]{1,0:T(8,128)(2,1)S(1)} %copy-done.1), channel_id=1, source_target_pairs={{0,16},{1,49},{2,18},{3,51},{4,20},{5,53},{6,22},{7,55},{8,24},{9,... | collective-permute-start | bytes 5505032 | tf_op jit(solution)/shard_map/ppermute | solution.py:216
  86.0 43.2 %collective-permute-start.23 = (bf16[1024,896]{1,0:T(8,128)(2,1)S(1)}, bf16[1024,896]{1,0:T(8,128)(2,1)S(1)}, u32[]{:S(2)}, u32[]{:S(2)}) collective-permute-start(bf16[1024,896]{1,0:T(8,128)(2,1)S(1)} %copy-done.1), channel_id=1, source_target_pairs={{0,48},{1,17},{2,50},{3,19},{4,52},{5,21},{6,54},{7,23},{8,56},{9,... | collective-permute-start | bytes 5505032 | tf_op jit(solution)/shard_map/ppermute | solution.py:216
  111.7 37.6 %collective-permute-start.6 = (bf16[96,8192]{1,0:T(8,128)(2,1)S(1)}, bf16[96,8192]{1,0:T(8,128)(2,1)S(1)}, u32[]{:S(2)}, u32[]{:S(2)}) collective-permute-start(bf16[96,8192]{1,0:T(8,128)(2,1)S(1)} %collective-permute-done.2.refs_3_), channel_id=1, source_target_pairs={{0,1},{1,0},{2,3},{3,2},{4,5},{5,4},{6,7},{7,6},{8,9},{9,8},{10,11... | collective-permute-start | bytes 4718600 | tf_op jit(solution)/shard_map/ppermute | solution.py:216
  117.1 32.5 %collective-permute-start.4 = (bf16[96,8192]{1,0:T(8,128)(2,1)S(1)}, bf16[96,8192]{1,0:T(8,128)(2,1)S(1)}, u32[]{:S(2)}, u32[]{:S(2)}) collective-permute-start(bf16[96,8192]{1,0:T(8,128)(2,1)S(1)} %collective-permute-done.refs_1_), channel_id=1, source_target_pairs={{0,1},{1,0},{2,3},{3,2},{4,5},{5,4},{6,7},{7,6},{8,9},{9,8},{10,11... | collective-permute-start | bytes 4718600 | tf_op jit(solution)/shard_map/ppermute | solution.py:216
  117.1 27.0 %collective-permute-start.22 = (bf16[512,896]{1,0:T(8,128)(2,1)S(1)}, bf16[512,896]{1,0:T(8,128)(2,1)S(1)}, u32[]{:S(2)}, u32[]{:S(2)}) collective-permute-start(bf16[512,896]{1,0:T(8,128)(2,1)S(1)} %collective-permute-done.20.refs_8_.refs_6_), channel_id=1, source_target_pairs={{0,48},{1,17},{2,50},{3,19},{4,52},{5,21},{6,54},{7,23},{8,56},{9,... | collective-permute-start | bytes 2752520 | tf_op jit(solution)/shard_map/ppermute | solution.py:216
  127.0 20.3 %collective-permute-start.21 = (bf16[512,896]{1,0:T(8,128)(2,1)S(1)}, bf16[512,896]{1,0:T(8,128)(2,1)S(1)}, u32[]{:S(2)}, u32[]{:S(2)}) collective-permute-start(bf16[512,896]{1,0:T(8,128)(2,1)S(1)} %collective-permute-done.20.refs_8_.refs_6_), channel_id=1, source_target_pairs={{0,16},{1,49},{2,18},{3,51},{4,20},{5,53},{6,22},{7,55},{8,24},{9,... | collective-permute-start | bytes 2752520 | tf_op jit(solution)/shard_map/ppermute | solution.py:216
  129.2 22.3 %collective-permute-start.7 = (bf16[96,8192]{1,0:T(8,128)(2,1)S(1)}, bf16[96,8192]{1,0:T(8,128)(2,1)S(1)}, u32[]{:S(2)}, u32[]{:S(2)}) collective-permute-start(bf16[96,8192]{1,0:T(8,128)(2,1)S(1)} %collective-permute-done.2.refs_3_), channel_id=1, source_target_pairs={{0,4},{1,13},{2,6},{3,15},{4,8},{5,1},{6,10},{7,3},{8,12},{9,5},{1... | collective-permute-start | bytes 4718600 | tf_op jit(solution)/shard_map/ppermute | solution.py:216
  144.1 37.6 %collective-permute-start.8 = (bf16[96,8192]{1,0:T(8,128)(2,1)S(1)}, bf16[96,8192]{1,0:T(8,128)(2,1)S(1)}, u32[]{:S(2)}, u32[]{:S(2)}) collective-permute-start(bf16[96,8192]{1,0:T(8,128)(2,1)S(1)} %collective-permute-done.2.refs_3_), channel_id=1, source_target_pairs={{0,12},{1,5},{2,14},{3,7},{4,0},{5,9},{6,2},{7,11},{8,4},{9,13},{1... | collective-permute-start | bytes 4718600 | tf_op jit(solution)/shard_map/ppermute | solution.py:216
  147.3 34.6 %collective-permute-start.5 = (bf16[96,8192]{1,0:T(8,128)(2,1)S(1)}, bf16[96,8192]{1,0:T(8,128)(2,1)S(1)}, u32[]{:S(2)}, u32[]{:S(2)}) collective-permute-start(bf16[96,8192]{1,0:T(8,128)(2,1)S(1)} %collective-permute-done.1.refs_2_), channel_id=1, source_target_pairs={{0,1},{1,0},{2,3},{3,2},{4,5},{5,4},{6,7},{7,6},{8,9},{9,8},{10,11... | collective-permute-start | bytes 4718600 | tf_op jit(solution)/shard_map/ppermute | solution.py:216
  149.3 35.8 %collective-permute-start.27 = (bf16[1024,896]{1,0:T(8,128)(2,1)S(1)}, bf16[1024,896]{1,0:T(8,128)(2,1)S(1)}, u32[]{:S(2)}, u32[]{:S(2)}) collective-permute-start(bf16[1024,896]{1,0:T(8,128)(2,1)S(1)} %collective-permute-done.18.whole.refs_9_.refs_3_), channel_id=1, source_target_pairs={{0,16},{1,49},{2,18},{3,51},{4,20},{5,53},{6,22},{7,55},{8,24},{9,... | collective-permute-start | bytes 5505032 | tf_op jit(solution)/shard_map/ppermute | solution.py:216
  149.6 34.2 %collective-permute-start.11 = (bf16[96,8192]{1,0:T(8,128)(2,1)S(1)}, bf16[96,8192]{1,0:T(8,128)(2,1)S(1)}, u32[]{:S(2)}, u32[]{:S(2)}) collective-permute-start(bf16[96,8192]{1,0:T(8,128)(2,1)S(1)} %collective-permute-done.refs_1_), channel_id=1, source_target_pairs={{0,4},{1,13},{2,6},{3,15},{4,8},{5,1},{6,10},{7,3},{8,12},{9,5},{1... | collective-permute-start | bytes 4718600 | tf_op jit(solution)/shard_map/ppermute | solution.py:216
  151.5 48.3 %collective-permute-start.9 = (bf16[96,8192]{1,0:T(8,128)(2,1)S(1)}, bf16[96,8192]{1,0:T(8,128)(2,1)S(1)}, u32[]{:S(2)}, u32[]{:S(2)}) collective-permute-start(bf16[96,8192]{1,0:T(8,128)(2,1)S(1)} %collective-permute-done.7.whole.refs_0_.refs_8_), channel_id=1, source_target_pairs={{0,1},{1,0},{2,3},{3,2},{4,5},{5,4},{6,7},{7,6},{8,9},{9,8},{10,11... | collective-permute-start | bytes 4718600 | tf_op jit(solution)/shard_map/ppermute | solution.py:216
  181.7 20.5 %collective-permute-start.10 = (bf16[96,8192]{1,0:T(8,128)(2,1)S(1)}, bf16[96,8192]{1,0:T(8,128)(2,1)S(1)}, u32[]{:S(2)}, u32[]{:S(2)}) collective-permute-start(bf16[96,8192]{1,0:T(8,128)(2,1)S(1)} %collective-permute-done.8.refs_1_.refs_9_), channel_id=1, source_target_pairs={{0,1},{1,0},{2,3},{3,2},{4,5},{5,4},{6,7},{7,6},{8,9},{9,8},{10,11... | collective-permute-start | bytes 4718600 | tf_op jit(solution)/shard_map/ppermute | solution.py:216
  181.8 16.7 %collective-permute-start.29 = (bf16[96,5120]{1,0:T(8,128)(2,1)S(1)}, bf16[96,5120]{1,0:T(8,128)(2,1)S(1)}, u32[]{:S(2)}, u32[]{:S(2)}) collective-permute-start(bf16[96,5120]{1,0:T(8,128)(2,1)S(1)} %get-tuple-element.8), channel_id=1, source_target_pairs={{0,4},{1,13},{2,6},{3,15},{4,8},{5,1},{6,10},{7,3},{8,12},{9,5},{1... | collective-permute-start | bytes 2949128 | tf_op jit(solution)/shard_map/ppermute | solution.py:216
  183.7 31.0 %collective-permute-start.12 = (bf16[96,8192]{1,0:T(8,128)(2,1)S(1)}, bf16[96,8192]{1,0:T(8,128)(2,1)S(1)}, u32[]{:S(2)}, u32[]{:S(2)}) collective-permute-start(bf16[96,8192]{1,0:T(8,128)(2,1)S(1)} %collective-permute-done.11.refs_0_.refs_12_), channel_id=1, source_target_pairs={{0,1},{1,0},{2,3},{3,2},{4,5},{5,4},{6,7},{7,6},{8,9},{9,8},{10,11... | collective-permute-start | bytes 4718600 | tf_op jit(solution)/shard_map/ppermute | solution.py:216
  185.2 12.3 %collective-permute-start.19 = (bf16[256,896]{1,0:T(8,128)(2,1)S(1)}, bf16[256,896]{1,0:T(8,128)(2,1)S(1)}, u32[]{:S(2)}, u32[]{:S(2)}) collective-permute-start(bf16[256,896]{1,0:T(8,128)(2,1)S(1)} %kS.5), channel_id=1, source_target_pairs={{0,64},{1,65},{2,66},{3,67},{4,68},{5,69},{6,70},{7,71},{8,72},{9,... | collective-permute-start | bytes 1376264 | tf_op jit(solution)/shard_map/ppermute | solution.py:216
  197.5 14.5 %collective-permute-start.24 = (bf16[256,896]{1,0:T(8,128)(2,1)S(1)}, bf16[256,896]{1,0:T(8,128)(2,1)S(1)}, u32[]{:S(2)}, u32[]{:S(2)}) collective-permute-start(bf16[256,896]{1,0:T(8,128)(2,1)S(1)} %kS.6), channel_id=1, source_target_pairs={{0,64},{1,65},{2,66},{3,67},{4,68},{5,69},{6,70},{7,71},{8,72},{9,... | collective-permute-start | bytes 1376264 | tf_op jit(solution)/shard_map/ppermute | solution.py:216
  198.6 13.5 %collective-permute-start.13 = (bf16[96,3072]{1,0:T(8,128)(2,1)S(1)}, bf16[96,3072]{1,0:T(8,128)(2,1)S(1)}, u32[]{:S(2)}, u32[]{:S(2)}) collective-permute-start(bf16[96,3072]{1,0:T(8,128)(2,1)S(1)} %get-tuple-element.7), channel_id=1, source_target_pairs={{0,4},{1,13},{2,6},{3,15},{4,8},{5,1},{6,10},{7,3},{8,12},{9,5},{1... | collective-permute-start | bytes 1769480 | tf_op jit(solution)/shard_map/ppermute | solution.py:216
  199.8 18.8 %collective-permute-start.30 = (bf16[96,5120]{1,0:T(8,128)(2,1)S(1)}, bf16[96,5120]{1,0:T(8,128)(2,1)S(1)}, u32[]{:S(2)}, u32[]{:S(2)}) collective-permute-start(bf16[96,5120]{1,0:T(8,128)(2,1)S(1)} %collective-permute-done.29.refs_0_), channel_id=1, source_target_pairs={{0,1},{1,0},{2,3},{3,2},{4,5},{5,4},{6,7},{7,6},{8,9},{9,8},{10,11... | collective-permute-start | bytes 2949128 | tf_op jit(solution)/shard_map/ppermute | solution.py:216
  202.2 18.7 %collective-permute-start.26 = (bf16[512,896]{1,0:T(8,128)(2,1)S(1)}, bf16[512,896]{1,0:T(8,128)(2,1)S(1)}, u32[]{:S(2)}, u32[]{:S(2)}) collective-permute-start(bf16[512,896]{1,0:T(8,128)(2,1)S(1)} %collective-permute-done.21.refs_13_.refs_10_.refs_18_), channel_id=1, source_target_pairs={{0,16},{1,49},{2,18},{3,51},{4,20},{5,53},{6,22},{7,55},{8,24},{9,... | collective-permute-start | bytes 2752520 | tf_op jit(solution)/shard_map/ppermute | solution.py:216
  212.0 15.7 %collective-permute-start.17 = (bf16[256,896]{1,0:T(8,128)(2,1)S(1)}, bf16[256,896]{1,0:T(8,128)(2,1)S(1)}, u32[]{:S(2)}, u32[]{:S(2)}) collective-permute-start(bf16[256,896]{1,0:T(8,128)(2,1)S(1)} %collective-permute-done.16.refs_12_.refs_20_), channel_id=1, source_target_pairs={{0,16},{1,49},{2,18},{3,51},{4,20},{5,53},{6,22},{7,55},{8,24},{9,... | collective-permute-start | bytes 1376264 | tf_op jit(solution)/shard_map/ppermute | solution.py:216
  212.1 15.6 %collective-permute-start.14 = (bf16[96,3072]{1,0:T(8,128)(2,1)S(1)}, bf16[96,3072]{1,0:T(8,128)(2,1)S(1)}, u32[]{:S(2)}, u32[]{:S(2)}) collective-permute-start(bf16[96,3072]{1,0:T(8,128)(2,1)S(1)} %collective-permute-done.13.refs_14_), channel_id=1, source_target_pairs={{0,1},{1,0},{2,3},{3,2},{4,5},{5,4},{6,7},{7,6},{8,9},{9,8},{10,11... | collective-permute-start | bytes 1769480 | tf_op jit(solution)/shard_map/ppermute | solution.py:216
  214.7 11.9 %collective-permute-start.28 = (bf16[256,896]{1,0:T(8,128)(2,1)S(1)}, bf16[256,896]{1,0:T(8,128)(2,1)S(1)}, u32[]{:S(2)}, u32[]{:S(2)}) collective-permute-start(bf16[256,896]{1,0:T(8,128)(2,1)S(1)} %kS.7), channel_id=1, source_target_pairs={{0,64},{1,65},{2,66},{3,67},{4,68},{5,69},{6,70},{7,71},{8,72},{9,... | collective-permute-start | bytes 1376264 | tf_op jit(solution)/shard_map/ppermute | solution.py:216
  (2 other events, 163.0 us)
